TPU v7x, 32 devices: a whole 2x2x4 slice. The times are simulated.
32 devices in a mesh: blk: 8 (over y, x, core), grp: 4 (over z).
Axes of the slice: x: 2, y: 2, z: 4, core: 2. Of those that a mesh axis runs over, the one named last changes fastest.
Arguments:
- source_rows: float32 [8, 4, 400, 768], P('blk', 'grp'), may hold values from -2.4 to 2.4
- source_state: float32 [8, 4, 768], P('blk', 'grp'), may hold values from 0.05 to 1
- target_rows: float32 [8, 4, 400, 512], P('blk', 'grp'), may hold values from -12.5 to 12.5
- destination_state: float32 [8, 4, 512], P('blk', 'grp'), may hold values from 0.05 to 1
- positives: int32 [4, 8, 4, 768], P(None, 'blk', 'grp'), may hold values from 0 to 511
- relation_ids: int32 [4, 8, 4], P(None, 'blk', 'grp'), may hold values from 0 to 1
- relations: float32 [2, 400, 400], replicated, may hold values from -0.36 to 1.36
Outputs:
- source_out: float32 [8, 4, 400, 768], P('blk', 'grp')
- source_state_out: float32 [8, 4, 768], P('blk', 'grp')
- target_out: float32 [8, 4, 400, 512], P('blk', 'grp')
- target_state_out: float32 [8, 4, 512], P('blk', 'grp')
- relations_out: float32 [2, 400, 400], replicated
- operator_grads: float32 [2, 2, 400, 400], replicated
All inputs are finite; a program needn't handle non-finite values.
Results may differ from a plain program's by a relative error of at most 0.0003.
Values sent between devices are 32-bit elements; how exact they have to be, the bound alone decides.
No kernel may reach another device: no remote copies, remote signals or barrier semaphores. Data moves between devices by JAX's collectives and lax.ppermute only.
A program may use at most 64 MiB of HBM per device.

v0:
```python
import functools
import math

import jax
import jax.numpy as jnp
from jax import lax
from jax.experimental import pallas as pl
from jax.experimental.pallas import tpu as pltpu
from jax.sharding import PartitionSpec as P

entity_rate = 0.1
operator_rate = 0.01
grad_gain = 6.0
AXES = ("blk", "grp")
LANES = 128
F32, BF16 = jnp.float32, jnp.bfloat16


def round_up(value, step):
    return -(-value // step) * step


def from_behind(value, axis, steps):
    count = lax.axis_size(axis)
    pairs = [(source, (source + steps) % count) for source in range(count)]
    return lax.ppermute(value, axis, pairs)


def exchange(value, blk_mask, grp_mask):
    blk, grp = lax.axis_size("blk"), lax.axis_size("grp")
    pairs = [(b * grp + g, (b ^ blk_mask) * grp + (g ^ grp_mask)) for b in range(blk) for g in range(grp)]
    return lax.ppermute(value, AXES, pairs)


def group_masks(bits):
    masks = []
    for member in range(1, 1 << len(bits)):
        blk_mask = sum(m for i, (axis, m) in enumerate(bits) if axis == "blk" and member >> i & 1)
        grp_mask = sum(m for i, (axis, m) in enumerate(bits) if axis == "grp" and member >> i & 1)
        masks.append((member, blk_mask, grp_mask))
    return sorted(masks, key=lambda t: -bin(t[0]).count("1"))


def own_member(bits):
    member = jnp.int32(0)
    for i, (axis, m) in enumerate(bits):
        member = member + (((lax.axis_index(axis) // m) % 2) << i)
    return member


def reduce_plan(blk, grp):
    if blk & (blk - 1) or grp & (grp - 1):
        return None
    blk_bits = [("blk", 1 << i) for i in range(blk.bit_length() - 1)]
    grp_bits = [("grp", 1 << i) for i in range(grp.bit_length() - 1)]
    stages = [s for s in (blk_bits[:1], blk_bits[1:3], grp_bits[:1]) if s]
    return (stages, blk_bits[3:] + grp_bits[1:]) if len(stages) > 1 else None


def scatter_sum(value, bits):
    blocks = value.reshape((1 << len(bits), -1) + value.shape[1:])
    total = blocks[0]
    for block in [exchange(blocks[d], mb, mg) for d, mb, mg in group_masks(bits)]:
        total = total + block
    return total


def gather(value, bits):
    arrived = {d: exchange(value, mb, mg) for d, mb, mg in group_masks(bits)}
    arrived[0] = value
    return jnp.concatenate([arrived[d] for d in range(1 << len(bits))], axis=0)


def piece_plan():
    plan = reduce_plan(lax.axis_size("blk"), lax.axis_size("grp"))
    if plan is None:
        return 1, jnp.int32(0)
    count, me = 1, jnp.int32(0)
    for stage in plan[0]:
        count <<= len(stage)
        me = (me << len(stage)) + own_member(stage)
    return count, me


def sum_everywhere(packed, work, args):
    plan = reduce_plan(lax.axis_size("blk"), lax.axis_size("grp"))
    if plan is None:
        after, *rest = work(*args)
        return lax.psum(packed, AXES), from_behind(after, "blk", 1), *rest
    stages, singles = plan
    for place, stage in enumerate(stages):
        if place == 1:
            packed, args = lax.optimization_barrier((packed, args))
            after, *rest = work(*args)
        packed = scatter_sum(packed, stage)
        if place == 1:
            packed, after = lax.optimization_barrier((packed, after))
            arriving = from_behind(after, "blk", 1)
    for axis, mask in singles:
        packed = packed + exchange(packed, mask if axis == "blk" else 0, mask if axis == "grp" else 0)
    for place, stage in reversed(list(enumerate(stages))):
        if place == 1:
            packed, arriving = lax.optimization_barrier((packed, arriving))
        packed = gather(packed, stage)
    return packed, arriving, *rest


NN = (((1,), (0,)), ((), ()))
NT = (((1,), (1,)), ((), ()))


def dot3(ah, al, bh, bl, dims):
    one = functools.partial(lax.dot_general, dimension_numbers=dims, preferred_element_type=F32)
    return one(ah, bh) + (one(ah, bl) + one(al, bh))


def split(x):
    high = x.astype(BF16)
    return high, (x - high.astype(F32)).astype(BF16)


def put_split(refs, x):
    rows = x.shape[0]
    refs[0][:rows], refs[1][:rows] = split(x)
    if rows < refs[0].shape[0]:
        blank = jnp.zeros((refs[0].shape[0] - rows, x.shape[1]), BF16)
        refs[0][rows:], refs[1][rows:] = blank, blank


def both(refs, rows=None):
    return (refs[0][...], refs[1][...]) if rows is None else (refs[0][:rows], refs[1][:rows])


def pad_rows(x, rows):
    return jnp.concatenate([x, jnp.zeros((rows - x.shape[0], x.shape[1]), x.dtype)], axis=0)


def square_of(pad_ref, matrix):
    width = matrix.shape[0]
    pad_ref[...] = jnp.zeros(pad_ref.shape, F32)
    pad_ref[:width, :width] = matrix


def queries_into(q_refs, square_ref, x_refs, width):
    transposed = split(square_ref[...].T[:width])
    put_split(q_refs, dot3(*transposed, *both(x_refs), NN))


def score_grad_into(sg_refs, q_refs, target, partner):
    wide = q_refs[0].shape[0]
    scores = dot3(*split(pad_rows(target, wide).T), *both(q_refs), NN)
    expo = jnp.exp(scores - jnp.max(scores, axis=0, keepdims=True))
    chance = expo * (1.0 / jnp.sum(expo, axis=0, keepdims=True))
    row = lax.broadcasted_iota(jnp.int32, scores.shape, 0)
    put_split(sg_refs, chance - jnp.where(row == partner, 1.0, 0.0))


def adagrad(values, state, gradient):
    state_new = state + jnp.sum(gradient * gradient, axis=0, keepdims=True) * (1.0 / values.shape[0])
    return values - gradient * (entity_rate / jnp.sqrt(state_new)), state_new


def target_into(out_ref, q_refs, sg_refs, target, state):
    width = target.shape[0]
    gradient = dot3(*both(q_refs, width), *both(sg_refs), NT)
    out_ref[:width], out_ref[width : width + 1] = adagrad(target, state, gradient)
    rest = out_ref.shape[0] - width - 1
    out_ref[width + 1 :] = jnp.zeros((rest, target.shape[1]), F32)


def query_grad_into(g_refs, sg_refs, target):
    put_split(g_refs, dot3(*split(target), *both(sg_refs), NN))


def source_into(x_out, state_out, square_ref, g_refs, source, state):
    width = source.shape[0]
    gradient = dot3(*split(square_ref[:width]), *both(g_refs), NN)
    x_out[...], state_out[...] = adagrad(source, state, gradient)


def pack_into(out_ref, parts, kinds):
    width = parts[0][1].shape[0]
    full, tail = divmod(width, LANES)
    span = tail_span(width, kinds)
    packed_tail = None
    for kind in range(kinds):
        total = sum(jnp.where(index == kind, part, 0.0) for index, part in parts)
        for block in range(full):
            start = (kind * full + block) * width
            out_ref[start : start + width] = total[:, block * LANES : (block + 1) * LANES]
        if tail:
            ends = pad_rows(total[:, full * LANES :], round_up(width, span))
            for place in range(ends.shape[0] // span):
                turn = (kind * (ends.shape[0] // span) + place) * tail
                moved = ends[place * span : (place + 1) * span]
                moved = pltpu.roll(moved, turn, 1) if turn else moved
                packed_tail = moved if packed_tail is None else packed_tail + moved
    start = kinds * full * width
    if tail:
        out_ref[start : start + span] = packed_tail
        start += span
    out_ref[start:] = jnp.zeros((out_ref.shape[0] - start, LANES), F32)


def tail_span(width, kinds):
    tail = width % LANES
    return round_up(-(-width // (LANES // tail // kinds)), 8) if tail else 0


def packed_rows(width, kinds, pieces):
    return round_up(kinds * (width // LANES) * width + tail_span(width, kinds), 8 * pieces)


def unpack(flat_ref, scaled_out, kinds, width, scale):
    full, tail = divmod(width, LANES)
    span = tail_span(width, kinds)
    for kind in range(kinds):
        for block in range(full):
            start = (kind * full + block) * width
            scaled_out[kind, :, block * LANES : (block + 1) * LANES] = scale * flat_ref[start : start + width]
        if tail:
            start = kinds * full * width
            ends = flat_ref[start : start + span]
            places = -(-width // span)
            for place in range(places):
                rows = min(span, width - place * span)
                turn = (kind * places + place) * tail
                moved = pltpu.roll(ends, LANES - turn, 1) if turn else ends
                scaled_out[kind, place * span : place * span + rows, full * LANES :] = scale * moved[:rows, :tail]


def put_pieces(out_ref, in_ref, me, pieces):
    rows = in_ref.shape[0] // pieces
    for piece in range(pieces):
        out_ref[piece * rows : (piece + 1) * rows] = in_ref[pl.ds(pl.multiple_of((me ^ piece) * rows, 8), rows)]


def first_kernel(ids, me, partners, relations, source, target, *refs, bucket, updated):
    if updated:
        target_out, sgh, sgl, square, xh, xl, qh, ql = refs
        square_of(square, relations[ids[bucket]])
        put_split((xh, xl), source[...])
        body, state = target[: source.shape[0]], target[source.shape[0] : source.shape[0] + 1]
        queries_into((qh, ql), square, (xh, xl), source.shape[0])
    else:
        target_state, target_out, sgh, sgl, square, xh, xl, qh, ql, matrix, source_in, target_in, sems = refs
        loads = [
            pltpu.make_async_copy(relations.at[ids[bucket]], matrix, sems.at[0]),
            pltpu.make_async_copy(source, source_in, sems.at[1]),
            pltpu.make_async_copy(target, target_in, sems.at[2]),
        ]
        for load in loads:
            load.start()
        loads[0].wait()
        square_of(square, matrix[...])
        loads[1].wait()
        put_split((xh, xl), source_in[...])
        queries_into((qh, ql), square, (xh, xl), source.shape[0])
        loads[2].wait()
        body, state = target_in[...], target_state[0]
    score_grad_into((sgh, sgl), (qh, ql), body, partners[bucket, 0])
    target_into(target_out, (qh, ql), (sgh, sgl), body, state)


def update_kernel(me, packed, relations, *refs, pieces, scale, place, last):
    grads_out, relations_out, flat, scaled, sems = refs[1 if place else 0 :][:5]
    kinds, width = relations.shape[0], relations.shape[1]
    put_pieces(flat, packed, me[0], pieces)
    unpack(flat, scaled, kinds, width, scale)
    stores = [pltpu.make_async_copy(scaled, grads_out.at[place], sems.at[0])]
    stores[0].start()
    renewed = refs[-1] if last else relations_out
    for kind in range(kinds):
        renewed[kind] = relations[kind] - operator_rate * scaled[kind]
    if last:
        stores.append(pltpu.make_async_copy(renewed, relations_out, sems.at[1]))
        stores[1].start()
    for store in stores:
        store.wait()


def second_kernel(ids, relations, source, source_state, target, sgh, sgl, source_out, state_out, grad_out, qh, ql, square, xh, xl, gh, gl, *, bucket):
    width = source.shape[0]
    query_grad_into((gh, gl), (sgh, sgl), target[:width])
    put_split((xh, xl), source[...])
    grad_out[...] = dot3(*both((xh, xl), width), *both((gh, gl)), NT)
    square_of(square, relations[ids[bucket]])
    source_into(source_out, state_out.at[0], square, (gh, gl), source[...], source_state[0])
    square_of(square, relations[ids[bucket + 1]])
    put_split((xh, xl), source_out[...])
    queries_into((qh, ql), square, (xh, xl), width)


def third_kernel(ids, me, partners, source, target, qh, ql, grad_before, packed, sgh, sgl, gh, gl, flat, *, bucket, kinds, pieces):
    width = source.shape[0]
    body = target[:width]
    score_grad_into((sgh, sgl), (qh, ql), body, partners[bucket, 0])
    query_grad_into((gh, gl), (sgh, sgl), body)
    grad = dot3(*split(source[...]), *both((gh, gl)), NT)
    pack_into(flat, ((ids[bucket - 1], grad_before[...]), (ids[bucket], grad)), kinds)
    put_pieces(packed, flat, me[0], pieces)


def fourth_kernel(ids, relations, source, source_state, target, qh, ql, sgh, sgl, gh, gl, target_out, source_out, state_out, square, *, bucket):
    width = source.shape[0]
    target_into(target_out, (qh, ql), (sgh, sgl), target[:width], target[width : width + 1])
    square_of(square, relations[ids[bucket]])
    source_into(source_out, state_out.at[0], square, (gh, gl), source[...], source_state[0])


VMEM = pl.BlockSpec(memory_space=pltpu.VMEM)
SMEM = pl.BlockSpec(memory_space=pltpu.SMEM)
HBM = pl.BlockSpec(memory_space=pltpu.HBM)


def call(kernel, name, args, args_in, outs, scratch=(), flops=0, outs_in=None, aliases=None):
    return pl.pallas_call(
        kernel,
        in_specs=args_in,
        out_specs=outs_in or [VMEM] * len(outs),
        out_shape=[jax.ShapeDtypeStruct(shape, dtype) for shape, dtype in outs],
        scratch_shapes=[pltpu.VMEM(*s) if isinstance(s, tuple) else s for s in scratch],
        input_output_aliases=aliases or {},
        compiler_params=pltpu.CompilerParams(vmem_limit_bytes=VMEM_LIMIT),
        cost_estimate=pl.CostEstimate(flops=flops, transcendentals=0, bytes_accessed=0),
        name=name,
    )(*args)


VMEM_LIMIT = 16 << 20


def shards(source_rows, source_state, target_rows, destination_state, positives, relation_ids, relations):
    buckets, kinds, width = positives.shape[0], relations.shape[0], relations.shape[1]
    source, state = source_rows[0, 0], source_state
    target, target_state = target_rows[0, 0], destination_state
    columns, block = source.shape[1], target.shape[1]
    scale = grad_gain / math.sqrt(columns * lax.axis_size("blk") * lax.axis_size("grp"))
    pieces, me = piece_plan()
    me, ids = me[None], relation_ids[:, 0, 0]
    wide, tall = round_up(width, LANES), round_up(width + 1, 8)
    rows = packed_rows(width, kinds, pieces)
    q_pair = [((wide, columns), BF16)] * 2
    sg_pair = [((block, columns), BF16)] * 2
    square = [((wide, wide), F32)]
    moving = [((tall, block), F32)]
    source_outs = [((width, columns), F32), (source_state.shape, F32)]
    product = 6 * width * width * columns
    updates = buckets // 2
    grads = ()
    for update in range(updates):
        bucket = 2 * update
        args, args_in, extra = (ids, me, positives, relations, source, target), [SMEM] * 2 + [VMEM] * 4, []
        if update == 0:
            args, args_in = args + (target_state,), [SMEM] * 2 + [VMEM] + [HBM] * 3 + [VMEM]
            extra = [((width, width), F32), (source.shape, F32), (target.shape, F32), pltpu.SemaphoreType.DMA((3,))]
        after, sgh, sgl = call(
            functools.partial(first_kernel, bucket=bucket, updated=update > 0), "first",
            args, args_in, moving + sg_pair, square + q_pair + q_pair + extra, 3 * product)
        arriving = from_behind(after, "blk", 1)
        source, state, grad, qh, ql = call(
            functools.partial(second_kernel, bucket=bucket), "second",
            (ids, relations, source, state, target, sgh, sgl), [SMEM] + [VMEM] * 6,
            source_outs + [((width, wide), F32)] + q_pair, square + q_pair + q_pair, 4 * product)
        target = arriving
        packed, sgh, sgl, gh, gl = call(
            functools.partial(third_kernel, bucket=bucket + 1, kinds=kinds, pieces=pieces), "third",
            (ids, me, positives, source, target, qh, ql, grad), [SMEM] * 2 + [VMEM] * 6,
            [((rows, LANES), F32)] + sg_pair + q_pair, [((rows, LANES), F32)], 3 * product)
        total, target, source, state = sum_everywhere(
            packed,
            lambda *args: call(
                functools.partial(fourth_kernel, bucket=bucket + 1), "fourth",
                (ids, *args), [SMEM] + [VMEM] * len(args), moving + source_outs, square, 2 * product),
            (relations, source, state, target, qh, ql, sgh, sgl, gh, gl))
        last = update == updates - 1
        grads, relations = call(
            functools.partial(update_kernel, pieces=pieces, scale=scale, place=update, last=last), "update",
            (me, total, relations, *((grads,) if update else ())), [SMEM, VMEM, VMEM] + ([HBM] if update else []),
            [((updates, *relations.shape), F32), (relations.shape, F32)],
            [((rows, LANES), F32), (relations.shape, F32), pltpu.SemaphoreType.DMA((2,))] + ([(relations.shape, F32)] if last else []),
            product, [HBM, HBM if last else VMEM], {3: 0} if update else None)
    return (
        source[None, None],
        state,
        target[None, None, :width],
        target[None, width : width + 1],
        relations,
        grads,
    )


def solution(mesh):
    rows, columns = P("blk", "grp", None, None), P("blk", "grp", None)
    in_specs = (rows, columns, rows, columns, P(None, "blk", "grp", None), P(None, "blk", "grp"), P())
    out_specs = (rows, columns, rows, columns, P(), P())
    return jax.shard_map(shards, mesh=mesh, in_specs=in_specs, out_specs=out_specs, check_vma=False)
```

profile of v0, /device:TPU:0, one launch (start us, length us, event | category | flops | bytes accessed | tf_op | source)
XLA Modules:
  0.0 150.0 jit_solution(1605948903718753304)
XLA Ops:
  6.6 7.8 %first.2 = (f32[408,512]{1,0:T(8,128)S(1)}, bf16[512,768]{1,0:T(8,128)(2,1)S(1)}, bf16[512,768]{1,0:T(8,128)(2,1)S(1)}) custom-call(s32[4]{0:T(128)S(1)} %bitcast.9, s32[1]{0:T(128)} %bitcast.1.me, s32[4,1,1,768]{3,2,1,0:T(1,128)S(1)} %copy-done.8, f32[2,400,400]{2,1,0:T(8,128)S(1)} %copy-done, f32[400,768]{1,0:T(8,128)S(1)} %bitcast.17, ...), custom_call_target="tpu_custom_call" | custom-call | flops 2211840000 | tf_op jit(solution)/shard_map/first/pallas_call | solution.py:317
  15.2 7.0 %second.2 = (f32[400,768]{1,0:T(8,128)S(1)}, f32[1,1,768]{2,1,0:T(1,128)S(1)}, f32[400,512]{1,0:T(8,128)S(1)}, bf16[512,768]{1,0:T(8,128)(2,1)S(1)}, bf16[512,768]{1,0:T(8,128)(2,1)S(1)}) custom-call(s32[4]{0:T(128)S(1)} %bitcast.10, f32[2,400,400]{2,1,0:T(8,128)S(1)} %copy-done.1, f32[400,768]{1,0:T(8,128)S(1)} %bitcast.18, f32[1,1,768]{2,1,0:T(1,128)S(1)} %copy-done.10, ...), custom_call_target="tpu_custom_call" | custom-call | flops 2949120000 | tf_op jit(solution)/shard_map/second/pallas_call | solution.py:317
  22.2 6.0 %collective-permute-done.target = f32[408,512]{1,0:T(8,128)S(1)} collective-permute-done((f32[408,512]{1,0:T(8,128)S(1)}, f32[408,512]{1,0:T(8,128)S(1)}, u32[]{:S(2)}, u32[]{:S(2)}) %collective-permute-start) | collective-permute-done | bytes 835616 | tf_op jit(solution)/shard_map/ppermute | solution.py:26
  28.2 6.5 %third.2 = (f32[2560,128]{1,0:T(8,128)S(1)}, bf16[512,768]{1,0:T(8,128)(2,1)S(1)}, bf16[512,768]{1,0:T(8,128)(2,1)S(1)}, bf16[512,768]{1,0:T(8,128)(2,1)S(1)}, bf16[512,768]{1,0:T(8,128)(2,1)S(1)}) custom-call(s32[4]{0:T(128)S(1)} %bitcast.11, s32[1]{0:T(128)} %bitcast.1.me, s32[4,1,1,768]{3,2,1,0:T(1,128)S(1)} %copy-done.8, ...), custom_call_target="tpu_custom_call" | custom-call | flops 2211840000 | tf_op jit(solution)/shard_map/third/pallas_call | solution.py:317
  34.9 2.1 %collective-permute-done.1 = f32[1280,128]{1,0:T(8,128)S(1)} collective-permute-done((f32[1280,128]{1,0:T(8,128)S(1)}, f32[1280,128]{1,0:T(8,128)S(1)}, u32[]{:S(2)}, u32[]{:S(2)}) %collective-permute-start.1) | collective-permute-done | bytes 655392 | tf_op jit(solution)/shard_map/ppermute | solution.py:32
  37.1 2.4 %collective-permute-start.2 = (f32[320,128]{1,0:T(8,128)S(1)}, f32[320,128]{1,0:T(8,128)S(1)}, u32[]{:S(2)}, u32[]{:S(2)}) collective-permute-start(f32[320,128]{1,0:T(8,128)S(1)} %get-tuple-element.141), channel_id=1, source_target_pairs={{0,24},{1,25},{2,26},{3,27},{4,28},{5,29},{6,30},{7,31},{8,16},{9,... | collective-permute-start | bytes 491528 | tf_op jit(solution)/shard_map/ppermute | solution.py:32
  40.9 3.1 %fourth.2 = (f32[408,512]{1,0:T(8,128)S(1)}, f32[400,768]{1,0:T(8,128)S(1)}, f32[1,1,768]{2,1,0:T(1,128)S(1)}) custom-call(s32[4]{0:T(128)S(1)} %bitcast.12, f32[2,400,400]{2,1,0:T(8,128)S(1)} %copy-done.1, f32[400,768]{1,0:T(8,128)S(1)} %get-tuple-element.87.source, f32[1,1,768]{2,1,0:T(1,128)S(1)} %get-tuple-element.88.source_state, ...), custom_call_target="tpu_custom_call" | custom-call | flops 1474560000 | tf_op jit(solution)/shard_map/fourth/pallas_call | solution.py:317
  45.1 3.5 %collective-permute-done.3 = f32[320,128]{1,0:T(8,128)S(1)} collective-permute-done((f32[320,128]{1,0:T(8,128)S(1)}, f32[320,128]{1,0:T(8,128)S(1)}, u32[]{:S(2)}, u32[]{:S(2)}) %collective-permute-start.3) | collective-permute-done | bytes 163872 | tf_op jit(solution)/shard_map/ppermute | solution.py:32
  49.0 1.6 %collective-permute-start.5 = (f32[160,128]{1,0:T(8,128)S(1)}, f32[160,128]{1,0:T(8,128)S(1)}, u32[]{:S(2)}, u32[]{:S(2)}) collective-permute-start(f32[160,128]{1,0:T(8,128)S(1)} %slice.77), channel_id=1, source_target_pairs={{0,1},{1,0},{2,3},{3,2},{4,5},{5,4},{6,7},{7,6},{8,9},{9,8},{10,11... | collective-permute-start | bytes 245768 | tf_op jit(solution)/shard_map/ppermute | solution.py:32
  50.7 3.4 %collective-permute-done.5 = f32[160,128]{1,0:T(8,128)S(1)} collective-permute-done((f32[160,128]{1,0:T(8,128)S(1)}, f32[160,128]{1,0:T(8,128)S(1)}, u32[]{:S(2)}, u32[]{:S(2)}) %collective-permute-start.5) | collective-permute-done | bytes 81952 | tf_op jit(solution)/shard_map/ppermute | solution.py:32
  54.1 2.7 %collective-permute-start.6 = (f32[160,128]{1,0:T(8,128)S(1)}, f32[160,128]{1,0:T(8,128)S(1)}, u32[]{:S(2)}, u32[]{:S(2)}) collective-permute-start(f32[160,128]{1,0:T(8,128)S(1)} %slice_add_fusion.3), channel_id=1, source_target_pairs={{0,2},{1,3},{2,0},{3,1},{4,6},{5,7},{6,4},{7,5},{8,10},{9,11},{10,... | collective-permute-start | bytes 245768 | tf_op jit(solution)/shard_map/ppermute | solution.py:32
  56.7 4.3 %collective-permute-done.6 = f32[160,128]{1,0:T(8,128)S(1)} collective-permute-done((f32[160,128]{1,0:T(8,128)S(1)}, f32[160,128]{1,0:T(8,128)S(1)}, u32[]{:S(2)}, u32[]{:S(2)}) %collective-permute-start.6) | collective-permute-done | bytes 81952 | tf_op jit(solution)/shard_map/ppermute | solution.py:32
  61.6 3.9 %collective-permute-done.7 = f32[160,128]{1,0:T(8,128)S(1)} collective-permute-done((f32[160,128]{1,0:T(8,128)S(1)}, f32[160,128]{1,0:T(8,128)S(1)}, u32[]{:S(2)}, u32[]{:S(2)}) %collective-permute-start.7) | collective-permute-done | bytes 81952 | tf_op jit(solution)/shard_map/ppermute | solution.py:32
  69.1 2.4 %collective-permute-done.10 = f32[320,128]{1,0:T(8,128)S(1)} collective-permute-done((f32[320,128]{1,0:T(8,128)S(1)}, f32[320,128]{1,0:T(8,128)S(1)}, u32[]{:S(2)}, u32[]{:S(2)}) %collective-permute-start.10) | collective-permute-done | bytes 163872 | tf_op jit(solution)/shard_map/ppermute | solution.py:32
  71.5 1.8 %collective-permute-done.11 = f32[320,128]{1,0:T(8,128)S(1)} collective-permute-done((f32[320,128]{1,0:T(8,128)S(1)}, f32[320,128]{1,0:T(8,128)S(1)}, u32[]{:S(2)}, u32[]{:S(2)}) %collective-permute-start.11) | collective-permute-done | bytes 163872 | tf_op jit(solution)/shard_map/ppermute | solution.py:32
  74.9 2.0 %collective-permute-done.12 = f32[1280,128]{1,0:T(8,128)S(1)} collective-permute-done((f32[1280,128]{1,0:T(8,128)S(1)}, f32[1280,128]{1,0:T(8,128)S(1)}, u32[]{:S(2)}, u32[]{:S(2)}) %collective-permute-start.12) | collective-permute-done | bytes 655392 | tf_op jit(solution)/shard_map/ppermute | solution.py:32
  77.0 1.8 %update.2 = (f32[2,2,400,400]{3,2,1,0:T(8,128)}, f32[2,400,400]{2,1,0:T(8,128)S(1)}) custom-call(s32[1]{0:T(128)} %bitcast.1.me, f32[2560,128]{1,0:T(8,128)S(1)} %constant_dynamic-update-slice_fusion.packed, f32[2,400,400]{2,1,0:T(8,128)S(1)} %copy-done.1), custom_call_target="tpu_custom_call" | custom-call | flops 737280000 | tf_op jit(solution)/shard_map/update/pallas_call | solution.py:317
  78.8 7.0 %first.3 = (f32[408,512]{1,0:T(8,128)S(1)}, bf16[512,768]{1,0:T(8,128)(2,1)S(1)}, bf16[512,768]{1,0:T(8,128)(2,1)S(1)}) custom-call(s32[4]{0:T(128)S(1)} %bitcast.13, s32[1]{0:T(128)} %bitcast.1.me, s32[4,1,1,768]{3,2,1,0:T(1,128)S(1)} %copy-done.9, f32[2,400,400]{2,1,0:T(8,128)S(1)} %get-tuple-element.117.relations, ...), custom_call_target="tpu_custom_call" | custom-call | flops 2211840000 | tf_op jit(solution)/shard_map/first/pallas_call | solution.py:317
  85.9 7.0 %second.3 = (f32[400,768]{1,0:T(8,128)S(1)}, f32[1,1,768]{2,1,0:T(1,128)S(1)}, f32[400,512]{1,0:T(8,128)S(1)}, bf16[512,768]{1,0:T(8,128)(2,1)S(1)}, bf16[512,768]{1,0:T(8,128)(2,1)S(1)}) custom-call(s32[4]{0:T(128)S(1)} %bitcast.14, f32[2,400,400]{2,1,0:T(8,128)S(1)} %get-tuple-element.117.relations, f32[400,768]{1,0:T(8,128)S(1)} %get-tuple-element.101.source, ...), custom_call_target="tpu_custom_call" | custom-call | flops 2949120000 | tf_op jit(solution)/shard_map/second/pallas_call | solution.py:317
  93.0 5.7 %collective-permute-done.13.target = f32[408,512]{1,0:T(8,128)S(1)} collective-permute-done((f32[408,512]{1,0:T(8,128)S(1)}, f32[408,512]{1,0:T(8,128)S(1)}, u32[]{:S(2)}, u32[]{:S(2)}) %collective-permute-start.13) | collective-permute-done | bytes 835616 | tf_op jit(solution)/shard_map/ppermute | solution.py:26
  98.6 6.5 %third.3 = (f32[2560,128]{1,0:T(8,128)S(1)}, bf16[512,768]{1,0:T(8,128)(2,1)S(1)}, bf16[512,768]{1,0:T(8,128)(2,1)S(1)}, bf16[512,768]{1,0:T(8,128)(2,1)S(1)}, bf16[512,768]{1,0:T(8,128)(2,1)S(1)}) custom-call(s32[4]{0:T(128)S(1)} %bitcast.15, s32[1]{0:T(128)} %bitcast.1.me, s32[4,1,1,768]{3,2,1,0:T(1,128)S(1)} %copy-done.9, ...), custom_call_target="tpu_custom_call" | custom-call | flops 2211840000 | tf_op jit(solution)/shard_map/third/pallas_call | solution.py:317
  105.3 2.1 %collective-permute-done.14 = f32[1280,128]{1,0:T(8,128)S(1)} collective-permute-done((f32[1280,128]{1,0:T(8,128)S(1)}, f32[1280,128]{1,0:T(8,128)S(1)}, u32[]{:S(2)}, u32[]{:S(2)}) %collective-permute-start.14) | collective-permute-done | bytes 655392 | tf_op jit(solution)/shard_map/ppermute | solution.py:32
  107.5 1.6 %collective-permute-start.15 = (f32[320,128]{1,0:T(8,128)S(1)}, f32[320,128]{1,0:T(8,128)S(1)}, u32[]{:S(2)}, u32[]{:S(2)}) collective-permute-start(f32[320,128]{1,0:T(8,128)S(1)} %get-tuple-element.138), channel_id=1, source_target_pairs={{0,24},{1,25},{2,26},{3,27},{4,28},{5,29},{6,30},{7,31},{8,16},{9,... | collective-permute-start | bytes 491528 | tf_op jit(solution)/shard_map/ppermute | solution.py:32
  111.1 4.2 %fourth.3 = (f32[408,512]{1,0:T(8,128)S(1)}, f32[400,768]{1,0:T(8,128)}, f32[1,1,768]{2,1,0:T(1,128)}) custom-call(s32[4]{0:T(128)S(1)} %bitcast.16, f32[2,400,400]{2,1,0:T(8,128)S(1)} %get-tuple-element.117.relations, f32[400,768]{1,0:T(8,128)S(1)} %get-tuple-element.118.source, f32[1,1,768]{2,1,0:T(1,128)S(1)} %get-tuple-element.119.source_state, ...), custom_call_target="tpu_custom_call" | custom-call | flops 1474560000 | tf_op jit(solution)/shard_map/fourth/pallas_call | solution.py:317
  115.6 2.1 %collective-permute-done.16 = f32[320,128]{1,0:T(8,128)S(1)} collective-permute-done((f32[320,128]{1,0:T(8,128)S(1)}, f32[320,128]{1,0:T(8,128)S(1)}, u32[]{:S(2)}, u32[]{:S(2)}) %collective-permute-start.16) | collective-permute-done | bytes 163872 | tf_op jit(solution)/shard_map/ppermute | solution.py:32
  119.4 4.2 %collective-permute-done.18 = f32[160,128]{1,0:T(8,128)S(1)} collective-permute-done((f32[160,128]{1,0:T(8,128)S(1)}, f32[160,128]{1,0:T(8,128)S(1)}, u32[]{:S(2)}, u32[]{:S(2)}) %collective-permute-start.18) | collective-permute-done | bytes 81952 | tf_op jit(solution)/shard_map/ppermute | solution.py:32
  123.6 3.2 %collective-permute-start.19 = (f32[160,128]{1,0:T(8,128)S(1)}, f32[160,128]{1,0:T(8,128)S(1)}, u32[]{:S(2)}, u32[]{:S(2)}) collective-permute-start(f32[160,128]{1,0:T(8,128)S(1)} %slice_add_fusion.2), channel_id=1, source_target_pairs={{0,2},{1,3},{2,0},{3,1},{4,6},{5,7},{6,4},{7,5},{8,10},{9,11},{10,... | collective-permute-start | bytes 245768 | tf_op jit(solution)/shard_map/ppermute | solution.py:32
  126.7 4.4 %collective-permute-done.19 = f32[160,128]{1,0:T(8,128)S(1)} collective-permute-done((f32[160,128]{1,0:T(8,128)S(1)}, f32[160,128]{1,0:T(8,128)S(1)}, u32[]{:S(2)}, u32[]{:S(2)}) %collective-permute-start.19) | collective-permute-done | bytes 81952 | tf_op jit(solution)/shard_map/ppermute | solution.py:32
  132.0 3.7 %collective-permute-done.20 = f32[160,128]{1,0:T(8,128)S(1)} collective-permute-done((f32[160,128]{1,0:T(8,128)S(1)}, f32[160,128]{1,0:T(8,128)S(1)}, u32[]{:S(2)}, u32[]{:S(2)}) %collective-permute-start.20) | collective-permute-done | bytes 81952 | tf_op jit(solution)/shard_map/ppermute | solution.py:32
  139.9 2.4 %collective-permute-done.22 = f32[320,128]{1,0:T(8,128)S(1)} collective-permute-done((f32[320,128]{1,0:T(8,128)S(1)}, f32[320,128]{1,0:T(8,128)S(1)}, u32[]{:S(2)}, u32[]{:S(2)}) %collective-permute-start.22) | collective-permute-done | bytes 163872 | tf_op jit(solution)/shard_map/ppermute | solution.py:32
  142.3 2.9 %collective-permute-done.23 = f32[320,128]{1,0:T(8,128)S(1)} collective-permute-done((f32[320,128]{1,0:T(8,128)S(1)}, f32[320,128]{1,0:T(8,128)S(1)}, u32[]{:S(2)}, u32[]{:S(2)}) %collective-permute-start.23) | collective-permute-done | bytes 163872 | tf_op jit(solution)/shard_map/ppermute | solution.py:32
  147.5 2.3 %update.3 = (f32[2,2,400,400]{3,2,1,0:T(8,128)}, f32[2,400,400]{2,1,0:T(8,128)}) custom-call(s32[1]{0:T(128)} %bitcast.1.me, f32[2560,128]{1,0:T(8,128)S(1)} %constant_dynamic-update-slice_fusion.5.packed, f32[2,400,400]{2,1,0:T(8,128)S(1)} %get-tuple-element.117.relations, ...), custom_call_target="tpu_custom_call", output_to_operand_aliasing={{0}: (3, {})} | custom-call | flops 737280000 | tf_op jit(solution)/shard_map/update/pallas_call | solution.py:317
  (84 shorter events, 27.2 us)
Async XLA Ops:
  6.6 8.5 %copy-start.1 = (f32[2,400,400]{2,1,0:T(8,128)S(1)}, f32[2,400,400]{2,1,0:T(8,128)}, u32[]{:S(2)}) copy-start(f32[2,400,400]{2,1,0:T(8,128)} %relations.6) | copy-start | bytes 3840004
  6.6 8.5 %copy-start.5 = (f32[1,1,400,768]{3,2,1,0:T(8,128)S(1)}, f32[1,1,400,768]{3,2,1,0:T(8,128)}, u32[]{:S(2)}) copy-start(f32[1,1,400,768]{3,2,1,0:T(8,128)} %param.7) | copy-start | bytes 3686404
  6.6 8.5 %copy-start.7 = (f32[1,1,400,512]{3,2,1,0:T(8,128)S(1)}, f32[1,1,400,512]{3,2,1,0:T(8,128)}, u32[]{:S(2)}) copy-start(f32[1,1,400,512]{3,2,1,0:T(8,128)} %param.9) | copy-start | bytes 2457604
  6.6 8.5 %copy-start.10 = (f32[1,1,768]{2,1,0:T(1,128)S(1)}, f32[1,1,768]{2,1,0:T(1,128)}, u32[]{:S(2)}) copy-start(f32[1,1,768]{2,1,0:T(1,128)} %source_state.1) | copy-start | bytes 9220
  14.4 13.8 %collective-permute-start = (f32[408,512]{1,0:T(8,128)S(1)}, f32[408,512]{1,0:T(8,128)S(1)}, u32[]{:S(2)}, u32[]{:S(2)}) collective-permute-start(f32[408,512]{1,0:T(8,128)S(1)} %get-tuple-element.75), channel_id=1, source_target_pairs={{0,4},{4,8},{8,12},{12,16},{16,20},{20,24},{24,28},{28,0},{1,5},{5... | collective-permute-start | bytes 2506760 | tf_op jit(solution)/shard_map/ppermute | solution.py:26
  34.8 2.2 %collective-permute-start.1 = (f32[1280,128]{1,0:T(8,128)S(1)}, f32[1280,128]{1,0:T(8,128)S(1)}, u32[]{:S(2)}, u32[]{:S(2)}) collective-permute-start(f32[1280,128]{1,0:T(8,128)S(1)} %slice.71), channel_id=1, source_target_pairs={{0,4},{1,5},{2,6},{3,7},{4,0},{5,1},{6,2},{7,3},{8,12},{9,13},{10,... | collective-permute-start | bytes 1966088 | tf_op jit(solution)/shard_map/ppermute | solution.py:32
  37.1 8.0 %collective-permute-start.2 = (f32[320,128]{1,0:T(8,128)S(1)}, f32[320,128]{1,0:T(8,128)S(1)}, u32[]{:S(2)}, u32[]{:S(2)}) collective-permute-start(f32[320,128]{1,0:T(8,128)S(1)} %get-tuple-element.141), channel_id=1, source_target_pairs={{0,24},{1,25},{2,26},{3,27},{4,28},{5,29},{6,30},{7,31},{8,16},{9,... | collective-permute-start | bytes 491528 | tf_op jit(solution)/shard_map/ppermute | solution.py:32
  39.5 9.2 %collective-permute-start.3 = (f32[320,128]{1,0:T(8,128)S(1)}, f32[320,128]{1,0:T(8,128)S(1)}, u32[]{:S(2)}, u32[]{:S(2)}) collective-permute-start(f32[320,128]{1,0:T(8,128)S(1)} %get-tuple-element.143), channel_id=1, source_target_pairs={{0,8},{1,9},{2,10},{3,11},{4,12},{5,13},{6,14},{7,15},{8,0},{9,1},... | collective-permute-start | bytes 491528 | tf_op jit(solution)/shard_map/ppermute | solution.py:32
  40.9 7.8 %collective-permute-start.4 = (f32[320,128]{1,0:T(8,128)S(1)}, f32[320,128]{1,0:T(8,128)S(1)}, u32[]{:S(2)}, u32[]{:S(2)}) collective-permute-start(f32[320,128]{1,0:T(8,128)S(1)} %get-tuple-element.142), channel_id=1, source_target_pairs={{0,16},{1,17},{2,18},{3,19},{4,20},{5,21},{6,22},{7,23},{8,24},{9,... | collective-permute-start | bytes 491528 | tf_op jit(solution)/shard_map/ppermute | solution.py:32
  48.7 16.9 %collective-permute-start.8 = (f32[408,512]{1,0:T(8,128)S(1)}, f32[408,512]{1,0:T(8,128)S(1)}, u32[]{:S(2)}, u32[]{:S(2)}) collective-permute-start(f32[408,512]{1,0:T(8,128)S(1)} %get-tuple-element.98), channel_id=1, source_target_pairs={{0,4},{4,8},{8,12},{12,16},{16,20},{20,24},{24,28},{28,0},{1,5},{5... | collective-permute-start | bytes 2506760 | tf_op jit(solution)/shard_map/ppermute | solution.py:26
  49.0 5.0 %collective-permute-start.5 = (f32[160,128]{1,0:T(8,128)S(1)}, f32[160,128]{1,0:T(8,128)S(1)}, u32[]{:S(2)}, u32[]{:S(2)}) collective-permute-start(f32[160,128]{1,0:T(8,128)S(1)} %slice.77), channel_id=1, source_target_pairs={{0,1},{1,0},{2,3},{3,2},{4,5},{5,4},{6,7},{7,6},{8,9},{9,8},{10,11... | collective-permute-start | bytes 245768 | tf_op jit(solution)/shard_map/ppermute | solution.py:32
  54.1 7.0 %collective-permute-start.6 = (f32[160,128]{1,0:T(8,128)S(1)}, f32[160,128]{1,0:T(8,128)S(1)}, u32[]{:S(2)}, u32[]{:S(2)}) collective-permute-start(f32[160,128]{1,0:T(8,128)S(1)} %slice_add_fusion.3), channel_id=1, source_target_pairs={{0,2},{1,3},{2,0},{3,1},{4,6},{5,7},{6,4},{7,5},{8,10},{9,11},{10,... | collective-permute-start | bytes 245768 | tf_op jit(solution)/shard_map/ppermute | solution.py:32
  61.0 4.5 %collective-permute-start.7 = (f32[160,128]{1,0:T(8,128)S(1)}, f32[160,128]{1,0:T(8,128)S(1)}, u32[]{:S(2)}, u32[]{:S(2)}) collective-permute-start(f32[160,128]{1,0:T(8,128)S(1)} %add.75), channel_id=1, source_target_pairs={{0,1},{1,0},{2,3},{3,2},{4,5},{5,4},{6,7},{7,6},{8,9},{9,8},{10,11... | collective-permute-start | bytes 245768 | tf_op jit(solution)/shard_map/ppermute | solution.py:32
  65.6 5.9 %collective-permute-start.10 = (f32[320,128]{1,0:T(8,128)S(1)}, f32[320,128]{1,0:T(8,128)S(1)}, u32[]{:S(2)}, u32[]{:S(2)}) collective-permute-start(f32[320,128]{1,0:T(8,128)S(1)} %pad_maximum_fusion.2), channel_id=1, source_target_pairs={{0,16},{1,17},{2,18},{3,19},{4,20},{5,21},{6,22},{7,23},{8,24},{9,... | collective-permute-start | bytes 491528 | tf_op jit(solution)/shard_map/ppermute | solution.py:32
  67.1 6.3 %collective-permute-start.11 = (f32[320,128]{1,0:T(8,128)S(1)}, f32[320,128]{1,0:T(8,128)S(1)}, u32[]{:S(2)}, u32[]{:S(2)}) collective-permute-start(f32[320,128]{1,0:T(8,128)S(1)} %pad_maximum_fusion.2), channel_id=1, source_target_pairs={{0,24},{1,25},{2,26},{3,27},{4,28},{5,29},{6,30},{7,31},{8,16},{9,... | collective-permute-start | bytes 491528 | tf_op jit(solution)/shard_map/ppermute | solution.py:32
  68.0 6.8 %collective-permute-start.9 = (f32[320,128]{1,0:T(8,128)S(1)}, f32[320,128]{1,0:T(8,128)S(1)}, u32[]{:S(2)}, u32[]{:S(2)}) collective-permute-start(f32[320,128]{1,0:T(8,128)S(1)} %pad_maximum_fusion.2), channel_id=1, source_target_pairs={{0,8},{1,9},{2,10},{3,11},{4,12},{5,13},{6,14},{7,15},{8,0},{9,1},... | collective-permute-start | bytes 491528 | tf_op jit(solution)/shard_map/ppermute | solution.py:32
  74.8 2.2 %collective-permute-start.12 = (f32[1280,128]{1,0:T(8,128)S(1)}, f32[1280,128]{1,0:T(8,128)S(1)}, u32[]{:S(2)}, u32[]{:S(2)}) collective-permute-start(f32[1280,128]{1,0:T(8,128)S(1)} %pad_maximum_fusion), channel_id=1, source_target_pairs={{0,4},{1,5},{2,6},{3,7},{4,0},{5,1},{6,2},{7,3},{8,12},{9,13},{10,... | collective-permute-start | bytes 1966088 | tf_op jit(solution)/shard_map/ppermute | solution.py:32
  77.0 1.8 %copy-start.3 = (s32[4,1,1]{0,2,1:T(1,128)S(1)}, s32[4,1,1]{0,2,1:T(1,128)}, u32[]{:S(2)}) copy-start(s32[4,1,1]{0,2,1:T(1,128)} %param.12) | copy-start | bytes 52
  77.0 1.8 %copy-start.9 = (s32[4,1,1,768]{3,2,1,0:T(1,128)S(1)}, s32[4,1,1,768]{3,2,1,0:T(1,128)}, u32[]{:S(2)}) copy-start(s32[4,1,1,768]{3,2,1,0:T(1,128)} %partners.7) | copy-start | bytes 36868
  85.7 12.9 %collective-permute-start.13 = (f32[408,512]{1,0:T(8,128)S(1)}, f32[408,512]{1,0:T(8,128)S(1)}, u32[]{:S(2)}, u32[]{:S(2)}) collective-permute-start(f32[408,512]{1,0:T(8,128)S(1)} %get-tuple-element.107), channel_id=1, source_target_pairs={{0,4},{4,8},{8,12},{12,16},{16,20},{20,24},{24,28},{28,0},{1,5},{5... | collective-permute-start | bytes 2506760 | tf_op jit(solution)/shard_map/ppermute | solution.py:26
  105.2 2.2 %collective-permute-start.14 = (f32[1280,128]{1,0:T(8,128)S(1)}, f32[1280,128]{1,0:T(8,128)S(1)}, u32[]{:S(2)}, u32[]{:S(2)}) collective-permute-start(f32[1280,128]{1,0:T(8,128)S(1)} %slice.79), channel_id=1, source_target_pairs={{0,4},{1,5},{2,6},{3,7},{4,0},{5,1},{6,2},{7,3},{8,12},{9,13},{10,... | collective-permute-start | bytes 1966088 | tf_op jit(solution)/shard_map/ppermute | solution.py:32
  107.5 8.1 %collective-permute-start.15 = (f32[320,128]{1,0:T(8,128)S(1)}, f32[320,128]{1,0:T(8,128)S(1)}, u32[]{:S(2)}, u32[]{:S(2)}) collective-permute-start(f32[320,128]{1,0:T(8,128)S(1)} %get-tuple-element.138), channel_id=1, source_target_pairs={{0,24},{1,25},{2,26},{3,27},{4,28},{5,29},{6,30},{7,31},{8,16},{9,... | collective-permute-start | bytes 491528 | tf_op jit(solution)/shard_map/ppermute | solution.py:32
  109.1 8.6 %collective-permute-start.16 = (f32[320,128]{1,0:T(8,128)S(1)}, f32[320,128]{1,0:T(8,128)S(1)}, u32[]{:S(2)}, u32[]{:S(2)}) collective-permute-start(f32[320,128]{1,0:T(8,128)S(1)} %get-tuple-element.140), channel_id=1, source_target_pairs={{0,8},{1,9},{2,10},{3,11},{4,12},{5,13},{6,14},{7,15},{8,0},{9,1},... | collective-permute-start | bytes 491528 | tf_op jit(solution)/shard_map/ppermute | solution.py:32
  110.0 8.3 %collective-permute-start.17 = (f32[320,128]{1,0:T(8,128)S(1)}, f32[320,128]{1,0:T(8,128)S(1)}, u32[]{:S(2)}, u32[]{:S(2)}) collective-permute-start(f32[320,128]{1,0:T(8,128)S(1)} %get-tuple-element.139), channel_id=1, source_target_pairs={{0,16},{1,17},{2,18},{3,19},{4,20},{5,21},{6,22},{7,23},{8,24},{9,... | collective-permute-start | bytes 491528 | tf_op jit(solution)/shard_map/ppermute | solution.py:32
  118.3 17.4 %collective-permute-start.21 = (f32[408,512]{1,0:T(8,128)S(1)}, f32[408,512]{1,0:T(8,128)S(1)}, u32[]{:S(2)}, u32[]{:S(2)}) collective-permute-start(f32[408,512]{1,0:T(8,128)S(1)} %get-tuple-element.132), channel_id=1, source_target_pairs={{0,4},{4,8},{8,12},{12,16},{16,20},{20,24},{24,28},{28,0},{1,5},{5... | collective-permute-start | bytes 2506760 | tf_op jit(solution)/shard_map/ppermute | solution.py:26
  118.4 5.2 %collective-permute-start.18 = (f32[160,128]{1,0:T(8,128)S(1)}, f32[160,128]{1,0:T(8,128)S(1)}, u32[]{:S(2)}, u32[]{:S(2)}) collective-permute-start(f32[160,128]{1,0:T(8,128)S(1)} %slice.85), channel_id=1, source_target_pairs={{0,1},{1,0},{2,3},{3,2},{4,5},{5,4},{6,7},{7,6},{8,9},{9,8},{10,11... | collective-permute-start | bytes 245768 | tf_op jit(solution)/shard_map/ppermute | solution.py:32
  123.6 7.6 %collective-permute-start.19 = (f32[160,128]{1,0:T(8,128)S(1)}, f32[160,128]{1,0:T(8,128)S(1)}, u32[]{:S(2)}, u32[]{:S(2)}) collective-permute-start(f32[160,128]{1,0:T(8,128)S(1)} %slice_add_fusion.2), channel_id=1, source_target_pairs={{0,2},{1,3},{2,0},{3,1},{4,6},{5,7},{6,4},{7,5},{8,10},{9,11},{10,... | collective-permute-start | bytes 245768 | tf_op jit(solution)/shard_map/ppermute | solution.py:32
  131.2 4.5 %collective-permute-start.20 = (f32[160,128]{1,0:T(8,128)S(1)}, f32[160,128]{1,0:T(8,128)S(1)}, u32[]{:S(2)}, u32[]{:S(2)}) collective-permute-start(f32[160,128]{1,0:T(8,128)S(1)} %add.81), channel_id=1, source_target_pairs={{0,1},{1,0},{2,3},{3,2},{4,5},{5,4},{6,7},{7,6},{8,9},{9,8},{10,11... | collective-permute-start | bytes 245768 | tf_op jit(solution)/shard_map/ppermute | solution.py:32
  135.7 6.5 %collective-permute-start.22 = (f32[320,128]{1,0:T(8,128)S(1)}, f32[320,128]{1,0:T(8,128)S(1)}, u32[]{:S(2)}, u32[]{:S(2)}) collective-permute-start(f32[320,128]{1,0:T(8,128)S(1)} %pad_maximum_fusion.3), channel_id=1, source_target_pairs={{0,8},{1,9},{2,10},{3,11},{4,12},{5,13},{6,14},{7,15},{8,0},{9,1},... | collective-permute-start | bytes 491528 | tf_op jit(solution)/shard_map/ppermute | solution.py:32
  136.8 8.4 %collective-permute-start.23 = (f32[320,128]{1,0:T(8,128)S(1)}, f32[320,128]{1,0:T(8,128)S(1)}, u32[]{:S(2)}, u32[]{:S(2)}) collective-permute-start(f32[320,128]{1,0:T(8,128)S(1)} %pad_maximum_fusion.3), channel_id=1, source_target_pairs={{0,16},{1,17},{2,18},{3,19},{4,20},{5,21},{6,22},{7,23},{8,24},{9,... | collective-permute-start | bytes 491528 | tf_op jit(solution)/shard_map/ppermute | solution.py:32
  138.2 7.0 %collective-permute-start.24 = (f32[320,128]{1,0:T(8,128)S(1)}, f32[320,128]{1,0:T(8,128)S(1)}, u32[]{:S(2)}, u32[]{:S(2)}) collective-permute-start(f32[320,128]{1,0:T(8,128)S(1)} %pad_maximum_fusion.3), channel_id=1, source_target_pairs={{0,24},{1,25},{2,26},{3,27},{4,28},{5,29},{6,30},{7,31},{8,16},{9,... | collective-permute-start | bytes 491528 | tf_op jit(solution)/shard_map/ppermute | solution.py:32
  145.3 2.2 %collective-permute-start.25 = (f32[1280,128]{1,0:T(8,128)S(1)}, f32[1280,128]{1,0:T(8,128)S(1)}, u32[]{:S(2)}, u32[]{:S(2)}) collective-permute-start(f32[1280,128]{1,0:T(8,128)S(1)} %pad_maximum_fusion.1), channel_id=1, source_target_pairs={{0,4},{1,5},{2,6},{3,7},{4,0},{5,1},{6,2},{7,3},{8,12},{9,13},{10,... | collective-permute-start | bytes 1966088 | tf_op jit(solution)/shard_map/ppermute | solution.py:32
  (6 other events, 5.9 us)
where the time goes:
time: 150 us
  waiting for transfers between devices  61.5 us (41%)
  Pallas kernels  53.2 us (35%)
  starting transfers between devices  25.9 us (17%)
  local copies, waits for them, and re-layouts  7.81 us (5%)
    pallas_call x10, Pallas kernels, call(): pl.pallas_call(kernel, in_specs=args_in, out_specs=outs_in or [VMEM] * le...  53.2 us
    ppermute x22, waiting for transfers between devices, exchange(): return lax.ppermute(value, AXES, pairs)  49.8 us
    ppermute x22, starting transfers between devices, exchange(): return lax.ppermute(value, AXES, pairs)  24.6 us
    ppermute x4, waiting for transfers between devices, from_behind(): return lax.ppermute(value, axis, pairs)  11.7 us
    unnamed x32, local copies, waits for them, and re-layouts  6.03 us
  transfers between devices with their start and end apart: 26, of which 22 were waited for; matrix products, arithmetic and copies ran while one was open for 1% of the time, Pallas kernels for 14%

commit v1 on v0

--- a/solution.py
+++ b/solution.py
@@ -13,6 +13,7 @@
 grad_gain = 6.0
 AXES = ("blk", "grp")
 LANES = 128
+PART = 256
 F32, BF16 = jnp.float32, jnp.bfloat16
 
 
@@ -82,11 +83,12 @@
     return count, me
 
 
-def sum_everywhere(packed, work, args):
+def sum_everywhere(packed, work, args, work_on_arrival):
     plan = reduce_plan(lax.axis_size("blk"), lax.axis_size("grp"))
     if plan is None:
         after, *rest = work(*args)
-        return lax.psum(packed, AXES), from_behind(after, "blk", 1), *rest
+        arriving = from_behind(after, "blk", 1)
+        return lax.psum(packed, AXES), arriving, *rest, *(work_on_arrival(arriving) if work_on_arrival else ())
     stages, singles = plan
     for place, stage in enumerate(stages):
         if place == 1:
@@ -101,7 +103,10 @@
     for place, stage in reversed(list(enumerate(stages))):
         if place == 1:
             packed, arriving = lax.optimization_barrier((packed, arriving))
+            rest += work_on_arrival(arriving) if work_on_arrival else []
         packed = gather(packed, stage)
+        if place == 1:
+            packed, rest = lax.optimization_barrier((packed, rest))
     return packed, arriving, *rest
 
 
@@ -141,18 +146,41 @@
     pad_ref[:width, :width] = matrix
 
 
+def parts_of(size):
+    return [slice(start, min(start + PART, size)) for start in range(0, size, PART)]
+
+
+def columns_of(refs, part, rows=None):
+    return (refs[0][:rows, part], refs[1][:rows, part])
+
+
+def split_columns(refs, compute):
+    for part in parts_of(refs[0].shape[1]):
+        high, low = split(compute(part))
+        rows = high.shape[0]
+        refs[0][:rows, part], refs[1][:rows, part] = high, low
+        if rows < refs[0].shape[0]:
+            blank = jnp.zeros((refs[0].shape[0] - rows, high.shape[1]), BF16)
+            refs[0][rows:, part], refs[1][rows:, part] = blank, blank
+
+
 def queries_into(q_refs, square_ref, x_refs, width):
-    transposed = split(square_ref[...].T[:width])
-    put_split(q_refs, dot3(*transposed, *both(x_refs), NN))
-
-
-def score_grad_into(sg_refs, q_refs, target, partner):
-    wide = q_refs[0].shape[0]
-    scores = dot3(*split(pad_rows(target, wide).T), *both(q_refs), NN)
-    expo = jnp.exp(scores - jnp.max(scores, axis=0, keepdims=True))
-    chance = expo * (1.0 / jnp.sum(expo, axis=0, keepdims=True))
-    row = lax.broadcasted_iota(jnp.int32, scores.shape, 0)
-    put_split(sg_refs, chance - jnp.where(row == partner, 1.0, 0.0))
+    turned = split(square_ref[...].T[:width])
+    split_columns(q_refs, lambda part: dot3(*turned, *columns_of(x_refs, part), NN))
+
+
+def score_grad_into(sg_refs, scores, q_refs, target_turned, partner):
+    for part in parts_of(scores.shape[1]):
+        scores[:, part] = dot3(*target_turned, *columns_of(q_refs, part), NN)
+
+    def gradient(part):
+        score = scores[:, part]
+        expo = jnp.exp(score - jnp.max(score, axis=0, keepdims=True))
+        chance = expo * (1.0 / jnp.sum(expo, axis=0, keepdims=True))
+        row = lax.broadcasted_iota(jnp.int32, score.shape, 0)
+        return chance - jnp.where(row == partner[:, part], 1.0, 0.0)
+
+    split_columns(sg_refs, gradient)
 
 
 def adagrad(values, state, gradient):
@@ -162,20 +190,28 @@
 
 def target_into(out_ref, q_refs, sg_refs, target, state):
     width = target.shape[0]
-    gradient = dot3(*both(q_refs, width), *both(sg_refs), NT)
-    out_ref[:width], out_ref[width : width + 1] = adagrad(target, state, gradient)
+    for part in parts_of(target.shape[1]):
+        gradient = dot3(*both(q_refs, width), sg_refs[0][part], sg_refs[1][part], NT)
+        out_ref[:width, part], out_ref[width : width + 1, part] = adagrad(target[:, part], state[:, part], gradient)
     rest = out_ref.shape[0] - width - 1
     out_ref[width + 1 :] = jnp.zeros((rest, target.shape[1]), F32)
 
 
 def query_grad_into(g_refs, sg_refs, target):
-    put_split(g_refs, dot3(*split(target), *both(sg_refs), NN))
+    halves = split(target)
+    split_columns(g_refs, lambda part: dot3(*halves, *columns_of(sg_refs, part), NN))
+
+
+def operator_grad(x_halves, g_refs):
+    return jnp.concatenate(
+        [dot3(*x_halves, g_refs[0][part], g_refs[1][part], NT) for part in parts_of(g_refs[0].shape[0])], axis=1)
 
 
 def source_into(x_out, state_out, square_ref, g_refs, source, state):
-    width = source.shape[0]
-    gradient = dot3(*split(square_ref[:width]), *both(g_refs), NN)
-    x_out[...], state_out[...] = adagrad(source, state, gradient)
+    halves = split(square_ref[: source.shape[0]])
+    for part in parts_of(source.shape[1]):
+        gradient = dot3(*halves, *columns_of(g_refs, part), NN)
+        x_out[:, part], state_out[:, part] = adagrad(source[:, part], state[:, part], gradient)
 
 
 def pack_into(out_ref, parts, kinds):
@@ -211,22 +247,21 @@
     return round_up(kinds * (width // LANES) * width + tail_span(width, kinds), 8 * pieces)
 
 
-def unpack(flat_ref, scaled_out, kinds, width, scale):
-    full, tail = divmod(width, LANES)
+def unpack(flat_ref, scaled_out, kind, width, scale):
+    kinds, (full, tail) = scaled_out.shape[0], divmod(width, LANES)
     span = tail_span(width, kinds)
-    for kind in range(kinds):
-        for block in range(full):
-            start = (kind * full + block) * width
-            scaled_out[kind, :, block * LANES : (block + 1) * LANES] = scale * flat_ref[start : start + width]
-        if tail:
-            start = kinds * full * width
-            ends = flat_ref[start : start + span]
-            places = -(-width // span)
-            for place in range(places):
-                rows = min(span, width - place * span)
-                turn = (kind * places + place) * tail
-                moved = pltpu.roll(ends, LANES - turn, 1) if turn else ends
-                scaled_out[kind, place * span : place * span + rows, full * LANES :] = scale * moved[:rows, :tail]
+    for block in range(full):
+        start = (kind * full + block) * width
+        scaled_out[kind, :, block * LANES : (block + 1) * LANES] = scale * flat_ref[start : start + width]
+    if tail:
+        start = kinds * full * width
+        ends = flat_ref[start : start + span]
+        places = -(-width // span)
+        for place in range(places):
+            rows = min(span, width - place * span)
+            turn = (kind * places + place) * tail
+            moved = pltpu.roll(ends, LANES - turn, 1) if turn else ends
+            scaled_out[kind, place * span : place * span + rows, full * LANES :] = scale * moved[:rows, :tail]
 
 
 def put_pieces(out_ref, in_ref, me, pieces):
@@ -235,82 +270,106 @@
         out_ref[piece * rows : (piece + 1) * rows] = in_ref[pl.ds(pl.multiple_of((me ^ piece) * rows, 8), rows)]
 
 
-def first_kernel(ids, me, partners, relations, source, target, *refs, bucket, updated):
-    if updated:
-        target_out, sgh, sgl, square, xh, xl, qh, ql = refs
-        square_of(square, relations[ids[bucket]])
-        put_split((xh, xl), source[...])
-        body, state = target[: source.shape[0]], target[source.shape[0] : source.shape[0] + 1]
-        queries_into((qh, ql), square, (xh, xl), source.shape[0])
-    else:
-        target_state, target_out, sgh, sgl, square, xh, xl, qh, ql, matrix, source_in, target_in, sems = refs
-        loads = [
-            pltpu.make_async_copy(relations.at[ids[bucket]], matrix, sems.at[0]),
-            pltpu.make_async_copy(source, source_in, sems.at[1]),
-            pltpu.make_async_copy(target, target_in, sems.at[2]),
-        ]
-        for load in loads:
-            load.start()
-        loads[0].wait()
-        square_of(square, matrix[...])
-        loads[1].wait()
-        put_split((xh, xl), source_in[...])
-        queries_into((qh, ql), square, (xh, xl), source.shape[0])
-        loads[2].wait()
-        body, state = target_in[...], target_state[0]
-    score_grad_into((sgh, sgl), (qh, ql), body, partners[bucket, 0])
-    target_into(target_out, (qh, ql), (sgh, sgl), body, state)
-
-
-def update_kernel(me, packed, relations, *refs, pieces, scale, place, last):
-    grads_out, relations_out, flat, scaled, sems = refs[1 if place else 0 :][:5]
-    kinds, width = relations.shape[0], relations.shape[1]
+def opening_kernel(me, ids, partners, relations, source, target, target_state, target_out, sgh, sgl, square, xh, xl, qh, ql, scores, matrix, source_in, target_in, state_in, partners_in, ids_in, sems):
+    width = source.shape[0]
+    pairs = ((ids, ids_in), (source, source_in), (relations, matrix), (target, target_in), (target_state, state_in), (partners.at[0], partners_in))
+    loads = [pltpu.make_async_copy(here, there, sems.at[place]) for place, (here, there) in enumerate(pairs)]
+    for load in loads:
+        load.start()
+    loads[1].wait()
+    put_split((xh, xl), source_in[...])
+    loads[0].wait()
+    loads[2].wait()
+    square_of(square, matrix[ids_in[0]])
+    queries_into((qh, ql), square, (xh, xl), width)
+    for load in loads[3:]:
+        load.wait()
+    body = target_in[...]
+    score_grad_into((sgh, sgl), scores, (qh, ql), split(pad_rows(body, qh.shape[0]).T), partners_in[0])
+    target_into(target_out, (qh, ql), (sgh, sgl), body, state_in[0])
+
+
+def prepare_kernel(target, yh, yl, *, width):
+    yh[...], yl[...] = split(pad_rows(target[:width], yh.shape[1]).T)
+
+
+def renew(flat, relations, scaled, renewed, kind, scale):
+    unpack(flat, scaled, kind, relations.shape[1], scale)
+    renewed[kind] = relations[kind] - operator_rate * scaled[kind]
+
+
+def first_kernel(ids, me, partners, packed, relations, xh, xl, target, yh, yl, relations_out, scaled, target_out, sgh, sgl, flat, square, qh, ql, scores, *, bucket, pieces, scale):
+    width = relations.shape[1]
     put_pieces(flat, packed, me[0], pieces)
-    unpack(flat, scaled, kinds, width, scale)
-    stores = [pltpu.make_async_copy(scaled, grads_out.at[place], sems.at[0])]
-    stores[0].start()
-    renewed = refs[-1] if last else relations_out
-    for kind in range(kinds):
-        renewed[kind] = relations[kind] - operator_rate * scaled[kind]
-    if last:
-        stores.append(pltpu.make_async_copy(renewed, relations_out, sems.at[1]))
-        stores[1].start()
+    for kind in range(relations.shape[0]):
+        renew(flat, relations, scaled, relations_out, kind, scale)
+    square_of(square, relations_out[ids[bucket]])
+    queries_into((qh, ql), square, (xh, xl), width)
+    score_grad_into((sgh, sgl), scores, (qh, ql), both((yh, yl)), partners[bucket, 0])
+    target_into(target_out, (qh, ql), (sgh, sgl), target[:width], target[width : width + 1])
+
+
+def closing_kernel(me, packed, relations, *refs, pieces, scale, place):
+    grads_out, relations_out, flat, scaled, renewed, sems = refs[1 if place else 0 :]
+    put_pieces(flat, packed, me[0], pieces)
+    stores = []
+    for kind in range(relations.shape[0]):
+        renew(flat, relations, scaled, renewed, kind, scale)
+        for here, there in ((scaled, grads_out.at[place]), (renewed, relations_out)):
+            stores.append(pltpu.make_async_copy(here.at[kind], there.at[kind], sems.at[len(stores)]))
+            stores[-1].start()
     for store in stores:
         store.wait()
 
 
-def second_kernel(ids, relations, source, source_state, target, sgh, sgl, source_out, state_out, grad_out, qh, ql, square, xh, xl, gh, gl, *, bucket):
+def second_kernel(ids, relations, source, source_state, target, sgh, sgl, *refs, bucket, place):
+    if place is None:
+        source_out, state_out, grad_out, qh, ql, xh, xl, square, gh, gl = refs
+    else:
+        scaled, *refs = refs
+        source_out, state_out, grad_out, qh, ql, xh, xl, grads_out, square, gh, gl, sem = refs[1 if place else 0 :]
+        store = pltpu.make_async_copy(scaled, grads_out.at[place], sem.at[0])
+        store.start()
     width = source.shape[0]
     query_grad_into((gh, gl), (sgh, sgl), target[:width])
     put_split((xh, xl), source[...])
-    grad_out[...] = dot3(*both((xh, xl), width), *both((gh, gl)), NT)
+    grad_out[...] = operator_grad(both((xh, xl), width), (gh, gl))
     square_of(square, relations[ids[bucket]])
     source_into(source_out, state_out.at[0], square, (gh, gl), source[...], source_state[0])
     square_of(square, relations[ids[bucket + 1]])
     put_split((xh, xl), source_out[...])
     queries_into((qh, ql), square, (xh, xl), width)
-
-
-def third_kernel(ids, me, partners, source, target, qh, ql, grad_before, packed, sgh, sgl, gh, gl, flat, *, bucket, kinds, pieces):
-    width = source.shape[0]
+    if place is not None:
+        store.wait()
+
+
+def third_kernel(ids, me, partners, xh, xl, target, qh, ql, grad_before, packed, sgh, sgl, gh, gl, flat, scores, *, bucket, kinds, pieces):
+    width = grad_before.shape[0]
     body = target[:width]
-    score_grad_into((sgh, sgl), (qh, ql), body, partners[bucket, 0])
+    score_grad_into((sgh, sgl), scores, (qh, ql), split(pad_rows(body, qh.shape[0]).T), partners[bucket, 0])
     query_grad_into((gh, gl), (sgh, sgl), body)
-    grad = dot3(*split(source[...]), *both((gh, gl)), NT)
+    grad = operator_grad(both((xh, xl), width), (gh, gl))
     pack_into(flat, ((ids[bucket - 1], grad_before[...]), (ids[bucket], grad)), kinds)
     put_pieces(packed, flat, me[0], pieces)
 
 
-def fourth_kernel(ids, relations, source, source_state, target, qh, ql, sgh, sgl, gh, gl, target_out, source_out, state_out, square, *, bucket):
+def fourth_kernel(ids, relations, source, source_state, target, qh, ql, sgh, sgl, gh, gl, target_out, source_out, state_out, *refs, bucket):
     width = source.shape[0]
     target_into(target_out, (qh, ql), (sgh, sgl), target[:width], target[width : width + 1])
+    square = refs[-1]
     square_of(square, relations[ids[bucket]])
     source_into(source_out, state_out.at[0], square, (gh, gl), source[...], source_state[0])
+    if len(refs) > 1:
+        put_split(refs[:2], source_out[...])
 
 
 VMEM = pl.BlockSpec(memory_space=pltpu.VMEM)
 SMEM = pl.BlockSpec(memory_space=pltpu.SMEM)
 HBM = pl.BlockSpec(memory_space=pltpu.HBM)
+
+
+def in_hbm(x):
+    return pltpu.with_memory_space_constraint(x, pltpu.HBM)
 
 
 def call(kernel, name, args, args_in, outs, scratch=(), flops=0, outs_in=None, aliases=None):
@@ -344,42 +403,61 @@
     sg_pair = [((block, columns), BF16)] * 2
     square = [((wide, wide), F32)]
     moving = [((tall, block), F32)]
+    scores = [((block, columns), F32)]
     source_outs = [((width, columns), F32), (source_state.shape, F32)]
     product = 6 * width * width * columns
     updates = buckets // 2
-    grads = ()
+    rel_out, flat, y_pair = (relations.shape, F32), ((rows, LANES), F32), [((block, wide), BF16)] * 2
+    grads, grads_out = None, ((updates, *relations.shape), F32)
     for update in range(updates):
-        bucket = 2 * update
-        args, args_in, extra = (ids, me, positives, relations, source, target), [SMEM] * 2 + [VMEM] * 4, []
+        bucket, last = 2 * update, update == updates - 1
         if update == 0:
-            args, args_in = args + (target_state,), [SMEM] * 2 + [VMEM] + [HBM] * 3 + [VMEM]
-            extra = [((width, width), F32), (source.shape, F32), (target.shape, F32), pltpu.SemaphoreType.DMA((3,))]
-        after, sgh, sgl = call(
-            functools.partial(first_kernel, bucket=bucket, updated=update > 0), "first",
-            args, args_in, moving + sg_pair, square + q_pair + q_pair + extra, 3 * product)
+            after, sgh, sgl = call(
+                opening_kernel, "opening",
+                [me, *(in_hbm(x) for x in (ids, positives, relations, source, target, target_state))], [SMEM] + [HBM] * 6, moving + sg_pair,
+                square + q_pair + q_pair + scores + [
+                    (relations.shape, F32), (source.shape, F32), (target.shape, F32), (target_state.shape, F32),
+                    (positives.shape[1:], jnp.int32), pltpu.SMEM(ids.shape, jnp.int32), pltpu.SemaphoreType.DMA((6,))],
+                3 * product)
+        else:
+            relations, scaled, after, sgh, sgl = call(
+                functools.partial(first_kernel, bucket=bucket, pieces=pieces, scale=scale), "first",
+                (ids, me, positives, total, relations, xh, xl, target, yh, yl), [SMEM] * 2 + [VMEM] * 8,
+                [rel_out, rel_out] + moving + sg_pair, [flat] + square + q_pair + scores, 3 * product)
         arriving = from_behind(after, "blk", 1)
-        source, state, grad, qh, ql = call(
-            functools.partial(second_kernel, bucket=bucket), "second",
-            (ids, relations, source, state, target, sgh, sgl), [SMEM] + [VMEM] * 6,
-            source_outs + [((width, wide), F32)] + q_pair, square + q_pair + q_pair, 4 * product)
+        args, outs = (ids, relations, source, state, target, sgh, sgl), source_outs + [((width, wide), F32)] + q_pair + q_pair
+        if update == 0:
+            source, state, grad, qh, ql, xh, xl = call(
+                functools.partial(second_kernel, bucket=bucket, place=None), "second",
+                args, [SMEM] + [VMEM] * 6, outs, square + q_pair, 4 * product)
+        else:
+            before = () if grads is None else (grads,)
+            source, state, grad, qh, ql, xh, xl, grads = call(
+                functools.partial(second_kernel, bucket=bucket, place=update - 1), "second",
+                (*args, scaled, *before), [SMEM] + [VMEM] * 7 + [HBM] * len(before), outs + [grads_out],
+                square + q_pair + [pltpu.SemaphoreType.DMA((1,))], 4 * product,
+                [VMEM] * len(outs) + [HBM], {8: len(outs)} if before else None)
         target = arriving
         packed, sgh, sgl, gh, gl = call(
             functools.partial(third_kernel, bucket=bucket + 1, kinds=kinds, pieces=pieces), "third",
-            (ids, me, positives, source, target, qh, ql, grad), [SMEM] * 2 + [VMEM] * 6,
-            [((rows, LANES), F32)] + sg_pair + q_pair, [((rows, LANES), F32)], 3 * product)
-        total, target, source, state = sum_everywhere(
+            (ids, me, positives, xh, xl, target, qh, ql, grad), [SMEM] * 2 + [VMEM] * 7,
+            [flat] + sg_pair + q_pair, [flat] + scores, 3 * product)
+        total, target, source, state, *prepared = sum_everywhere(
             packed,
             lambda *args: call(
                 functools.partial(fourth_kernel, bucket=bucket + 1), "fourth",
-                (ids, *args), [SMEM] + [VMEM] * len(args), moving + source_outs, square, 2 * product),
-            (relations, source, state, target, qh, ql, sgh, sgl, gh, gl))
-        last = update == updates - 1
-        grads, relations = call(
-            functools.partial(update_kernel, pieces=pieces, scale=scale, place=update, last=last), "update",
-            (me, total, relations, *((grads,) if update else ())), [SMEM, VMEM, VMEM] + ([HBM] if update else []),
-            [((updates, *relations.shape), F32), (relations.shape, F32)],
-            [((rows, LANES), F32), (relations.shape, F32), pltpu.SemaphoreType.DMA((2,))] + ([(relations.shape, F32)] if last else []),
-            product, [HBM, HBM if last else VMEM], {3: 0} if update else None)
+                (ids, *args), [SMEM] + [VMEM] * len(args), moving + source_outs + ([] if last else q_pair), square, 2 * product),
+            (relations, source, state, target, qh, ql, sgh, sgl, gh, gl),
+            None if last else lambda target: call(
+                functools.partial(prepare_kernel, width=width), "prepare", (target,), [VMEM], y_pair, (), product // 4))
+        if not last:
+            xh, xl, yh, yl = prepared
+    before = () if grads is None else (grads,)
+    grads, relations = call(
+        functools.partial(closing_kernel, pieces=pieces, scale=scale, place=updates - 1), "closing",
+        (me, total, relations, *before), [SMEM, VMEM, VMEM] + [HBM] * len(before),
+        [grads_out, rel_out], [flat, rel_out, rel_out, pltpu.SemaphoreType.DMA((2 * kinds,))],
+        product, [HBM, HBM], {3: 0} if before else None)
     return (
         source[None, None],
         state,

time: 150 us -> 135 us (0.900)
  Pallas kernels: 53.2 us -> 42.6 us
  local copies, waits for them, and re-layouts: 7.81 us -> 1.72 us
  waiting for transfers between devices: 61.5 us -> 63.2 us
    pallas_call x10, Pallas kernels: 53.2 us -> 42.6 us  [call(): pl.pallas_call(kernel, in_specs=args_in, out_specs=outs_in or [VMEM] * le...]
    unnamed x32 -> x12, local copies, waits for them, and re-layouts: 6.03 us -> 0.03 us
    ppermute x4, waiting for transfers between devices: 11.7 us -> 15.1 us  [from_behind(): return lax.ppermute(value, axis, pairs)]
    ppermute x22, waiting for transfers between devices: 49.8 us -> 48.1 us  [exchange(): return lax.ppermute(value, AXES, pairs)]
  transfers between devices with their start and end apart: 26 -> 26, of which waited for: 22 -> 24; matrix products, arithmetic and copies ran while one was open for 1% -> 1% of each run, Pallas kernels for 14% -> 14%
where the time goes in v1:
time: 135 us
  waiting for transfers between devices  63.2 us (47%)
  Pallas kernels  42.6 us (32%)
  starting transfers between devices  25.8 us (19%)
  local copies, waits for them, and re-layouts  1.72 us (1%)
    ppermute x22, waiting for transfers between devices, exchange(): return lax.ppermute(value, AXES, pairs)  48.1 us
    pallas_call x10, Pallas kernels, call(): pl.pallas_call(kernel, in_specs=args_in, out_specs=outs_in or [VMEM] * le...  42.6 us
    ppermute x22, starting transfers between devices, exchange(): return lax.ppermute(value, AXES, pairs)  24.5 us
    ppermute x4, waiting for transfers between devices, from_behind(): return lax.ppermute(value, axis, pairs)  15.1 us
  transfers between devices with their start and end apart: 26, of which 24 were waited for; matrix products, arithmetic and copies ran while one was open for 1% of the time, Pallas kernels for 14%

profile of v1, /device:TPU:0, one launch (start us, length us, event | category | flops | bytes accessed | tf_op | source)
XLA Modules:
  0.0 135.0 jit_solution(11296658388283923676)
XLA Ops:
  0.7 7.0 %opening.1 = (f32[408,512]{1,0:T(8,128)S(1)}, bf16[512,768]{1,0:T(8,128)(2,1)S(1)}, bf16[512,768]{1,0:T(8,128)(2,1)S(1)}) custom-call(s32[1]{0:T(128)} %bitcast.1.me, s32[4]{0:T(128)} %bitcast.9, s32[4,1,1,768]{3,2,1,0:T(1,128)} %partners.7, f32[2,400,400]{2,1,0:T(8,128)} %relations.6, f32[400,768]{1,0:T(8,128)} %bitcast.17, f32[400,512]{1,0:T(8,128)} %bitcast.19, ...), custom_call_target="tpu_custom_call" | custom-call | flops 2211840000 | tf_op jit(solution)/shard_map/opening/pallas_call | solution.py:376
  8.5 5.2 %second.2 = (f32[400,768]{1,0:T(8,128)S(1)}, f32[1,1,768]{2,1,0:T(1,128)S(1)}, f32[400,512]{1,0:T(8,128)S(1)}, bf16[512,768]{1,0:T(8,128)(2,1)S(1)}, bf16[512,76...) custom-call(s32[4]{0:T(128)S(1)} %bitcast.10, f32[2,400,400]{2,1,0:T(8,128)S(1)} %copy-done, ...), custom_call_target="tpu_custom_call" | custom-call | flops 2949120000 | tf_op jit(solution)/shard_map/second/pallas_call | solution.py:376
  13.7 7.8 %collective-permute-done.target = f32[408,512]{1,0:T(8,128)S(1)} collective-permute-done((f32[408,512]{1,0:T(8,128)S(1)}, f32[408,512]{1,0:T(8,128)S(1)}, u32[]{:S(2)}, u32[]{:S(2)}) %collective-permute-start) | collective-permute-done | bytes 835616 | tf_op jit(solution)/shard_map/ppermute | solution.py:27
  21.6 4.8 %third.2 = (f32[2560,128]{1,0:T(8,128)S(1)}, bf16[512,768]{1,0:T(8,128)(2,1)S(1)}, bf16[512,768]{1,0:T(8,128)(2,1)S(1)}, bf16[512,768]{1,0:T(8,128)(2,1)S(1)}, bf16[512,768]{1,0:T(8,128)(2,1)S(1)}) custom-call(s32[4]{0:T(128)S(1)} %bitcast.11, s32[1]{0:T(128)} %bitcast.1.me, s32[4,1,1,768]{3,2,1,0:T(1,128)S(1)} %copy-done.4, ...), custom_call_target="tpu_custom_call" | custom-call | flops 2211840000 | tf_op jit(solution)/shard_map/third/pallas_call | solution.py:376
  26.5 2.1 %collective-permute-done.1 = f32[1280,128]{1,0:T(8,128)S(1)} collective-permute-done((f32[1280,128]{1,0:T(8,128)S(1)}, f32[1280,128]{1,0:T(8,128)S(1)}, u32[]{:S(2)}, u32[]{:S(2)}) %collective-permute-start.1) | collective-permute-done | bytes 655392 | tf_op jit(solution)/shard_map/ppermute | solution.py:33
  28.7 2.4 %collective-permute-start.2 = (f32[320,128]{1,0:T(8,128)S(1)}, f32[320,128]{1,0:T(8,128)S(1)}, u32[]{:S(2)}, u32[]{:S(2)}) collective-permute-start(f32[320,128]{1,0:T(8,128)S(1)} %get-tuple-element.179), channel_id=1, source_target_pairs={{0,24},{1,25},{2,26},{3,27},{4,28},{5,29},{6,30},{7,31},{8,16},{9,... | collective-permute-start | bytes 491528 | tf_op jit(solution)/shard_map/ppermute | solution.py:33
  32.5 3.4 %fourth.2 = (f32[408,512]{1,0:T(8,128)S(1)}, f32[400,768]{1,0:T(8,128)S(1)}, f32[1,1,768]{2,1,0:T(1,128)S(1)}, bf16[512,768]{1,0:T(8,128)(2,1)S(1)}, bf16[512,768]{1,0:T(8,128)(2,1)S(1)}) custom-call(s32[4]{0:T(128)S(1)} %bitcast.12, f32[2,400,400]{2,1,0:T(8,128)S(1)} %copy-done, f32[400,768]{1,0:T(8,128)S(1)} %get-tuple-element.108.source, ...), custom_call_target="tpu_custom_call" | custom-call | flops 1474560000 | tf_op jit(solution)/shard_map/fourth/pallas_call | solution.py:376
  36.7 2.7 %collective-permute-done.4 = f32[320,128]{1,0:T(8,128)S(1)} collective-permute-done((f32[320,128]{1,0:T(8,128)S(1)}, f32[320,128]{1,0:T(8,128)S(1)}, u32[]{:S(2)}, u32[]{:S(2)}) %collective-permute-start.4) | collective-permute-done | bytes 163872 | tf_op jit(solution)/shard_map/ppermute | solution.py:33
  40.6 1.6 %collective-permute-start.5 = (f32[160,128]{1,0:T(8,128)S(1)}, f32[160,128]{1,0:T(8,128)S(1)}, u32[]{:S(2)}, u32[]{:S(2)}) collective-permute-start(f32[160,128]{1,0:T(8,128)S(1)} %slice.77), channel_id=1, source_target_pairs={{0,1},{1,0},{2,3},{3,2},{4,5},{5,4},{6,7},{7,6},{8,9},{9,8},{10,11... | collective-permute-start | bytes 245768 | tf_op jit(solution)/shard_map/ppermute | solution.py:33
  42.2 3.4 %collective-permute-done.5 = f32[160,128]{1,0:T(8,128)S(1)} collective-permute-done((f32[160,128]{1,0:T(8,128)S(1)}, f32[160,128]{1,0:T(8,128)S(1)}, u32[]{:S(2)}, u32[]{:S(2)}) %collective-permute-start.5) | collective-permute-done | bytes 81952 | tf_op jit(solution)/shard_map/ppermute | solution.py:33
  45.6 2.6 %collective-permute-start.6 = (f32[160,128]{1,0:T(8,128)S(1)}, f32[160,128]{1,0:T(8,128)S(1)}, u32[]{:S(2)}, u32[]{:S(2)}) collective-permute-start(f32[160,128]{1,0:T(8,128)S(1)} %slice_add_fusion.3), channel_id=1, source_target_pairs={{0,2},{1,3},{2,0},{3,1},{4,6},{5,7},{6,4},{7,5},{8,10},{9,11},{10,... | collective-permute-start | bytes 245768 | tf_op jit(solution)/shard_map/ppermute | solution.py:33
  48.3 4.3 %collective-permute-done.6 = f32[160,128]{1,0:T(8,128)S(1)} collective-permute-done((f32[160,128]{1,0:T(8,128)S(1)}, f32[160,128]{1,0:T(8,128)S(1)}, u32[]{:S(2)}, u32[]{:S(2)}) %collective-permute-start.6) | collective-permute-done | bytes 81952 | tf_op jit(solution)/shard_map/ppermute | solution.py:33
  53.2 3.9 %collective-permute-done.7 = f32[160,128]{1,0:T(8,128)S(1)} collective-permute-done((f32[160,128]{1,0:T(8,128)S(1)}, f32[160,128]{1,0:T(8,128)S(1)}, u32[]{:S(2)}, u32[]{:S(2)}) %collective-permute-start.7) | collective-permute-done | bytes 81952 | tf_op jit(solution)/shard_map/ppermute | solution.py:33
  57.2 2.0 %collective-permute-start.11 = (f32[320,128]{1,0:T(8,128)S(1)}, f32[320,128]{1,0:T(8,128)S(1)}, u32[]{:S(2)}, u32[]{:S(2)}) collective-permute-start(f32[320,128]{1,0:T(8,128)S(1)} %pad_maximum_fusion.4), channel_id=1, source_target_pairs={{0,24},{1,25},{2,26},{3,27},{4,28},{5,29},{6,30},{7,31},{8,16},{9,... | collective-permute-start | bytes 491528 | tf_op jit(solution)/shard_map/ppermute | solution.py:33
  61.1 3.9 %collective-permute-done.11 = f32[320,128]{1,0:T(8,128)S(1)} collective-permute-done((f32[320,128]{1,0:T(8,128)S(1)}, f32[320,128]{1,0:T(8,128)S(1)}, u32[]{:S(2)}, u32[]{:S(2)}) %collective-permute-start.11) | collective-permute-done | bytes 163872 | tf_op jit(solution)/shard_map/ppermute | solution.py:33
  66.1 2.1 %collective-permute-done.12 = f32[1280,128]{1,0:T(8,128)S(1)} collective-permute-done((f32[1280,128]{1,0:T(8,128)S(1)}, f32[1280,128]{1,0:T(8,128)S(1)}, u32[]{:S(2)}, u32[]{:S(2)}) %collective-permute-start.12) | collective-permute-done | bytes 655392 | tf_op jit(solution)/shard_map/ppermute | solution.py:33
  68.3 5.5 %first.1 = (f32[2,400,400]{2,1,0:T(8,128)S(1)}, f32[2,400,400]{2,1,0:T(8,128)S(1)}, f32[408,512]{1,0:T(8,128)S(1)}, bf16[512,768]{1,0:T(8,128)(2,1)S(1)}, bf16[512,768]{1,0:T(8,128)(2,1)S(1)}) custom-call(s32[4]{0:T(128)S(1)} %bitcast.13, s32[1]{0:T(128)} %bitcast.1.me, s32[4,1,1,768]{3,2,1,0:T(1,128)S(1)} %copy-done.4, ...), custom_call_target="tpu_custom_call" | custom-call | flops 2211840000 | tf_op jit(solution)/shard_map/first/pallas_call | solution.py:376
  74.0 5.4 %second.3 = (f32[400,768]{1,0:T(8,128)S(1)}, f32[1,1,768]{2,1,0:T(1,128)S(1)}, f32[400,512]{1,0:T(8,128)S(1)}, bf16[512,768]{1,0:T(8,128)(2,1)S(1)}, bf16[512,76...) custom-call(s32[4]{0:T(128)S(1)} %bitcast.14, ...), custom_call_target="tpu_custom_call" | custom-call | flops 2949120000 | tf_op jit(solution)/shard_map/second/pallas_call | solution.py:376
  79.4 7.3 %collective-permute-done.13.target = f32[408,512]{1,0:T(8,128)S(1)} collective-permute-done((f32[408,512]{1,0:T(8,128)S(1)}, f32[408,512]{1,0:T(8,128)S(1)}, u32[]{:S(2)}, u32[]{:S(2)}) %collective-permute-start.13) | collective-permute-done | bytes 835616 | tf_op jit(solution)/shard_map/ppermute | solution.py:27
  86.7 4.7 %third.3 = (f32[2560,128]{1,0:T(8,128)S(1)}, bf16[512,768]{1,0:T(8,128)(2,1)S(1)}, bf16[512,768]{1,0:T(8,128)(2,1)S(1)}, bf16[512,768]{1,0:T(8,128)(2,1)S(1)}, bf16[512,768]{1,0:T(8,128)(2,1)S(1)}) custom-call(s32[4]{0:T(128)S(1)} %bitcast.15, s32[1]{0:T(128)} %bitcast.1.me, s32[4,1,1,768]{3,2,1,0:T(1,128)S(1)} %copy-done.4, ...), custom_call_target="tpu_custom_call" | custom-call | flops 2211840000 | tf_op jit(solution)/shard_map/third/pallas_call | solution.py:376
  91.6 2.1 %collective-permute-done.14 = f32[1280,128]{1,0:T(8,128)S(1)} collective-permute-done((f32[1280,128]{1,0:T(8,128)S(1)}, f32[1280,128]{1,0:T(8,128)S(1)}, u32[]{:S(2)}, u32[]{:S(2)}) %collective-permute-start.14) | collective-permute-done | bytes 655392 | tf_op jit(solution)/shard_map/ppermute | solution.py:33
  94.7 1.4 %collective-permute-start.17 = (f32[320,128]{1,0:T(8,128)S(1)}, f32[320,128]{1,0:T(8,128)S(1)}, u32[]{:S(2)}, u32[]{:S(2)}) collective-permute-start(f32[320,128]{1,0:T(8,128)S(1)} %get-tuple-element.177), channel_id=1, source_target_pairs={{0,16},{1,17},{2,18},{3,19},{4,20},{5,21},{6,22},{7,23},{8,24},{9,... | collective-permute-start | bytes 491528 | tf_op jit(solution)/shard_map/ppermute | solution.py:33
  97.3 4.1 %fourth.3 = (f32[408,512]{1,0:T(8,128)S(1)}, f32[400,768]{1,0:T(8,128)}, f32[1,1,768]{2,1,0:T(1,128)}) custom-call(s32[4]{0:T(128)S(1)} %bitcast.16, f32[2,400,400]{2,1,0:T(8,128)S(1)} %get-tuple-element.153.relations, f32[400,768]{1,0:T(8,128)S(1)} %get-tuple-element.154.source, f32[1,1,768]{2,1,0:T(1,128)S(1)} %get-tuple-element.155.source_state, ...), custom_call_target="tpu_custom_call" | custom-call | flops 1474560000 | tf_op jit(solution)/shard_map/fourth/pallas_call | solution.py:376
  101.8 2.3 %collective-permute-done.17 = f32[320,128]{1,0:T(8,128)S(1)} collective-permute-done((f32[320,128]{1,0:T(8,128)S(1)}, f32[320,128]{1,0:T(8,128)S(1)}, u32[]{:S(2)}, u32[]{:S(2)}) %collective-permute-start.17) | collective-permute-done | bytes 163872 | tf_op jit(solution)/shard_map/ppermute | solution.py:33
  104.7 1.3 collective-permute-start.18
  105.9 4.0 %collective-permute-done.18 = f32[160,128]{1,0:T(8,128)S(1)} collective-permute-done((f32[160,128]{1,0:T(8,128)S(1)}, f32[160,128]{1,0:T(8,128)S(1)}, u32[]{:S(2)}, u32[]{:S(2)}) %collective-permute-start.18) | collective-permute-done | bytes 81952 | tf_op jit(solution)/shard_map/ppermute | solution.py:33
  109.9 3.1 %collective-permute-start.19 = (f32[160,128]{1,0:T(8,128)S(1)}, f32[160,128]{1,0:T(8,128)S(1)}, u32[]{:S(2)}, u32[]{:S(2)}) collective-permute-start(f32[160,128]{1,0:T(8,128)S(1)} %slice_add_fusion.2), channel_id=1, source_target_pairs={{0,2},{1,3},{2,0},{3,1},{4,6},{5,7},{6,4},{7,5},{8,10},{9,11},{10,... | collective-permute-start | bytes 245768 | tf_op jit(solution)/shard_map/ppermute | solution.py:33
  113.0 4.2 %collective-permute-done.19 = f32[160,128]{1,0:T(8,128)S(1)} collective-permute-done((f32[160,128]{1,0:T(8,128)S(1)}, f32[160,128]{1,0:T(8,128)S(1)}, u32[]{:S(2)}, u32[]{:S(2)}) %collective-permute-start.19) | collective-permute-done | bytes 81952 | tf_op jit(solution)/shard_map/ppermute | solution.py:33
  117.8 3.9 %collective-permute-done.20 = f32[160,128]{1,0:T(8,128)S(1)} collective-permute-done((f32[160,128]{1,0:T(8,128)S(1)}, f32[160,128]{1,0:T(8,128)S(1)}, u32[]{:S(2)}, u32[]{:S(2)}) %collective-permute-start.20) | collective-permute-done | bytes 81952 | tf_op jit(solution)/shard_map/ppermute | solution.py:33
  122.3 1.8 %collective-permute-start.23 = (f32[320,128]{1,0:T(8,128)S(1)}, f32[320,128]{1,0:T(8,128)S(1)}, u32[]{:S(2)}, u32[]{:S(2)}) collective-permute-start(f32[320,128]{1,0:T(8,128)S(1)} %pad_maximum_fusion.5), channel_id=1, source_target_pairs={{0,16},{1,17},{2,18},{3,19},{4,20},{5,21},{6,22},{7,23},{8,24},{9,... | collective-permute-start | bytes 491528 | tf_op jit(solution)/shard_map/ppermute | solution.py:33
  125.3 4.2 %collective-permute-done.24 = f32[320,128]{1,0:T(8,128)S(1)} collective-permute-done((f32[320,128]{1,0:T(8,128)S(1)}, f32[320,128]{1,0:T(8,128)S(1)}, u32[]{:S(2)}, u32[]{:S(2)}) %collective-permute-start.24) | collective-permute-done | bytes 163872 | tf_op jit(solution)/shard_map/ppermute | solution.py:33
  132.7 2.1 %closing.1 = (f32[2,2,400,400]{3,2,1,0:T(8,128)}, f32[2,400,400]{2,1,0:T(8,128)}) custom-call(s32[1]{0:T(128)} %bitcast.1.me, f32[2560,128]{1,0:T(8,128)S(1)} %pad_maximum_fusion.1.packed, f32[2,400,400]{2,1,0:T(8,128)S(1)} %get-tuple-element.153.relations, f32[2,2,400,400]{3,2,1,0:T(8,128)} %get-tuple-element.173.refs_0_), custom_call_target="tpu_custom_call", output_to_operand_aliasing={{0}: (3, {})} | custom-call | flops 737280000 | tf_op jit(solution)/shard_map/closing/pallas_call | solution.py:376
  (64 shorter events, 17.1 us)
Async XLA Ops:
  0.7 7.8 %copy-start = (f32[2,400,400]{2,1,0:T(8,128)S(1)}, f32[2,400,400]{2,1,0:T(8,128)}, u32[]{:S(2)}) copy-start(f32[2,400,400]{2,1,0:T(8,128)} %relations.6) | copy-start | bytes 3840004
  0.7 7.8 %copy-start.1 = (s32[4,1,1]{0,2,1:T(1,128)S(1)}, s32[4,1,1]{0,2,1:T(1,128)}, u32[]{:S(2)}) copy-start(s32[4,1,1]{0,2,1:T(1,128)} %param.12) | copy-start | bytes 52
  0.7 7.8 %copy-start.2 = (f32[1,1,400,768]{3,2,1,0:T(8,128)S(1)}, f32[1,1,400,768]{3,2,1,0:T(8,128)}, u32[]{:S(2)}) copy-start(f32[1,1,400,768]{3,2,1,0:T(8,128)} %param.7) | copy-start | bytes 3686404
  0.7 7.8 %copy-start.3 = (f32[1,1,400,512]{3,2,1,0:T(8,128)S(1)}, f32[1,1,400,512]{3,2,1,0:T(8,128)}, u32[]{:S(2)}) copy-start(f32[1,1,400,512]{3,2,1,0:T(8,128)} %param.9) | copy-start | bytes 2457604
  0.7 7.8 %copy-start.5 = (f32[1,1,768]{2,1,0:T(1,128)S(1)}, f32[1,1,768]{2,1,0:T(1,128)}, u32[]{:S(2)}) copy-start(f32[1,1,768]{2,1,0:T(1,128)} %source_state.1) | copy-start | bytes 9220
  7.8 13.8 %collective-permute-start = (f32[408,512]{1,0:T(8,128)S(1)}, f32[408,512]{1,0:T(8,128)S(1)}, u32[]{:S(2)}, u32[]{:S(2)}) collective-permute-start(f32[408,512]{1,0:T(8,128)S(1)} %get-tuple-element.95), channel_id=1, source_target_pairs={{0,4},{4,8},{8,12},{12,16},{16,20},{20,24},{24,28},{28,0},{1,5},{5... | collective-permute-start | bytes 2506760 | tf_op jit(solution)/shard_map/ppermute | solution.py:27
  8.5 13.1 %copy-start.4 = (s32[4,1,1,768]{3,2,1,0:T(1,128)S(1)}, s32[4,1,1,768]{3,2,1,0:T(1,128)}, u32[]{:S(2)}) copy-start(s32[4,1,1,768]{3,2,1,0:T(1,128)} %partners.7) | copy-start | bytes 36868
  26.4 2.2 %collective-permute-start.1 = (f32[1280,128]{1,0:T(8,128)S(1)}, f32[1280,128]{1,0:T(8,128)S(1)}, u32[]{:S(2)}, u32[]{:S(2)}) collective-permute-start(f32[1280,128]{1,0:T(8,128)S(1)} %slice.71), channel_id=1, source_target_pairs={{0,4},{1,5},{2,6},{3,7},{4,0},{5,1},{6,2},{7,3},{8,12},{9,13},{10,... | collective-permute-start | bytes 1966088 | tf_op jit(solution)/shard_map/ppermute | solution.py:33
  28.7 8.0 %collective-permute-start.2 = (f32[320,128]{1,0:T(8,128)S(1)}, f32[320,128]{1,0:T(8,128)S(1)}, u32[]{:S(2)}, u32[]{:S(2)}) collective-permute-start(f32[320,128]{1,0:T(8,128)S(1)} %get-tuple-element.179), channel_id=1, source_target_pairs={{0,24},{1,25},{2,26},{3,27},{4,28},{5,29},{6,30},{7,31},{8,16},{9,... | collective-permute-start | bytes 491528 | tf_op jit(solution)/shard_map/ppermute | solution.py:33
  31.0 8.3 %collective-permute-start.4 = (f32[320,128]{1,0:T(8,128)S(1)}, f32[320,128]{1,0:T(8,128)S(1)}, u32[]{:S(2)}, u32[]{:S(2)}) collective-permute-start(f32[320,128]{1,0:T(8,128)S(1)} %get-tuple-element.180), channel_id=1, source_target_pairs={{0,16},{1,17},{2,18},{3,19},{4,20},{5,21},{6,22},{7,23},{8,24},{9,... | collective-permute-start | bytes 491528 | tf_op jit(solution)/shard_map/ppermute | solution.py:33
  31.6 8.7 %collective-permute-start.3 = (f32[320,128]{1,0:T(8,128)S(1)}, f32[320,128]{1,0:T(8,128)S(1)}, u32[]{:S(2)}, u32[]{:S(2)}) collective-permute-start(f32[320,128]{1,0:T(8,128)S(1)} %get-tuple-element.181), channel_id=1, source_target_pairs={{0,8},{1,9},{2,10},{3,11},{4,12},{5,13},{6,14},{7,15},{8,0},{9,1},... | collective-permute-start | bytes 491528 | tf_op jit(solution)/shard_map/ppermute | solution.py:33
  40.3 16.9 %collective-permute-start.8 = (f32[408,512]{1,0:T(8,128)S(1)}, f32[408,512]{1,0:T(8,128)S(1)}, u32[]{:S(2)}, u32[]{:S(2)}) collective-permute-start(f32[408,512]{1,0:T(8,128)S(1)} %get-tuple-element.119), channel_id=1, source_target_pairs={{0,4},{4,8},{8,12},{12,16},{16,20},{20,24},{24,28},{28,0},{1,5},{5... | collective-permute-start | bytes 2506760 | tf_op jit(solution)/shard_map/ppermute | solution.py:27
  40.6 5.0 %collective-permute-start.5 = (f32[160,128]{1,0:T(8,128)S(1)}, f32[160,128]{1,0:T(8,128)S(1)}, u32[]{:S(2)}, u32[]{:S(2)}) collective-permute-start(f32[160,128]{1,0:T(8,128)S(1)} %slice.77), channel_id=1, source_target_pairs={{0,1},{1,0},{2,3},{3,2},{4,5},{5,4},{6,7},{7,6},{8,9},{9,8},{10,11... | collective-permute-start | bytes 245768 | tf_op jit(solution)/shard_map/ppermute | solution.py:33
  45.6 7.0 %collective-permute-start.6 = (f32[160,128]{1,0:T(8,128)S(1)}, f32[160,128]{1,0:T(8,128)S(1)}, u32[]{:S(2)}, u32[]{:S(2)}) collective-permute-start(f32[160,128]{1,0:T(8,128)S(1)} %slice_add_fusion.3), channel_id=1, source_target_pairs={{0,2},{1,3},{2,0},{3,1},{4,6},{5,7},{6,4},{7,5},{8,10},{9,11},{10,... | collective-permute-start | bytes 245768 | tf_op jit(solution)/shard_map/ppermute | solution.py:33
  52.6 4.5 %collective-permute-start.7 = (f32[160,128]{1,0:T(8,128)S(1)}, f32[160,128]{1,0:T(8,128)S(1)}, u32[]{:S(2)}, u32[]{:S(2)}) collective-permute-start(f32[160,128]{1,0:T(8,128)S(1)} %add.75), channel_id=1, source_target_pairs={{0,1},{1,0},{2,3},{3,2},{4,5},{5,4},{6,7},{7,6},{8,9},{9,8},{10,11... | collective-permute-start | bytes 245768 | tf_op jit(solution)/shard_map/ppermute | solution.py:33
  57.2 7.8 %collective-permute-start.11 = (f32[320,128]{1,0:T(8,128)S(1)}, f32[320,128]{1,0:T(8,128)S(1)}, u32[]{:S(2)}, u32[]{:S(2)}) collective-permute-start(f32[320,128]{1,0:T(8,128)S(1)} %pad_maximum_fusion.4), channel_id=1, source_target_pairs={{0,24},{1,25},{2,26},{3,27},{4,28},{5,29},{6,30},{7,31},{8,16},{9,... | collective-permute-start | bytes 491528 | tf_op jit(solution)/shard_map/ppermute | solution.py:33
  59.2 6.5 %collective-permute-start.10 = (f32[320,128]{1,0:T(8,128)S(1)}, f32[320,128]{1,0:T(8,128)S(1)}, u32[]{:S(2)}, u32[]{:S(2)}) collective-permute-start(f32[320,128]{1,0:T(8,128)S(1)} %pad_maximum_fusion.4), channel_id=1, source_target_pairs={{0,16},{1,17},{2,18},{3,19},{4,20},{5,21},{6,22},{7,23},{8,24},{9,... | collective-permute-start | bytes 491528 | tf_op jit(solution)/shard_map/ppermute | solution.py:33
  59.8 6.1 %collective-permute-start.9 = (f32[320,128]{1,0:T(8,128)S(1)}, f32[320,128]{1,0:T(8,128)S(1)}, u32[]{:S(2)}, u32[]{:S(2)}) collective-permute-start(f32[320,128]{1,0:T(8,128)S(1)} %pad_maximum_fusion.4), channel_id=1, source_target_pairs={{0,8},{1,9},{2,10},{3,11},{4,12},{5,13},{6,14},{7,15},{8,0},{9,1},... | collective-permute-start | bytes 491528 | tf_op jit(solution)/shard_map/ppermute | solution.py:33
  66.0 2.2 %collective-permute-start.12 = (f32[1280,128]{1,0:T(8,128)S(1)}, f32[1280,128]{1,0:T(8,128)S(1)}, u32[]{:S(2)}, u32[]{:S(2)}) collective-permute-start(f32[1280,128]{1,0:T(8,128)S(1)} %pad_maximum_fusion.2), channel_id=1, source_target_pairs={{0,4},{1,5},{2,6},{3,7},{4,0},{5,1},{6,2},{7,3},{8,12},{9,13},{10,... | collective-permute-start | bytes 1966088 | tf_op jit(solution)/shard_map/ppermute | solution.py:33
  73.8 12.9 %collective-permute-start.13 = (f32[408,512]{1,0:T(8,128)S(1)}, f32[408,512]{1,0:T(8,128)S(1)}, u32[]{:S(2)}, u32[]{:S(2)}) collective-permute-start(f32[408,512]{1,0:T(8,128)S(1)} %get-tuple-element.141), channel_id=1, source_target_pairs={{0,4},{4,8},{8,12},{12,16},{16,20},{20,24},{24,28},{28,0},{1,5},{5... | collective-permute-start | bytes 2506760 | tf_op jit(solution)/shard_map/ppermute | solution.py:27
  91.5 2.2 %collective-permute-start.14 = (f32[1280,128]{1,0:T(8,128)S(1)}, f32[1280,128]{1,0:T(8,128)S(1)}, u32[]{:S(2)}, u32[]{:S(2)}) collective-permute-start(f32[1280,128]{1,0:T(8,128)S(1)} %slice.79), channel_id=1, source_target_pairs={{0,4},{1,5},{2,6},{3,7},{4,0},{5,1},{6,2},{7,3},{8,12},{9,13},{10,... | collective-permute-start | bytes 1966088 | tf_op jit(solution)/shard_map/ppermute | solution.py:33
  93.8 8.1 %collective-permute-start.15 = (f32[320,128]{1,0:T(8,128)S(1)}, f32[320,128]{1,0:T(8,128)S(1)}, u32[]{:S(2)}, u32[]{:S(2)}) collective-permute-start(f32[320,128]{1,0:T(8,128)S(1)} %get-tuple-element.176), channel_id=1, source_target_pairs={{0,24},{1,25},{2,26},{3,27},{4,28},{5,29},{6,30},{7,31},{8,16},{9,... | collective-permute-start | bytes 491528 | tf_op jit(solution)/shard_map/ppermute | solution.py:33
  94.7 9.5 %collective-permute-start.17 = (f32[320,128]{1,0:T(8,128)S(1)}, f32[320,128]{1,0:T(8,128)S(1)}, u32[]{:S(2)}, u32[]{:S(2)}) collective-permute-start(f32[320,128]{1,0:T(8,128)S(1)} %get-tuple-element.177), channel_id=1, source_target_pairs={{0,16},{1,17},{2,18},{3,19},{4,20},{5,21},{6,22},{7,23},{8,24},{9,... | collective-permute-start | bytes 491528 | tf_op jit(solution)/shard_map/ppermute | solution.py:33
  96.1 8.4 %collective-permute-start.16 = (f32[320,128]{1,0:T(8,128)S(1)}, f32[320,128]{1,0:T(8,128)S(1)}, u32[]{:S(2)}, u32[]{:S(2)}) collective-permute-start(f32[320,128]{1,0:T(8,128)S(1)} %get-tuple-element.178), channel_id=1, source_target_pairs={{0,8},{1,9},{2,10},{3,11},{4,12},{5,13},{6,14},{7,15},{8,0},{9,1},... | collective-permute-start | bytes 491528 | tf_op jit(solution)/shard_map/ppermute | solution.py:33
  104.6 17.1 %collective-permute-start.21 = (f32[408,512]{1,0:T(8,128)S(1)}, f32[408,512]{1,0:T(8,128)S(1)}, u32[]{:S(2)}, u32[]{:S(2)}) collective-permute-start(f32[408,512]{1,0:T(8,128)S(1)} %get-tuple-element.165), channel_id=1, source_target_pairs={{0,4},{4,8},{8,12},{12,16},{16,20},{20,24},{24,28},{28,0},{1,5},{5... | collective-permute-start | bytes 2506760 | tf_op jit(solution)/shard_map/ppermute | solution.py:27
  104.7 5.2 %collective-permute-start.18 = (f32[160,128]{1,0:T(8,128)S(1)}, f32[160,128]{1,0:T(8,128)S(1)}, u32[]{:S(2)}, u32[]{:S(2)}) collective-permute-start(f32[160,128]{1,0:T(8,128)S(1)} %slice.85), channel_id=1, source_target_pairs={{0,1},{1,0},{2,3},{3,2},{4,5},{5,4},{6,7},{7,6},{8,9},{9,8},{10,11... | collective-permute-start | bytes 245768 | tf_op jit(solution)/shard_map/ppermute | solution.py:33
  109.9 7.3 %collective-permute-start.19 = (f32[160,128]{1,0:T(8,128)S(1)}, f32[160,128]{1,0:T(8,128)S(1)}, u32[]{:S(2)}, u32[]{:S(2)}) collective-permute-start(f32[160,128]{1,0:T(8,128)S(1)} %slice_add_fusion.2), channel_id=1, source_target_pairs={{0,2},{1,3},{2,0},{3,1},{4,6},{5,7},{6,4},{7,5},{8,10},{9,11},{10,... | collective-permute-start | bytes 245768 | tf_op jit(solution)/shard_map/ppermute | solution.py:33
  117.2 4.5 %collective-permute-start.20 = (f32[160,128]{1,0:T(8,128)S(1)}, f32[160,128]{1,0:T(8,128)S(1)}, u32[]{:S(2)}, u32[]{:S(2)}) collective-permute-start(f32[160,128]{1,0:T(8,128)S(1)} %add.81), channel_id=1, source_target_pairs={{0,1},{1,0},{2,3},{3,2},{4,5},{5,4},{6,7},{7,6},{8,9},{9,8},{10,11... | collective-permute-start | bytes 245768 | tf_op jit(solution)/shard_map/ppermute | solution.py:33
  121.7 7.8 %collective-permute-start.24 = (f32[320,128]{1,0:T(8,128)S(1)}, f32[320,128]{1,0:T(8,128)S(1)}, u32[]{:S(2)}, u32[]{:S(2)}) collective-permute-start(f32[320,128]{1,0:T(8,128)S(1)} %pad_maximum_fusion.5), channel_id=1, source_target_pairs={{0,24},{1,25},{2,26},{3,27},{4,28},{5,29},{6,30},{7,31},{8,16},{9,... | collective-permute-start | bytes 491528 | tf_op jit(solution)/shard_map/ppermute | solution.py:33
  122.3 8.0 %collective-permute-start.23 = (f32[320,128]{1,0:T(8,128)S(1)}, f32[320,128]{1,0:T(8,128)S(1)}, u32[]{:S(2)}, u32[]{:S(2)}) collective-permute-start(f32[320,128]{1,0:T(8,128)S(1)} %pad_maximum_fusion.5), channel_id=1, source_target_pairs={{0,16},{1,17},{2,18},{3,19},{4,20},{5,21},{6,22},{7,23},{8,24},{9,... | collective-permute-start | bytes 491528 | tf_op jit(solution)/shard_map/ppermute | solution.py:33
  124.1 6.4 %collective-permute-start.22 = (f32[320,128]{1,0:T(8,128)S(1)}, f32[320,128]{1,0:T(8,128)S(1)}, u32[]{:S(2)}, u32[]{:S(2)}) collective-permute-start(f32[320,128]{1,0:T(8,128)S(1)} %pad_maximum_fusion.5), channel_id=1, source_target_pairs={{0,8},{1,9},{2,10},{3,11},{4,12},{5,13},{6,14},{7,15},{8,0},{9,1},... | collective-permute-start | bytes 491528 | tf_op jit(solution)/shard_map/ppermute | solution.py:33
  130.5 2.2 %collective-permute-start.25 = (f32[1280,128]{1,0:T(8,128)S(1)}, f32[1280,128]{1,0:T(8,128)S(1)}, u32[]{:S(2)}, u32[]{:S(2)}) collective-permute-start(f32[1280,128]{1,0:T(8,128)S(1)} %pad_maximum_fusion.3), channel_id=1, source_target_pairs={{0,4},{1,5},{2,6},{3,7},{4,0},{5,1},{6,2},{7,3},{8,12},{9,13},{10,... | collective-permute-start | bytes 1966088 | tf_op jit(solution)/shard_map/ppermute | solution.py:33

commit v2 on v1

--- a/solution.py
+++ b/solution.py
@@ -54,8 +54,8 @@
         return None
     blk_bits = [("blk", 1 << i) for i in range(blk.bit_length() - 1)]
     grp_bits = [("grp", 1 << i) for i in range(grp.bit_length() - 1)]
-    stages = [s for s in (blk_bits[:1], blk_bits[1:3], grp_bits[:1]) if s]
-    return (stages, blk_bits[3:] + grp_bits[1:]) if len(stages) > 1 else None
+    stages = [s for s in (blk_bits[:1], blk_bits[1:3], grp_bits[:2]) if s]
+    return (stages, blk_bits[3:] + grp_bits[2:]) if len(stages) > 1 else None
 
 
 def scatter_sum(value, bits):
@@ -69,7 +69,7 @@
 def gather(value, bits):
     arrived = {d: exchange(value, mb, mg) for d, mb, mg in group_masks(bits)}
     arrived[0] = value
-    return jnp.concatenate([arrived[d] for d in range(1 << len(bits))], axis=0)
+    return jnp.concatenate([arrived[d] for d in range(len(arrived))], axis=0)
 
 
 def piece_plan():
@@ -214,7 +214,28 @@
         x_out[:, part], state_out[:, part] = adagrad(source[:, part], state[:, part], gradient)
 
 
-def pack_into(out_ref, parts, kinds):
+class Pieces:
+    def __init__(self, ref, me, count):
+        self.ref, self.me, self.rows = ref, me, ref.shape[0] // count
+
+    def runs(self, start, stop):
+        while start < stop:
+            piece, place = divmod(start, self.rows)
+            end = min(stop, (piece + 1) * self.rows)
+            first = pl.multiple_of((self.me ^ piece) * self.rows + place, 8)
+            yield start, end, pl.ds(first, end - start)
+            start = end
+
+    def put(self, start, value):
+        for first, end, here in self.runs(start, start + value.shape[0]):
+            self.ref[here] = value[first - start : end - start]
+
+    def get(self, start, size):
+        found = [self.ref[here] for _, _, here in self.runs(start, start + size)]
+        return jnp.concatenate(found, axis=0) if len(found) > 1 else found[0]
+
+
+def pack_into(packed, parts, kinds):
     width = parts[0][1].shape[0]
     full, tail = divmod(width, LANES)
     span = tail_span(width, kinds)
@@ -222,8 +243,7 @@
     for kind in range(kinds):
         total = sum(jnp.where(index == kind, part, 0.0) for index, part in parts)
         for block in range(full):
-            start = (kind * full + block) * width
-            out_ref[start : start + width] = total[:, block * LANES : (block + 1) * LANES]
+            packed.put((kind * full + block) * width, total[:, block * LANES : (block + 1) * LANES])
         if tail:
             ends = pad_rows(total[:, full * LANES :], round_up(width, span))
             for place in range(ends.shape[0] // span):
@@ -233,9 +253,9 @@
                 packed_tail = moved if packed_tail is None else packed_tail + moved
     start = kinds * full * width
     if tail:
-        out_ref[start : start + span] = packed_tail
+        packed.put(start, packed_tail)
         start += span
-    out_ref[start:] = jnp.zeros((out_ref.shape[0] - start, LANES), F32)
+    packed.put(start, jnp.zeros((packed.ref.shape[0] - start, LANES), F32))
 
 
 def tail_span(width, kinds):
@@ -247,15 +267,13 @@
     return round_up(kinds * (width // LANES) * width + tail_span(width, kinds), 8 * pieces)
 
 
-def unpack(flat_ref, scaled_out, kind, width, scale):
+def unpack(packed, scaled_out, kind, width, scale):
     kinds, (full, tail) = scaled_out.shape[0], divmod(width, LANES)
     span = tail_span(width, kinds)
     for block in range(full):
-        start = (kind * full + block) * width
-        scaled_out[kind, :, block * LANES : (block + 1) * LANES] = scale * flat_ref[start : start + width]
+        scaled_out[kind, :, block * LANES : (block + 1) * LANES] = scale * packed.get((kind * full + block) * width, width)
     if tail:
-        start = kinds * full * width
-        ends = flat_ref[start : start + span]
+        ends = packed.get(kinds * full * width, span)
         places = -(-width // span)
         for place in range(places):
             rows = min(span, width - place * span)
@@ -264,23 +282,17 @@
             scaled_out[kind, place * span : place * span + rows, full * LANES :] = scale * moved[:rows, :tail]
 
 
-def put_pieces(out_ref, in_ref, me, pieces):
-    rows = in_ref.shape[0] // pieces
-    for piece in range(pieces):
-        out_ref[piece * rows : (piece + 1) * rows] = in_ref[pl.ds(pl.multiple_of((me ^ piece) * rows, 8), rows)]
-
-
 def opening_kernel(me, ids, partners, relations, source, target, target_state, target_out, sgh, sgl, square, xh, xl, qh, ql, scores, matrix, source_in, target_in, state_in, partners_in, ids_in, sems):
     width = source.shape[0]
-    pairs = ((ids, ids_in), (source, source_in), (relations, matrix), (target, target_in), (target_state, state_in), (partners.at[0], partners_in))
+    pairs = ((ids, ids_in), (relations, matrix), (source, source_in), (target, target_in), (target_state, state_in), (partners.at[0], partners_in))
     loads = [pltpu.make_async_copy(here, there, sems.at[place]) for place, (here, there) in enumerate(pairs)]
     for load in loads:
         load.start()
+    loads[0].wait()
     loads[1].wait()
+    square_of(square, matrix[ids_in[0]])
+    loads[2].wait()
     put_split((xh, xl), source_in[...])
-    loads[0].wait()
-    loads[2].wait()
-    square_of(square, matrix[ids_in[0]])
     queries_into((qh, ql), square, (xh, xl), width)
     for load in loads[3:]:
         load.wait()
@@ -293,16 +305,15 @@
     yh[...], yl[...] = split(pad_rows(target[:width], yh.shape[1]).T)
 
 
-def renew(flat, relations, scaled, renewed, kind, scale):
-    unpack(flat, scaled, kind, relations.shape[1], scale)
+def renew(packed, relations, scaled, renewed, kind, scale):
+    unpack(packed, scaled, kind, relations.shape[1], scale)
     renewed[kind] = relations[kind] - operator_rate * scaled[kind]
 
 
-def first_kernel(ids, me, partners, packed, relations, xh, xl, target, yh, yl, relations_out, scaled, target_out, sgh, sgl, flat, square, qh, ql, scores, *, bucket, pieces, scale):
+def first_kernel(ids, me, partners, packed, relations, xh, xl, target, yh, yl, relations_out, scaled, target_out, sgh, sgl, square, qh, ql, scores, *, bucket, pieces, scale):
     width = relations.shape[1]
-    put_pieces(flat, packed, me[0], pieces)
     for kind in range(relations.shape[0]):
-        renew(flat, relations, scaled, relations_out, kind, scale)
+        renew(Pieces(packed, me[0], pieces), relations, scaled, relations_out, kind, scale)
     square_of(square, relations_out[ids[bucket]])
     queries_into((qh, ql), square, (xh, xl), width)
     score_grad_into((sgh, sgl), scores, (qh, ql), both((yh, yl)), partners[bucket, 0])
@@ -310,11 +321,10 @@
 
 
 def closing_kernel(me, packed, relations, *refs, pieces, scale, place):
-    grads_out, relations_out, flat, scaled, renewed, sems = refs[1 if place else 0 :]
-    put_pieces(flat, packed, me[0], pieces)
+    grads_out, relations_out, scaled, renewed, sems = refs[1 if place else 0 :]
     stores = []
     for kind in range(relations.shape[0]):
-        renew(flat, relations, scaled, renewed, kind, scale)
+        renew(Pieces(packed, me[0], pieces), relations, scaled, renewed, kind, scale)
         for here, there in ((scaled, grads_out.at[place]), (renewed, relations_out)):
             stores.append(pltpu.make_async_copy(here.at[kind], there.at[kind], sems.at[len(stores)]))
             stores[-1].start()
@@ -343,14 +353,13 @@
         store.wait()
 
 
-def third_kernel(ids, me, partners, xh, xl, target, qh, ql, grad_before, packed, sgh, sgl, gh, gl, flat, scores, *, bucket, kinds, pieces):
+def third_kernel(ids, me, partners, xh, xl, target, qh, ql, grad_before, packed, sgh, sgl, gh, gl, scores, *, bucket, kinds, pieces):
     width = grad_before.shape[0]
     body = target[:width]
     score_grad_into((sgh, sgl), scores, (qh, ql), split(pad_rows(body, qh.shape[0]).T), partners[bucket, 0])
     query_grad_into((gh, gl), (sgh, sgl), body)
     grad = operator_grad(both((xh, xl), width), (gh, gl))
-    pack_into(flat, ((ids[bucket - 1], grad_before[...]), (ids[bucket], grad)), kinds)
-    put_pieces(packed, flat, me[0], pieces)
+    pack_into(Pieces(packed, me[0], pieces), ((ids[bucket - 1], grad_before[...]), (ids[bucket], grad)), kinds)
 
 
 def fourth_kernel(ids, relations, source, source_state, target, qh, ql, sgh, sgl, gh, gl, target_out, source_out, state_out, *refs, bucket):
@@ -407,7 +416,7 @@
     source_outs = [((width, columns), F32), (source_state.shape, F32)]
     product = 6 * width * width * columns
     updates = buckets // 2
-    rel_out, flat, y_pair = (relations.shape, F32), ((rows, LANES), F32), [((block, wide), BF16)] * 2
+    rel_out, packed_out, y_pair = (relations.shape, F32), ((rows, LANES), F32), [((block, wide), BF16)] * 2
     grads, grads_out = None, ((updates, *relations.shape), F32)
     for update in range(updates):
         bucket, last = 2 * update, update == updates - 1
@@ -423,7 +432,7 @@
             relations, scaled, after, sgh, sgl = call(
                 functools.partial(first_kernel, bucket=bucket, pieces=pieces, scale=scale), "first",
                 (ids, me, positives, total, relations, xh, xl, target, yh, yl), [SMEM] * 2 + [VMEM] * 8,
-                [rel_out, rel_out] + moving + sg_pair, [flat] + square + q_pair + scores, 3 * product)
+                [rel_out, rel_out] + moving + sg_pair, square + q_pair + scores, 3 * product)
         arriving = from_behind(after, "blk", 1)
         args, outs = (ids, relations, source, state, target, sgh, sgl), source_outs + [((width, wide), F32)] + q_pair + q_pair
         if update == 0:
@@ -441,7 +450,7 @@
         packed, sgh, sgl, gh, gl = call(
             functools.partial(third_kernel, bucket=bucket + 1, kinds=kinds, pieces=pieces), "third",
             (ids, me, positives, xh, xl, target, qh, ql, grad), [SMEM] * 2 + [VMEM] * 7,
-            [flat] + sg_pair + q_pair, [flat] + scores, 3 * product)
+            [packed_out] + sg_pair + q_pair, scores, 3 * product)
         total, target, source, state, *prepared = sum_everywhere(
             packed,
             lambda *args: call(
@@ -456,7 +465,7 @@
     grads, relations = call(
         functools.partial(closing_kernel, pieces=pieces, scale=scale, place=updates - 1), "closing",
         (me, total, relations, *before), [SMEM, VMEM, VMEM] + [HBM] * len(before),
-        [grads_out, rel_out], [flat, rel_out, rel_out, pltpu.SemaphoreType.DMA((2 * kinds,))],
+        [grads_out, rel_out], [rel_out, rel_out, pltpu.SemaphoreType.DMA((2 * kinds,))],
         product, [HBM, HBM], {3: 0} if before else None)
     return (
         source[None, None],

time: 135 us -> 134 us (level)
  waiting for transfers between devices: 63.2 us -> 54.1 us
  starting transfers between devices: 25.8 us -> 33.8 us
    ppermute x22 -> x28, waiting for transfers between devices: 48.1 us -> 39 us  [exchange(): return lax.ppermute(value, AXES, pairs)]
    ppermute x22 -> x28, starting transfers between devices: 24.5 us -> 32.6 us  [exchange(): return lax.ppermute(value, AXES, pairs)]
  transfers between devices with their start and end apart: 26 -> 32, of which waited for: 24 -> 24; matrix products, arithmetic and copies ran while one was open for 1% -> 1% of each run, Pallas kernels for 14% -> 14%
where the time goes in v2:
time: 134 us
  waiting for transfers between devices  54.1 us (40%)
  Pallas kernels  42.1 us (31%)
  starting transfers between devices  33.8 us (25%)
  local copies, waits for them, and re-layouts  1.73 us (1%)
    pallas_call x10, Pallas kernels, call(): pl.pallas_call(kernel, in_specs=args_in, out_specs=outs_in or [VMEM] * le...  42.1 us
    ppermute x28, waiting for transfers between devices, exchange(): return lax.ppermute(value, AXES, pairs)  39 us
    ppermute x28, starting transfers between devices, exchange(): return lax.ppermute(value, AXES, pairs)  32.6 us
    ppermute x4, waiting for transfers between devices, from_behind(): return lax.ppermute(value, axis, pairs)  15.1 us
  transfers between devices with their start and end apart: 32, of which 24 were waited for; matrix products, arithmetic and copies ran while one was open for 1% of the time, Pallas kernels for 14%

profile of v2, /device:TPU:0, one launch (start us, length us, event | category | flops | bytes accessed | tf_op | source)
XLA Modules:
  0.0 133.5 jit_solution(7419708670250114612)
XLA Ops:
  0.8 7.0 %opening.1 = (f32[408,512]{1,0:T(8,128)S(1)}, bf16[512,768]{1,0:T(8,128)(2,1)S(1)}, bf16[512,768]{1,0:T(8,128)(2,1)S(1)}) custom-call(s32[1]{0:T(128)} %bitcast.1.me, s32[4]{0:T(128)} %bitcast.9, s32[4,1,1,768]{3,2,1,0:T(1,128)} %partners.7, f32[2,400,400]{2,1,0:T(8,128)} %relations.6, f32[400,768]{1,0:T(8,128)} %bitcast.17, f32[400,512]{1,0:T(8,128)} %bitcast.19, ...), custom_call_target="tpu_custom_call" | custom-call | flops 2211840000 | tf_op jit(solution)/shard_map/opening/pallas_call | solution.py:385
  8.5 5.2 %second.2 = (f32[400,768]{1,0:T(8,128)S(1)}, f32[1,1,768]{2,1,0:T(1,128)S(1)}, f32[400,512]{1,0:T(8,128)S(1)}, bf16[512,768]{1,0:T(8,128)(2,1)S(1)}, bf16[512,76...) custom-call(s32[4]{0:T(128)S(1)} %bitcast.10, f32[2,400,400]{2,1,0:T(8,128)S(1)} %copy-done, ...), custom_call_target="tpu_custom_call" | custom-call | flops 2949120000 | tf_op jit(solution)/shard_map/second/pallas_call | solution.py:385
  13.7 7.8 %collective-permute-done.target = f32[408,512]{1,0:T(8,128)S(1)} collective-permute-done((f32[408,512]{1,0:T(8,128)S(1)}, f32[408,512]{1,0:T(8,128)S(1)}, u32[]{:S(2)}, u32[]{:S(2)}) %collective-permute-start) | collective-permute-done | bytes 835616 | tf_op jit(solution)/shard_map/ppermute | solution.py:27
  21.5 4.7 %third.2 = (f32[2560,128]{1,0:T(8,128)S(1)}, bf16[512,768]{1,0:T(8,128)(2,1)S(1)}, bf16[512,768]{1,0:T(8,128)(2,1)S(1)}, bf16[512,768]{1,0:T(8,128)(2,1)S(1)}, bf16[512,768]{1,0:T(8,128)(2,1)S(1)}) custom-call(s32[4]{0:T(128)S(1)} %bitcast.11, s32[1]{0:T(128)} %bitcast.1.me, s32[4,1,1,768]{3,2,1,0:T(1,128)S(1)} %copy-done.4, ...), custom_call_target="tpu_custom_call" | custom-call | flops 2211840000 | tf_op jit(solution)/shard_map/third/pallas_call | solution.py:385
  26.4 2.1 %collective-permute-done.1 = f32[1280,128]{1,0:T(8,128)S(1)} collective-permute-done((f32[1280,128]{1,0:T(8,128)S(1)}, f32[1280,128]{1,0:T(8,128)S(1)}, u32[]{:S(2)}, u32[]{:S(2)}) %collective-permute-start.1) | collective-permute-done | bytes 655392 | tf_op jit(solution)/shard_map/ppermute | solution.py:33
  28.6 2.4 %collective-permute-start.2 = (f32[320,128]{1,0:T(8,128)S(1)}, f32[320,128]{1,0:T(8,128)S(1)}, u32[]{:S(2)}, u32[]{:S(2)}) collective-permute-start(f32[320,128]{1,0:T(8,128)S(1)} %get-tuple-element.179), channel_id=1, source_target_pairs={{0,24},{1,25},{2,26},{3,27},{4,28},{5,29},{6,30},{7,31},{8,16},{9,... | collective-permute-start | bytes 491528 | tf_op jit(solution)/shard_map/ppermute | solution.py:33
  32.4 3.4 %fourth.2 = (f32[408,512]{1,0:T(8,128)S(1)}, f32[400,768]{1,0:T(8,128)S(1)}, f32[1,1,768]{2,1,0:T(1,128)S(1)}, bf16[512,768]{1,0:T(8,128)(2,1)S(1)}, bf16[512,768]{1,0:T(8,128)(2,1)S(1)}) custom-call(s32[4]{0:T(128)S(1)} %bitcast.12, f32[2,400,400]{2,1,0:T(8,128)S(1)} %copy-done, f32[400,768]{1,0:T(8,128)S(1)} %get-tuple-element.108.source, ...), custom_call_target="tpu_custom_call" | custom-call | flops 1474560000 | tf_op jit(solution)/shard_map/fourth/pallas_call | solution.py:385
  36.6 2.7 %collective-permute-done.4 = f32[320,128]{1,0:T(8,128)S(1)} collective-permute-done((f32[320,128]{1,0:T(8,128)S(1)}, f32[320,128]{1,0:T(8,128)S(1)}, u32[]{:S(2)}, u32[]{:S(2)}) %collective-permute-start.4) | collective-permute-done | bytes 163872 | tf_op jit(solution)/shard_map/ppermute | solution.py:33
  40.5 3.7 %collective-permute-start.5 = (f32[80,128]{1,0:T(8,128)S(1)}, f32[80,128]{1,0:T(8,128)S(1)}, u32[]{:S(2)}, u32[]{:S(2)}) collective-permute-start(f32[80,128]{1,0:T(8,128)S(1)} %get-tuple-element.185), channel_id=1, source_target_pairs={{0,3},{1,2},{2,1},{3,0},{4,7},{5,6},{6,5},{7,4},{8,11},{9,10},{10,... | collective-permute-start | bytes 122888 | tf_op jit(solution)/shard_map/ppermute | solution.py:33
  44.9 1.7 %collective-permute-done.5 = f32[80,128]{1,0:T(8,128)S(1)} collective-permute-done((f32[80,128]{1,0:T(8,128)S(1)}, f32[80,128]{1,0:T(8,128)S(1)}, u32[]{:S(2)}, u32[]{:S(2)}) %collective-permute-start.5) | collective-permute-done | bytes 40992 | tf_op jit(solution)/shard_map/ppermute | solution.py:33
  46.6 2.5 %collective-permute-done.7 = f32[80,128]{1,0:T(8,128)S(1)} collective-permute-done((f32[80,128]{1,0:T(8,128)S(1)}, f32[80,128]{1,0:T(8,128)S(1)}, u32[]{:S(2)}, u32[]{:S(2)}) %collective-permute-start.7) | collective-permute-done | bytes 40992 | tf_op jit(solution)/shard_map/ppermute | solution.py:33
  49.1 2.0 %collective-permute-start.10 = (f32[80,128]{1,0:T(8,128)S(1)}, f32[80,128]{1,0:T(8,128)S(1)}, u32[]{:S(2)}, u32[]{:S(2)}) collective-permute-start(f32[80,128]{1,0:T(8,128)S(1)} %add_add_fusion.3), channel_id=1, source_target_pairs={{0,3},{1,2},{2,1},{3,0},{4,7},{5,6},{6,5},{7,4},{8,11},{9,10},{10,... | collective-permute-start | bytes 122888 | tf_op jit(solution)/shard_map/ppermute | solution.py:33
  51.6 1.9 %collective-permute-start.8 = (f32[80,128]{1,0:T(8,128)S(1)}, f32[80,128]{1,0:T(8,128)S(1)}, u32[]{:S(2)}, u32[]{:S(2)}) collective-permute-start(f32[80,128]{1,0:T(8,128)S(1)} %add_add_fusion.3), channel_id=1, source_target_pairs={{0,1},{1,0},{2,3},{3,2},{4,5},{5,4},{6,7},{7,6},{8,9},{9,8},{10,11... | collective-permute-start | bytes 122888 | tf_op jit(solution)/shard_map/ppermute | solution.py:33
  56.4 1.9 %collective-permute-start.14 = (f32[320,128]{1,0:T(8,128)S(1)}, f32[320,128]{1,0:T(8,128)S(1)}, u32[]{:S(2)}, u32[]{:S(2)}) collective-permute-start(f32[320,128]{1,0:T(8,128)S(1)} %pad_maximum_fusion.4), channel_id=1, source_target_pairs={{0,24},{1,25},{2,26},{3,27},{4,28},{5,29},{6,30},{7,31},{8,16},{9,... | collective-permute-start | bytes 491528 | tf_op jit(solution)/shard_map/ppermute | solution.py:33
  60.3 3.9 %collective-permute-done.14 = f32[320,128]{1,0:T(8,128)S(1)} collective-permute-done((f32[320,128]{1,0:T(8,128)S(1)}, f32[320,128]{1,0:T(8,128)S(1)}, u32[]{:S(2)}, u32[]{:S(2)}) %collective-permute-start.14) | collective-permute-done | bytes 163872 | tf_op jit(solution)/shard_map/ppermute | solution.py:33
  64.2 1.5 %collective-permute-done.13 = f32[320,128]{1,0:T(8,128)S(1)} collective-permute-done((f32[320,128]{1,0:T(8,128)S(1)}, f32[320,128]{1,0:T(8,128)S(1)}, u32[]{:S(2)}, u32[]{:S(2)}) %collective-permute-start.13) | collective-permute-done | bytes 163872 | tf_op jit(solution)/shard_map/ppermute | solution.py:33
  66.0 2.1 %collective-permute-done.15 = f32[1280,128]{1,0:T(8,128)S(1)} collective-permute-done((f32[1280,128]{1,0:T(8,128)S(1)}, f32[1280,128]{1,0:T(8,128)S(1)}, u32[]{:S(2)}, u32[]{:S(2)}) %collective-permute-start.15) | collective-permute-done | bytes 655392 | tf_op jit(solution)/shard_map/ppermute | solution.py:33
  68.2 5.4 %first.1 = (f32[2,400,400]{2,1,0:T(8,128)S(1)}, f32[2,400,400]{2,1,0:T(8,128)S(1)}, f32[408,512]{1,0:T(8,128)S(1)}, bf16[512,768]{1,0:T(8,128)(2,1)S(1)}, bf16[512,768]{1,0:T(8,128)(2,1)S(1)}) custom-call(s32[4]{0:T(128)S(1)} %bitcast.13, s32[1]{0:T(128)} %bitcast.1.me, s32[4,1,1,768]{3,2,1,0:T(1,128)S(1)} %copy-done.4, ...), custom_call_target="tpu_custom_call" | custom-call | flops 2211840000 | tf_op jit(solution)/shard_map/first/pallas_call | solution.py:385
  73.8 5.4 %second.3 = (f32[400,768]{1,0:T(8,128)S(1)}, f32[1,1,768]{2,1,0:T(1,128)S(1)}, f32[400,512]{1,0:T(8,128)S(1)}, bf16[512,768]{1,0:T(8,128)(2,1)S(1)}, bf16[512,76...) custom-call(s32[4]{0:T(128)S(1)} %bitcast.14, ...), custom_call_target="tpu_custom_call" | custom-call | flops 2949120000 | tf_op jit(solution)/shard_map/second/pallas_call | solution.py:385
  79.2 7.3 %collective-permute-done.16.target = f32[408,512]{1,0:T(8,128)S(1)} collective-permute-done((f32[408,512]{1,0:T(8,128)S(1)}, f32[408,512]{1,0:T(8,128)S(1)}, u32[]{:S(2)}, u32[]{:S(2)}) %collective-permute-start.16) | collective-permute-done | bytes 835616 | tf_op jit(solution)/shard_map/ppermute | solution.py:27
  86.5 4.7 %third.3 = (f32[2560,128]{1,0:T(8,128)S(1)}, bf16[512,768]{1,0:T(8,128)(2,1)S(1)}, bf16[512,768]{1,0:T(8,128)(2,1)S(1)}, bf16[512,768]{1,0:T(8,128)(2,1)S(1)}, bf16[512,768]{1,0:T(8,128)(2,1)S(1)}) custom-call(s32[4]{0:T(128)S(1)} %bitcast.15, s32[1]{0:T(128)} %bitcast.1.me, s32[4,1,1,768]{3,2,1,0:T(1,128)S(1)} %copy-done.4, ...), custom_call_target="tpu_custom_call" | custom-call | flops 2211840000 | tf_op jit(solution)/shard_map/third/pallas_call | solution.py:385
  91.3 2.1 %collective-permute-done.17 = f32[1280,128]{1,0:T(8,128)S(1)} collective-permute-done((f32[1280,128]{1,0:T(8,128)S(1)}, f32[1280,128]{1,0:T(8,128)S(1)}, u32[]{:S(2)}, u32[]{:S(2)}) %collective-permute-start.17) | collective-permute-done | bytes 655392 | tf_op jit(solution)/shard_map/ppermute | solution.py:33
  97.1 4.1 %fourth.3 = (f32[408,512]{1,0:T(8,128)S(1)}, f32[400,768]{1,0:T(8,128)}, f32[1,1,768]{2,1,0:T(1,128)}) custom-call(s32[4]{0:T(128)S(1)} %bitcast.16, f32[2,400,400]{2,1,0:T(8,128)S(1)} %get-tuple-element.153.relations, f32[400,768]{1,0:T(8,128)S(1)} %get-tuple-element.154.source, f32[1,1,768]{2,1,0:T(1,128)S(1)} %get-tuple-element.155.source_state, ...), custom_call_target="tpu_custom_call" | custom-call | flops 1474560000 | tf_op jit(solution)/shard_map/fourth/pallas_call | solution.py:385
  101.6 2.6 %collective-permute-done.20 = f32[320,128]{1,0:T(8,128)S(1)} collective-permute-done((f32[320,128]{1,0:T(8,128)S(1)}, f32[320,128]{1,0:T(8,128)S(1)}, u32[]{:S(2)}, u32[]{:S(2)}) %collective-permute-start.20) | collective-permute-done | bytes 163872 | tf_op jit(solution)/shard_map/ppermute | solution.py:33
  104.4 3.1 %collective-permute-start.21 = (f32[80,128]{1,0:T(8,128)S(1)}, f32[80,128]{1,0:T(8,128)S(1)}, u32[]{:S(2)}, u32[]{:S(2)}) collective-permute-start(f32[80,128]{1,0:T(8,128)S(1)} %get-tuple-element.182), channel_id=1, source_target_pairs={{0,3},{1,2},{2,1},{3,0},{4,7},{5,6},{6,5},{7,4},{8,11},{9,10},{10,... | collective-permute-start | bytes 122888 | tf_op jit(solution)/shard_map/ppermute | solution.py:33
  108.8 1.9 %collective-permute-done.21 = f32[80,128]{1,0:T(8,128)S(1)} collective-permute-done((f32[80,128]{1,0:T(8,128)S(1)}, f32[80,128]{1,0:T(8,128)S(1)}, u32[]{:S(2)}, u32[]{:S(2)}) %collective-permute-start.21) | collective-permute-done | bytes 40992 | tf_op jit(solution)/shard_map/ppermute | solution.py:33
  110.7 1.7 %collective-permute-done.23 = f32[80,128]{1,0:T(8,128)S(1)} collective-permute-done((f32[80,128]{1,0:T(8,128)S(1)}, f32[80,128]{1,0:T(8,128)S(1)}, u32[]{:S(2)}, u32[]{:S(2)}) %collective-permute-start.23) | collective-permute-done | bytes 40992 | tf_op jit(solution)/shard_map/ppermute | solution.py:33
  112.4 2.5 %collective-permute-start.26 = (f32[80,128]{1,0:T(8,128)S(1)}, f32[80,128]{1,0:T(8,128)S(1)}, u32[]{:S(2)}, u32[]{:S(2)}) collective-permute-start(f32[80,128]{1,0:T(8,128)S(1)} %add_add_fusion.2), channel_id=1, source_target_pairs={{0,3},{1,2},{2,1},{3,0},{4,7},{5,6},{6,5},{7,4},{8,11},{9,10},{10,... | collective-permute-start | bytes 122888 | tf_op jit(solution)/shard_map/ppermute | solution.py:33
  114.9 1.9 %collective-permute-start.24 = (f32[80,128]{1,0:T(8,128)S(1)}, f32[80,128]{1,0:T(8,128)S(1)}, u32[]{:S(2)}, u32[]{:S(2)}) collective-permute-start(f32[80,128]{1,0:T(8,128)S(1)} %add_add_fusion.2), channel_id=1, source_target_pairs={{0,1},{1,0},{2,3},{3,2},{4,5},{5,4},{6,7},{7,6},{8,9},{9,8},{10,11... | collective-permute-start | bytes 122888 | tf_op jit(solution)/shard_map/ppermute | solution.py:33
  118.3 1.7 %collective-permute-done.25 = f32[80,128]{1,0:T(8,128)S(1)} collective-permute-done((f32[80,128]{1,0:T(8,128)S(1)}, f32[80,128]{1,0:T(8,128)S(1)}, u32[]{:S(2)}, u32[]{:S(2)}) %collective-permute-start.25) | collective-permute-done | bytes 40992 | tf_op jit(solution)/shard_map/ppermute | solution.py:33
  123.5 4.3 %collective-permute-done.30 = f32[320,128]{1,0:T(8,128)S(1)} collective-permute-done((f32[320,128]{1,0:T(8,128)S(1)}, f32[320,128]{1,0:T(8,128)S(1)}, u32[]{:S(2)}, u32[]{:S(2)}) %collective-permute-start.30) | collective-permute-done | bytes 163872 | tf_op jit(solution)/shard_map/ppermute | solution.py:33
  131.4 1.9 %closing.1 = (f32[2,2,400,400]{3,2,1,0:T(8,128)}, f32[2,400,400]{2,1,0:T(8,128)}) custom-call(s32[1]{0:T(128)} %bitcast.1.me, f32[2560,128]{1,0:T(8,128)S(1)} %pad_maximum_fusion.1.packed, f32[2,400,400]{2,1,0:T(8,128)S(1)} %get-tuple-element.153.relations, f32[2,2,400,400]{3,2,1,0:T(8,128)} %get-tuple-element.173.refs_0_), custom_call_target="tpu_custom_call", output_to_operand_aliasing={{0}: (3, {})} | custom-call | flops 737280000 | tf_op jit(solution)/shard_map/closing/pallas_call | solution.py:385
  (74 shorter events, 25.5 us)
Async XLA Ops:
  7.7 13.8 %collective-permute-start = (f32[408,512]{1,0:T(8,128)S(1)}, f32[408,512]{1,0:T(8,128)S(1)}, u32[]{:S(2)}, u32[]{:S(2)}) collective-permute-start(f32[408,512]{1,0:T(8,128)S(1)} %get-tuple-element.95), channel_id=1, source_target_pairs={{0,4},{4,8},{8,12},{12,16},{16,20},{20,24},{24,28},{28,0},{1,5},{5... | collective-permute-start | bytes 2506760 | tf_op jit(solution)/shard_map/ppermute | solution.py:27
  26.3 2.2 %collective-permute-start.1 = (f32[1280,128]{1,0:T(8,128)S(1)}, f32[1280,128]{1,0:T(8,128)S(1)}, u32[]{:S(2)}, u32[]{:S(2)}) collective-permute-start(f32[1280,128]{1,0:T(8,128)S(1)} %slice.87), channel_id=1, source_target_pairs={{0,4},{1,5},{2,6},{3,7},{4,0},{5,1},{6,2},{7,3},{8,12},{9,13},{10,... | collective-permute-start | bytes 1966088 | tf_op jit(solution)/shard_map/ppermute | solution.py:33
  28.6 8.0 %collective-permute-start.2 = (f32[320,128]{1,0:T(8,128)S(1)}, f32[320,128]{1,0:T(8,128)S(1)}, u32[]{:S(2)}, u32[]{:S(2)}) collective-permute-start(f32[320,128]{1,0:T(8,128)S(1)} %get-tuple-element.179), channel_id=1, source_target_pairs={{0,24},{1,25},{2,26},{3,27},{4,28},{5,29},{6,30},{7,31},{8,16},{9,... | collective-permute-start | bytes 491528 | tf_op jit(solution)/shard_map/ppermute | solution.py:33
  30.9 8.4 %collective-permute-start.4 = (f32[320,128]{1,0:T(8,128)S(1)}, f32[320,128]{1,0:T(8,128)S(1)}, u32[]{:S(2)}, u32[]{:S(2)}) collective-permute-start(f32[320,128]{1,0:T(8,128)S(1)} %get-tuple-element.180), channel_id=1, source_target_pairs={{0,16},{1,17},{2,18},{3,19},{4,20},{5,21},{6,22},{7,23},{8,24},{9,... | collective-permute-start | bytes 491528 | tf_op jit(solution)/shard_map/ppermute | solution.py:33
  31.4 8.7 %collective-permute-start.3 = (f32[320,128]{1,0:T(8,128)S(1)}, f32[320,128]{1,0:T(8,128)S(1)}, u32[]{:S(2)}, u32[]{:S(2)}) collective-permute-start(f32[320,128]{1,0:T(8,128)S(1)} %get-tuple-element.181), channel_id=1, source_target_pairs={{0,8},{1,9},{2,10},{3,11},{4,12},{5,13},{6,14},{7,15},{8,0},{9,1},... | collective-permute-start | bytes 491528 | tf_op jit(solution)/shard_map/ppermute | solution.py:33
  40.2 16.2 %collective-permute-start.11 = (f32[408,512]{1,0:T(8,128)S(1)}, f32[408,512]{1,0:T(8,128)S(1)}, u32[]{:S(2)}, u32[]{:S(2)}) collective-permute-start(f32[408,512]{1,0:T(8,128)S(1)} %get-tuple-element.119), channel_id=1, source_target_pairs={{0,4},{4,8},{8,12},{12,16},{16,20},{20,24},{24,28},{28,0},{1,5},{5... | collective-permute-start | bytes 2506760 | tf_op jit(solution)/shard_map/ppermute | solution.py:27
  40.5 6.1 %collective-permute-start.5 = (f32[80,128]{1,0:T(8,128)S(1)}, f32[80,128]{1,0:T(8,128)S(1)}, u32[]{:S(2)}, u32[]{:S(2)}) collective-permute-start(f32[80,128]{1,0:T(8,128)S(1)} %get-tuple-element.185), channel_id=1, source_target_pairs={{0,3},{1,2},{2,1},{3,0},{4,7},{5,6},{6,5},{7,4},{8,11},{9,10},{10,... | collective-permute-start | bytes 122888 | tf_op jit(solution)/shard_map/ppermute | solution.py:33
  44.2 4.9 %collective-permute-start.7 = (f32[80,128]{1,0:T(8,128)S(1)}, f32[80,128]{1,0:T(8,128)S(1)}, u32[]{:S(2)}, u32[]{:S(2)}) collective-permute-start(f32[80,128]{1,0:T(8,128)S(1)} %get-tuple-element.186), channel_id=1, source_target_pairs={{0,2},{1,3},{2,0},{3,1},{4,6},{5,7},{6,4},{7,5},{8,10},{9,11},{10,... | collective-permute-start | bytes 122888 | tf_op jit(solution)/shard_map/ppermute | solution.py:33
  44.2 4.9 %collective-permute-start.6 = (f32[80,128]{1,0:T(8,128)S(1)}, f32[80,128]{1,0:T(8,128)S(1)}, u32[]{:S(2)}, u32[]{:S(2)}) collective-permute-start(f32[80,128]{1,0:T(8,128)S(1)} %get-tuple-element.187), channel_id=1, source_target_pairs={{0,1},{1,0},{2,3},{3,2},{4,5},{5,4},{6,7},{7,6},{8,9},{9,8},{10,11... | collective-permute-start | bytes 122888 | tf_op jit(solution)/shard_map/ppermute | solution.py:33
  49.1 5.9 %collective-permute-start.10 = (f32[80,128]{1,0:T(8,128)S(1)}, f32[80,128]{1,0:T(8,128)S(1)}, u32[]{:S(2)}, u32[]{:S(2)}) collective-permute-start(f32[80,128]{1,0:T(8,128)S(1)} %add_add_fusion.3), channel_id=1, source_target_pairs={{0,3},{1,2},{2,1},{3,0},{4,7},{5,6},{6,5},{7,4},{8,11},{9,10},{10,... | collective-permute-start | bytes 122888 | tf_op jit(solution)/shard_map/ppermute | solution.py:33
  51.1 5.3 %collective-permute-start.9 = (f32[80,128]{1,0:T(8,128)S(1)}, f32[80,128]{1,0:T(8,128)S(1)}, u32[]{:S(2)}, u32[]{:S(2)}) collective-permute-start(f32[80,128]{1,0:T(8,128)S(1)} %add_add_fusion.3), channel_id=1, source_target_pairs={{0,2},{1,3},{2,0},{3,1},{4,6},{5,7},{6,4},{7,5},{8,10},{9,11},{10,... | collective-permute-start | bytes 122888 | tf_op jit(solution)/shard_map/ppermute | solution.py:33
  51.6 4.8 %collective-permute-start.8 = (f32[80,128]{1,0:T(8,128)S(1)}, f32[80,128]{1,0:T(8,128)S(1)}, u32[]{:S(2)}, u32[]{:S(2)}) collective-permute-start(f32[80,128]{1,0:T(8,128)S(1)} %add_add_fusion.3), channel_id=1, source_target_pairs={{0,1},{1,0},{2,3},{3,2},{4,5},{5,4},{6,7},{7,6},{8,9},{9,8},{10,11... | collective-permute-start | bytes 122888 | tf_op jit(solution)/shard_map/ppermute | solution.py:33
  56.4 7.8 %collective-permute-start.14 = (f32[320,128]{1,0:T(8,128)S(1)}, f32[320,128]{1,0:T(8,128)S(1)}, u32[]{:S(2)}, u32[]{:S(2)}) collective-permute-start(f32[320,128]{1,0:T(8,128)S(1)} %pad_maximum_fusion.4), channel_id=1, source_target_pairs={{0,24},{1,25},{2,26},{3,27},{4,28},{5,29},{6,30},{7,31},{8,16},{9,... | collective-permute-start | bytes 491528 | tf_op jit(solution)/shard_map/ppermute | solution.py:33
  58.4 7.4 %collective-permute-start.13 = (f32[320,128]{1,0:T(8,128)S(1)}, f32[320,128]{1,0:T(8,128)S(1)}, u32[]{:S(2)}, u32[]{:S(2)}) collective-permute-start(f32[320,128]{1,0:T(8,128)S(1)} %pad_maximum_fusion.4), channel_id=1, source_target_pairs={{0,16},{1,17},{2,18},{3,19},{4,20},{5,21},{6,22},{7,23},{8,24},{9,... | collective-permute-start | bytes 491528 | tf_op jit(solution)/shard_map/ppermute | solution.py:33
  58.9 7.0 %collective-permute-start.12 = (f32[320,128]{1,0:T(8,128)S(1)}, f32[320,128]{1,0:T(8,128)S(1)}, u32[]{:S(2)}, u32[]{:S(2)}) collective-permute-start(f32[320,128]{1,0:T(8,128)S(1)} %pad_maximum_fusion.4), channel_id=1, source_target_pairs={{0,8},{1,9},{2,10},{3,11},{4,12},{5,13},{6,14},{7,15},{8,0},{9,1},... | collective-permute-start | bytes 491528 | tf_op jit(solution)/shard_map/ppermute | solution.py:33
  65.9 2.2 %collective-permute-start.15 = (f32[1280,128]{1,0:T(8,128)S(1)}, f32[1280,128]{1,0:T(8,128)S(1)}, u32[]{:S(2)}, u32[]{:S(2)}) collective-permute-start(f32[1280,128]{1,0:T(8,128)S(1)} %pad_maximum_fusion.2), channel_id=1, source_target_pairs={{0,4},{1,5},{2,6},{3,7},{4,0},{5,1},{6,2},{7,3},{8,12},{9,13},{10,... | collective-permute-start | bytes 1966088 | tf_op jit(solution)/shard_map/ppermute | solution.py:33
  73.6 12.9 %collective-permute-start.16 = (f32[408,512]{1,0:T(8,128)S(1)}, f32[408,512]{1,0:T(8,128)S(1)}, u32[]{:S(2)}, u32[]{:S(2)}) collective-permute-start(f32[408,512]{1,0:T(8,128)S(1)} %get-tuple-element.141), channel_id=1, source_target_pairs={{0,4},{4,8},{8,12},{12,16},{16,20},{20,24},{24,28},{28,0},{1,5},{5... | collective-permute-start | bytes 2506760 | tf_op jit(solution)/shard_map/ppermute | solution.py:27
  91.2 2.2 %collective-permute-start.17 = (f32[1280,128]{1,0:T(8,128)S(1)}, f32[1280,128]{1,0:T(8,128)S(1)}, u32[]{:S(2)}, u32[]{:S(2)}) collective-permute-start(f32[1280,128]{1,0:T(8,128)S(1)} %slice.97), channel_id=1, source_target_pairs={{0,4},{1,5},{2,6},{3,7},{4,0},{5,1},{6,2},{7,3},{8,12},{9,13},{10,... | collective-permute-start | bytes 1966088 | tf_op jit(solution)/shard_map/ppermute | solution.py:33
  93.5 8.1 %collective-permute-start.18 = (f32[320,128]{1,0:T(8,128)S(1)}, f32[320,128]{1,0:T(8,128)S(1)}, u32[]{:S(2)}, u32[]{:S(2)}) collective-permute-start(f32[320,128]{1,0:T(8,128)S(1)} %get-tuple-element.176), channel_id=1, source_target_pairs={{0,24},{1,25},{2,26},{3,27},{4,28},{5,29},{6,30},{7,31},{8,16},{9,... | collective-permute-start | bytes 491528 | tf_op jit(solution)/shard_map/ppermute | solution.py:33
  94.9 9.3 %collective-permute-start.20 = (f32[320,128]{1,0:T(8,128)S(1)}, f32[320,128]{1,0:T(8,128)S(1)}, u32[]{:S(2)}, u32[]{:S(2)}) collective-permute-start(f32[320,128]{1,0:T(8,128)S(1)} %get-tuple-element.177), channel_id=1, source_target_pairs={{0,16},{1,17},{2,18},{3,19},{4,20},{5,21},{6,22},{7,23},{8,24},{9,... | collective-permute-start | bytes 491528 | tf_op jit(solution)/shard_map/ppermute | solution.py:33
  95.6 8.6 %collective-permute-start.19 = (f32[320,128]{1,0:T(8,128)S(1)}, f32[320,128]{1,0:T(8,128)S(1)}, u32[]{:S(2)}, u32[]{:S(2)}) collective-permute-start(f32[320,128]{1,0:T(8,128)S(1)} %get-tuple-element.178), channel_id=1, source_target_pairs={{0,8},{1,9},{2,10},{3,11},{4,12},{5,13},{6,14},{7,15},{8,0},{9,1},... | collective-permute-start | bytes 491528 | tf_op jit(solution)/shard_map/ppermute | solution.py:33
  104.3 15.6 %collective-permute-start.27 = (f32[408,512]{1,0:T(8,128)S(1)}, f32[408,512]{1,0:T(8,128)S(1)}, u32[]{:S(2)}, u32[]{:S(2)}) collective-permute-start(f32[408,512]{1,0:T(8,128)S(1)} %get-tuple-element.165), channel_id=1, source_target_pairs={{0,4},{4,8},{8,12},{12,16},{16,20},{20,24},{24,28},{28,0},{1,5},{5... | collective-permute-start | bytes 2506760 | tf_op jit(solution)/shard_map/ppermute | solution.py:27
  104.4 6.3 %collective-permute-start.21 = (f32[80,128]{1,0:T(8,128)S(1)}, f32[80,128]{1,0:T(8,128)S(1)}, u32[]{:S(2)}, u32[]{:S(2)}) collective-permute-start(f32[80,128]{1,0:T(8,128)S(1)} %get-tuple-element.182), channel_id=1, source_target_pairs={{0,3},{1,2},{2,1},{3,0},{4,7},{5,6},{6,5},{7,4},{8,11},{9,10},{10,... | collective-permute-start | bytes 122888 | tf_op jit(solution)/shard_map/ppermute | solution.py:33
  107.4 4.9 %collective-permute-start.23 = (f32[80,128]{1,0:T(8,128)S(1)}, f32[80,128]{1,0:T(8,128)S(1)}, u32[]{:S(2)}, u32[]{:S(2)}) collective-permute-start(f32[80,128]{1,0:T(8,128)S(1)} %get-tuple-element.183), channel_id=1, source_target_pairs={{0,2},{1,3},{2,0},{3,1},{4,6},{5,7},{6,4},{7,5},{8,10},{9,11},{10,... | collective-permute-start | bytes 122888 | tf_op jit(solution)/shard_map/ppermute | solution.py:33
  107.4 4.9 %collective-permute-start.22 = (f32[80,128]{1,0:T(8,128)S(1)}, f32[80,128]{1,0:T(8,128)S(1)}, u32[]{:S(2)}, u32[]{:S(2)}) collective-permute-start(f32[80,128]{1,0:T(8,128)S(1)} %get-tuple-element.184), channel_id=1, source_target_pairs={{0,1},{1,0},{2,3},{3,2},{4,5},{5,4},{6,7},{7,6},{8,9},{9,8},{10,11... | collective-permute-start | bytes 122888 | tf_op jit(solution)/shard_map/ppermute | solution.py:33
  112.4 5.9 %collective-permute-start.26 = (f32[80,128]{1,0:T(8,128)S(1)}, f32[80,128]{1,0:T(8,128)S(1)}, u32[]{:S(2)}, u32[]{:S(2)}) collective-permute-start(f32[80,128]{1,0:T(8,128)S(1)} %add_add_fusion.2), channel_id=1, source_target_pairs={{0,3},{1,2},{2,1},{3,0},{4,7},{5,6},{6,5},{7,4},{8,11},{9,10},{10,... | collective-permute-start | bytes 122888 | tf_op jit(solution)/shard_map/ppermute | solution.py:33
  114.9 5.0 %collective-permute-start.25 = (f32[80,128]{1,0:T(8,128)S(1)}, f32[80,128]{1,0:T(8,128)S(1)}, u32[]{:S(2)}, u32[]{:S(2)}) collective-permute-start(f32[80,128]{1,0:T(8,128)S(1)} %add_add_fusion.2), channel_id=1, source_target_pairs={{0,2},{1,3},{2,0},{3,1},{4,6},{5,7},{6,4},{7,5},{8,10},{9,11},{10,... | collective-permute-start | bytes 122888 | tf_op jit(solution)/shard_map/ppermute | solution.py:33
  114.9 5.0 %collective-permute-start.24 = (f32[80,128]{1,0:T(8,128)S(1)}, f32[80,128]{1,0:T(8,128)S(1)}, u32[]{:S(2)}, u32[]{:S(2)}) collective-permute-start(f32[80,128]{1,0:T(8,128)S(1)} %add_add_fusion.2), channel_id=1, source_target_pairs={{0,1},{1,0},{2,3},{3,2},{4,5},{5,4},{6,7},{7,6},{8,9},{9,8},{10,11... | collective-permute-start | bytes 122888 | tf_op jit(solution)/shard_map/ppermute | solution.py:33
  119.9 7.8 %collective-permute-start.30 = (f32[320,128]{1,0:T(8,128)S(1)}, f32[320,128]{1,0:T(8,128)S(1)}, u32[]{:S(2)}, u32[]{:S(2)}) collective-permute-start(f32[320,128]{1,0:T(8,128)S(1)} %pad_maximum_fusion.5), channel_id=1, source_target_pairs={{0,24},{1,25},{2,26},{3,27},{4,28},{5,29},{6,30},{7,31},{8,16},{9,... | collective-permute-start | bytes 491528 | tf_op jit(solution)/shard_map/ppermute | solution.py:33
  121.1 8.0 %collective-permute-start.29 = (f32[320,128]{1,0:T(8,128)S(1)}, f32[320,128]{1,0:T(8,128)S(1)}, u32[]{:S(2)}, u32[]{:S(2)}) collective-permute-start(f32[320,128]{1,0:T(8,128)S(1)} %pad_maximum_fusion.5), channel_id=1, source_target_pairs={{0,16},{1,17},{2,18},{3,19},{4,20},{5,21},{6,22},{7,23},{8,24},{9,... | collective-permute-start | bytes 491528 | tf_op jit(solution)/shard_map/ppermute | solution.py:33
  122.3 6.8 %collective-permute-start.28 = (f32[320,128]{1,0:T(8,128)S(1)}, f32[320,128]{1,0:T(8,128)S(1)}, u32[]{:S(2)}, u32[]{:S(2)}) collective-permute-start(f32[320,128]{1,0:T(8,128)S(1)} %pad_maximum_fusion.5), channel_id=1, source_target_pairs={{0,8},{1,9},{2,10},{3,11},{4,12},{5,13},{6,14},{7,15},{8,0},{9,1},... | collective-permute-start | bytes 491528 | tf_op jit(solution)/shard_map/ppermute | solution.py:33
  129.2 2.2 %collective-permute-start.31 = (f32[1280,128]{1,0:T(8,128)S(1)}, f32[1280,128]{1,0:T(8,128)S(1)}, u32[]{:S(2)}, u32[]{:S(2)}) collective-permute-start(f32[1280,128]{1,0:T(8,128)S(1)} %pad_maximum_fusion.3), channel_id=1, source_target_pairs={{0,4},{1,5},{2,6},{3,7},{4,0},{5,1},{6,2},{7,3},{8,12},{9,13},{10,... | collective-permute-start | bytes 1966088 | tf_op jit(solution)/shard_map/ppermute | solution.py:33
  (6 other events, 51.7 us)

commit v3 on v2

--- a/solution.py
+++ b/solution.py
@@ -83,12 +83,15 @@
     return count, me
 
 
-def sum_everywhere(packed, work, args, work_on_arrival):
+def sum_everywhere(packed, work, args, work_on_arrival, work_on_half):
     plan = reduce_plan(lax.axis_size("blk"), lax.axis_size("grp"))
     if plan is None:
         after, *rest = work(*args)
         arriving = from_behind(after, "blk", 1)
-        return lax.psum(packed, AXES), arriving, *rest, *(work_on_arrival(arriving) if work_on_arrival else ())
+        total = lax.psum(packed, AXES)
+        middle = total.shape[0] // 2
+        own, other = work_on_half(total[:middle]), total[middle:]
+        return own, other, arriving, *rest, *work_on_arrival(arriving)
     stages, singles = plan
     for place, stage in enumerate(stages):
         if place == 1:
@@ -100,14 +103,15 @@
             arriving = from_behind(after, "blk", 1)
     for axis, mask in singles:
         packed = packed + exchange(packed, mask if axis == "blk" else 0, mask if axis == "grp" else 0)
-    for place, stage in reversed(list(enumerate(stages))):
+    for place, stage in reversed(list(enumerate(stages))[1:]):
         if place == 1:
             packed, arriving = lax.optimization_barrier((packed, arriving))
-            rest += work_on_arrival(arriving) if work_on_arrival else []
+            rest += work_on_arrival(arriving)
         packed = gather(packed, stage)
         if place == 1:
             packed, rest = lax.optimization_barrier((packed, rest))
-    return packed, arriving, *rest
+    other = exchange(packed, *group_masks(stages[0])[0][1:])
+    return work_on_half(packed), other, arriving, *rest
 
 
 NN = (((1,), (0,)), ((), ()))
@@ -238,48 +242,48 @@
 def pack_into(packed, parts, kinds):
     width = parts[0][1].shape[0]
     full, tail = divmod(width, LANES)
-    span = tail_span(width, kinds)
-    packed_tail = None
+    span, rows = tail_span(width), packed.ref.shape[0] // kinds
     for kind in range(kinds):
         total = sum(jnp.where(index == kind, part, 0.0) for index, part in parts)
+        start = kind * rows
         for block in range(full):
-            packed.put((kind * full + block) * width, total[:, block * LANES : (block + 1) * LANES])
+            packed.put(start, total[:, block * LANES : (block + 1) * LANES])
+            start += width
         if tail:
-            ends = pad_rows(total[:, full * LANES :], round_up(width, span))
-            for place in range(ends.shape[0] // span):
-                turn = (kind * (ends.shape[0] // span) + place) * tail
-                moved = ends[place * span : (place + 1) * span]
-                moved = pltpu.roll(moved, turn, 1) if turn else moved
+            ends, packed_tail = total[:, full * LANES :], None
+            for place, first in enumerate(range(0, width, span)):
+                moved = ends[first : first + span]
+                moved = moved if moved.shape[0] == span else pad_rows(moved, span)
+                moved = pltpu.roll(moved, place * tail, 1) if place else moved
                 packed_tail = moved if packed_tail is None else packed_tail + moved
-    start = kinds * full * width
+            packed.put(start, packed_tail)
+            start += span
+        if start < (kind + 1) * rows:
+            packed.put(start, jnp.zeros(((kind + 1) * rows - start, LANES), F32))
+
+
+def tail_span(width):
+    tail = width % LANES
+    return round_up(-(-width // (LANES // tail)), 8) if tail else 0
+
+
+def packed_rows(width, kinds, pieces):
+    return kinds * round_up((width // LANES) * width + tail_span(width), 8 * pieces)
+
+
+def unpack(packed, place_of_kind, kinds, scaled_out, kind, scale):
+    width, (full, tail) = scaled_out.shape[1], divmod(scaled_out.shape[1], LANES)
+    start = place_of_kind * (packed.ref.shape[0] // kinds)
+    for block in range(full):
+        scaled_out[kind, :, block * LANES : (block + 1) * LANES] = scale * packed.get(start, width)
+        start += width
     if tail:
-        packed.put(start, packed_tail)
-        start += span
-    packed.put(start, jnp.zeros((packed.ref.shape[0] - start, LANES), F32))
-
-
-def tail_span(width, kinds):
-    tail = width % LANES
-    return round_up(-(-width // (LANES // tail // kinds)), 8) if tail else 0
-
-
-def packed_rows(width, kinds, pieces):
-    return round_up(kinds * (width // LANES) * width + tail_span(width, kinds), 8 * pieces)
-
-
-def unpack(packed, scaled_out, kind, width, scale):
-    kinds, (full, tail) = scaled_out.shape[0], divmod(width, LANES)
-    span = tail_span(width, kinds)
-    for block in range(full):
-        scaled_out[kind, :, block * LANES : (block + 1) * LANES] = scale * packed.get((kind * full + block) * width, width)
-    if tail:
-        ends = packed.get(kinds * full * width, span)
-        places = -(-width // span)
-        for place in range(places):
-            rows = min(span, width - place * span)
-            turn = (kind * places + place) * tail
-            moved = pltpu.roll(ends, LANES - turn, 1) if turn else ends
-            scaled_out[kind, place * span : place * span + rows, full * LANES :] = scale * moved[:rows, :tail]
+        span = tail_span(width)
+        ends = packed.get(start, span)
+        for place, first in enumerate(range(0, width, span)):
+            rows = min(span, width - first)
+            moved = pltpu.roll(ends, LANES - place * tail, 1) if place else ends
+            scaled_out[kind, first : first + rows, full * LANES :] = scale * moved[:rows, :tail]
 
 
 def opening_kernel(me, ids, partners, relations, source, target, target_state, target_out, sgh, sgl, square, xh, xl, qh, ql, scores, matrix, source_in, target_in, state_in, partners_in, ids_in, sems):
@@ -305,31 +309,41 @@
     yh[...], yl[...] = split(pad_rows(target[:width], yh.shape[1]).T)
 
 
-def renew(packed, relations, scaled, renewed, kind, scale):
-    unpack(packed, scaled, kind, relations.shape[1], scale)
-    renewed[kind] = relations[kind] - operator_rate * scaled[kind]
-
-
-def first_kernel(ids, me, partners, packed, relations, xh, xl, target, yh, yl, relations_out, scaled, target_out, sgh, sgl, square, qh, ql, scores, *, bucket, pieces, scale):
+def renew(me, packed, relations, scaled, renewed, pieces, scale, half, done=None):
+    kinds, count = relations.shape[0] // 2, max(pieces // 2, 1)
+    for place in range(kinds):
+        kind = ((me[0] // count) ^ half if pieces > 1 else half) * kinds + place
+        unpack(Pieces(packed, me[0] % count, count), place, kinds, scaled, kind, scale)
+        renewed[kind] = relations[kind] - operator_rate * scaled[kind]
+        if done is not None:
+            done(place, kind)
+
+
+def own_kernel(me, packed, relations, scaled, renewed, *, pieces, scale):
+    renew(me, packed, relations, scaled, renewed, pieces, scale, 0)
+
+
+def first_kernel(ids, me, partners, packed, relations, own_scaled, own_renewed, xh, xl, target, yh, yl, scaled, renewed, target_out, sgh, sgl, square, qh, ql, scores, *, bucket, pieces, scale):
     width = relations.shape[1]
-    for kind in range(relations.shape[0]):
-        renew(Pieces(packed, me[0], pieces), relations, scaled, relations_out, kind, scale)
-    square_of(square, relations_out[ids[bucket]])
+    renew(me, packed, relations, scaled, renewed, pieces, scale, 1)
+    square_of(square, renewed[ids[bucket]])
     queries_into((qh, ql), square, (xh, xl), width)
     score_grad_into((sgh, sgl), scores, (qh, ql), both((yh, yl)), partners[bucket, 0])
     target_into(target_out, (qh, ql), (sgh, sgl), target[:width], target[width : width + 1])
 
 
-def closing_kernel(me, packed, relations, *refs, pieces, scale, place):
-    grads_out, relations_out, scaled, renewed, sems = refs[1 if place else 0 :]
+def closing_kernel(me, packed, relations, *refs, pieces, scale, place, half):
+    grads_out, relations_out, scaled, renewed, sems = refs[-5:]
     stores = []
-    for kind in range(relations.shape[0]):
-        renew(Pieces(packed, me[0], pieces), relations, scaled, renewed, kind, scale)
+
+    def store(slot, kind):
         for here, there in ((scaled, grads_out.at[place]), (renewed, relations_out)):
             stores.append(pltpu.make_async_copy(here.at[kind], there.at[kind], sems.at[len(stores)]))
             stores[-1].start()
-    for store in stores:
-        store.wait()
+
+    renew(me, packed, relations, scaled, renewed, pieces, scale, half, store)
+    for copy in stores:
+        copy.wait()
 
 
 def second_kernel(ids, relations, source, source_state, target, sgh, sgl, *refs, bucket, place):
@@ -400,6 +414,8 @@
 
 def shards(source_rows, source_state, target_rows, destination_state, positives, relation_ids, relations):
     buckets, kinds, width = positives.shape[0], relations.shape[0], relations.shape[1]
+    if kinds % 2 or buckets % 2 or width % 16:
+        raise ValueError("unsupported shapes")
     source, state = source_rows[0, 0], source_state
     target, target_state = target_rows[0, 0], destination_state
     columns, block = source.shape[1], target.shape[1]
@@ -429,10 +445,10 @@
                     (positives.shape[1:], jnp.int32), pltpu.SMEM(ids.shape, jnp.int32), pltpu.SemaphoreType.DMA((6,))],
                 3 * product)
         else:
-            relations, scaled, after, sgh, sgl = call(
+            scaled, relations, after, sgh, sgl = call(
                 functools.partial(first_kernel, bucket=bucket, pieces=pieces, scale=scale), "first",
-                (ids, me, positives, total, relations, xh, xl, target, yh, yl), [SMEM] * 2 + [VMEM] * 8,
-                [rel_out, rel_out] + moving + sg_pair, square + q_pair + scores, 3 * product)
+                (ids, me, positives, other, relations, *own, xh, xl, target, yh, yl), [SMEM] * 2 + [VMEM] * 10,
+                [rel_out, rel_out] + moving + sg_pair, square + q_pair + scores, 3 * product, aliases={5: 0, 6: 1})
         arriving = from_behind(after, "blk", 1)
         args, outs = (ids, relations, source, state, target, sgh, sgl), source_outs + [((width, wide), F32)] + q_pair + q_pair
         if update == 0:
@@ -451,27 +467,33 @@
             functools.partial(third_kernel, bucket=bucket + 1, kinds=kinds, pieces=pieces), "third",
             (ids, me, positives, xh, xl, target, qh, ql, grad), [SMEM] * 2 + [VMEM] * 7,
             [packed_out] + sg_pair + q_pair, scores, 3 * product)
-        total, target, source, state, *prepared = sum_everywhere(
+
+        def close(half, own=None):
+            before = tuple(own) if own is not None else () if grads is None else (grads,)
+            return call(
+                functools.partial(closing_kernel, pieces=pieces, scale=scale, place=updates - 1, half=0 if own is None else 1), "closing",
+                (me, half, relations, *before), [SMEM, VMEM, VMEM] + [HBM] * len(before),
+                [grads_out, rel_out], [rel_out, rel_out, pltpu.SemaphoreType.DMA((kinds,))],
+                product // 4, [HBM, HBM], {3 + i: i for i in range(len(before))})
+
+        own, other, target, source, state, *prepared = sum_everywhere(
             packed,
             lambda *args: call(
                 functools.partial(fourth_kernel, bucket=bucket + 1), "fourth",
                 (ids, *args), [SMEM] + [VMEM] * len(args), moving + source_outs + ([] if last else q_pair), square, 2 * product),
             (relations, source, state, target, qh, ql, sgh, sgl, gh, gl),
-            None if last else lambda target: call(
-                functools.partial(prepare_kernel, width=width), "prepare", (target,), [VMEM], y_pair, (), product // 4))
+            (lambda target: [target[None, None, :width], target[None, width : width + 1]]) if last else lambda target: call(
+                functools.partial(prepare_kernel, width=width), "prepare", (target,), [VMEM], y_pair, (), product // 4),
+            close if last else lambda half: call(
+                functools.partial(own_kernel, pieces=pieces, scale=scale), "own",
+                (me, half, relations), [SMEM, VMEM, VMEM], [rel_out, rel_out], (), product // 4))
         if not last:
             xh, xl, yh, yl = prepared
-    before = () if grads is None else (grads,)
-    grads, relations = call(
-        functools.partial(closing_kernel, pieces=pieces, scale=scale, place=updates - 1), "closing",
-        (me, total, relations, *before), [SMEM, VMEM, VMEM] + [HBM] * len(before),
-        [grads_out, rel_out], [rel_out, rel_out, pltpu.SemaphoreType.DMA((2 * kinds,))],
-        product, [HBM, HBM], {3: 0} if before else None)
+    grads, relations = close(other, own)
     return (
         source[None, None],
         state,
-        target[None, None, :width],
-        target[None, width : width + 1],
+        *prepared,
         relations,
         grads,
     )

time: 134 us -> 133 us (level)
  waiting for transfers between devices: 54.1 us -> 52.2 us
    ppermute x28, waiting for transfers between devices: 39 us -> 37.1 us  [exchange(): return lax.ppermute(value, AXES, pairs)]
    pallas_call x10 -> x12, Pallas kernels: 42.1 us -> 43.3 us  [call(): pl.pallas_call(kernel, in_specs=args_in, out_specs=outs_in or [VMEM] * le...]
  transfers between devices with their start and end apart: 32 -> 32, of which waited for: 24 -> 24; matrix products, arithmetic and copies ran while one was open for 1% -> 1% of each run, Pallas kernels for 14% -> 15%
where the time goes in v3:
time: 133 us
  waiting for transfers between devices  52.2 us (39%)
  Pallas kernels  43.3 us (33%)
  starting transfers between devices  33.8 us (25%)
  local copies, waits for them, and re-layouts  1.73 us (1%)
    pallas_call x12, Pallas kernels, call(): pl.pallas_call(kernel, in_specs=args_in, out_specs=outs_in or [VMEM] * le...  43.3 us
    ppermute x28, waiting for transfers between devices, exchange(): return lax.ppermute(value, AXES, pairs)  37.1 us
    ppermute x28, starting transfers between devices, exchange(): return lax.ppermute(value, AXES, pairs)  32.5 us
    ppermute x4, waiting for transfers between devices, from_behind(): return lax.ppermute(value, axis, pairs)  15.1 us
  transfers between devices with their start and end apart: 32, of which 24 were waited for; matrix products, arithmetic and copies ran while one was open for 1% of the time, Pallas kernels for 15%

profile of v3, /device:TPU:0, one launch (start us, length us, event | category | flops | bytes accessed | tf_op | source)
XLA Modules:
  0.0 132.7 jit_solution(5492823255083195719)
XLA Ops:
  0.8 7.0 %opening.1 = (f32[408,512]{1,0:T(8,128)S(1)}, bf16[512,768]{1,0:T(8,128)(2,1)S(1)}, bf16[512,768]{1,0:T(8,128)(2,1)S(1)}) custom-call(s32[1]{0:T(128)} %bitcast.1.me, s32[4]{0:T(128)} %bitcast.9, s32[4,1,1,768]{3,2,1,0:T(1,128)} %partners.7, f32[2,400,400]{2,1,0:T(8,128)} %relations.8, f32[400,768]{1,0:T(8,128)} %bitcast.17, f32[400,512]{1,0:T(8,128)} %bitcast.19, ...), custom_call_target="tpu_custom_call" | custom-call | flops 2211840000 | tf_op jit(solution)/shard_map/opening/pallas_call | solution.py:399
  8.5 5.2 %second.2 = (f32[400,768]{1,0:T(8,128)S(1)}, f32[1,1,768]{2,1,0:T(1,128)S(1)}, f32[400,512]{1,0:T(8,128)S(1)}, bf16[512,768]{1,0:T(8,128)(2,1)S(1)}, bf16[512,76...) custom-call(s32[4]{0:T(128)S(1)} %bitcast.10, f32[2,400,400]{2,1,0:T(8,128)S(1)} %copy-done, ...), custom_call_target="tpu_custom_call" | custom-call | flops 2949120000 | tf_op jit(solution)/shard_map/second/pallas_call | solution.py:399
  13.7 7.8 %collective-permute-done.target = f32[408,512]{1,0:T(8,128)S(1)} collective-permute-done((f32[408,512]{1,0:T(8,128)S(1)}, f32[408,512]{1,0:T(8,128)S(1)}, u32[]{:S(2)}, u32[]{:S(2)}) %collective-permute-start) | collective-permute-done | bytes 835616 | tf_op jit(solution)/shard_map/ppermute | solution.py:27
  21.5 4.7 %third.2 = (f32[2560,128]{1,0:T(8,128)S(1)}, bf16[512,768]{1,0:T(8,128)(2,1)S(1)}, bf16[512,768]{1,0:T(8,128)(2,1)S(1)}, bf16[512,768]{1,0:T(8,128)(2,1)S(1)}, bf16[512,768]{1,0:T(8,128)(2,1)S(1)}) custom-call(s32[4]{0:T(128)S(1)} %bitcast.11, s32[1]{0:T(128)} %bitcast.1.me, s32[4,1,1,768]{3,2,1,0:T(1,128)S(1)} %copy-done.1, ...), custom_call_target="tpu_custom_call" | custom-call | flops 2211840000 | tf_op jit(solution)/shard_map/third/pallas_call | solution.py:399
  26.4 2.1 %collective-permute-done.1 = f32[1280,128]{1,0:T(8,128)S(1)} collective-permute-done((f32[1280,128]{1,0:T(8,128)S(1)}, f32[1280,128]{1,0:T(8,128)S(1)}, u32[]{:S(2)}, u32[]{:S(2)}) %collective-permute-start.1) | collective-permute-done | bytes 655392 | tf_op jit(solution)/shard_map/ppermute | solution.py:33
  28.6 2.4 %collective-permute-start.2 = (f32[320,128]{1,0:T(8,128)S(1)}, f32[320,128]{1,0:T(8,128)S(1)}, u32[]{:S(2)}, u32[]{:S(2)}) collective-permute-start(f32[320,128]{1,0:T(8,128)S(1)} %get-tuple-element.191), channel_id=1, source_target_pairs={{0,24},{1,25},{2,26},{3,27},{4,28},{5,29},{6,30},{7,31},{8,16},{9,... | collective-permute-start | bytes 491528 | tf_op jit(solution)/shard_map/ppermute | solution.py:33
  32.4 3.4 %fourth.2 = (f32[408,512]{1,0:T(8,128)S(1)}, f32[400,768]{1,0:T(8,128)S(1)}, f32[1,1,768]{2,1,0:T(1,128)S(1)}, bf16[512,768]{1,0:T(8,128)(2,1)S(1)}, bf16[512,768]{1,0:T(8,128)(2,1)S(1)}) custom-call(s32[4]{0:T(128)S(1)} %bitcast.12, f32[2,400,400]{2,1,0:T(8,128)S(1)} %copy-done, f32[400,768]{1,0:T(8,128)S(1)} %get-tuple-element.114.source, ...), custom_call_target="tpu_custom_call" | custom-call | flops 1474560000 | tf_op jit(solution)/shard_map/fourth/pallas_call | solution.py:399
  36.6 2.7 %collective-permute-done.4 = f32[320,128]{1,0:T(8,128)S(1)} collective-permute-done((f32[320,128]{1,0:T(8,128)S(1)}, f32[320,128]{1,0:T(8,128)S(1)}, u32[]{:S(2)}, u32[]{:S(2)}) %collective-permute-start.4) | collective-permute-done | bytes 163872 | tf_op jit(solution)/shard_map/ppermute | solution.py:33
  40.5 3.7 %collective-permute-start.5 = (f32[80,128]{1,0:T(8,128)S(1)}, f32[80,128]{1,0:T(8,128)S(1)}, u32[]{:S(2)}, u32[]{:S(2)}) collective-permute-start(f32[80,128]{1,0:T(8,128)S(1)} %get-tuple-element.197), channel_id=1, source_target_pairs={{0,3},{1,2},{2,1},{3,0},{4,7},{5,6},{6,5},{7,4},{8,11},{9,10},{10,... | collective-permute-start | bytes 122888 | tf_op jit(solution)/shard_map/ppermute | solution.py:33
  44.9 1.7 %collective-permute-done.5 = f32[80,128]{1,0:T(8,128)S(1)} collective-permute-done((f32[80,128]{1,0:T(8,128)S(1)}, f32[80,128]{1,0:T(8,128)S(1)}, u32[]{:S(2)}, u32[]{:S(2)}) %collective-permute-start.5) | collective-permute-done | bytes 40992 | tf_op jit(solution)/shard_map/ppermute | solution.py:33
  46.6 2.5 %collective-permute-done.7 = f32[80,128]{1,0:T(8,128)S(1)} collective-permute-done((f32[80,128]{1,0:T(8,128)S(1)}, f32[80,128]{1,0:T(8,128)S(1)}, u32[]{:S(2)}, u32[]{:S(2)}) %collective-permute-start.7) | collective-permute-done | bytes 40992 | tf_op jit(solution)/shard_map/ppermute | solution.py:33
  49.1 2.0 %collective-permute-start.10 = (f32[80,128]{1,0:T(8,128)S(1)}, f32[80,128]{1,0:T(8,128)S(1)}, u32[]{:S(2)}, u32[]{:S(2)}) collective-permute-start(f32[80,128]{1,0:T(8,128)S(1)} %add_add_fusion.3), channel_id=1, source_target_pairs={{0,3},{1,2},{2,1},{3,0},{4,7},{5,6},{6,5},{7,4},{8,11},{9,10},{10,... | collective-permute-start | bytes 122888 | tf_op jit(solution)/shard_map/ppermute | solution.py:33
  51.6 1.9 %collective-permute-start.8 = (f32[80,128]{1,0:T(8,128)S(1)}, f32[80,128]{1,0:T(8,128)S(1)}, u32[]{:S(2)}, u32[]{:S(2)}) collective-permute-start(f32[80,128]{1,0:T(8,128)S(1)} %add_add_fusion.3), channel_id=1, source_target_pairs={{0,1},{1,0},{2,3},{3,2},{4,5},{5,4},{6,7},{7,6},{8,9},{9,8},{10,11... | collective-permute-start | bytes 122888 | tf_op jit(solution)/shard_map/ppermute | solution.py:33
  56.4 1.9 %collective-permute-start.14 = (f32[320,128]{1,0:T(8,128)S(1)}, f32[320,128]{1,0:T(8,128)S(1)}, u32[]{:S(2)}, u32[]{:S(2)}) collective-permute-start(f32[320,128]{1,0:T(8,128)S(1)} %pad_maximum_fusion.2), channel_id=1, source_target_pairs={{0,24},{1,25},{2,26},{3,27},{4,28},{5,29},{6,30},{7,31},{8,16},{9,... | collective-permute-start | bytes 491528 | tf_op jit(solution)/shard_map/ppermute | solution.py:33
  60.3 3.9 %collective-permute-done.14 = f32[320,128]{1,0:T(8,128)S(1)} collective-permute-done((f32[320,128]{1,0:T(8,128)S(1)}, f32[320,128]{1,0:T(8,128)S(1)}, u32[]{:S(2)}, u32[]{:S(2)}) %collective-permute-start.14) | collective-permute-done | bytes 163872 | tf_op jit(solution)/shard_map/ppermute | solution.py:33
  64.2 1.5 %collective-permute-done.13 = f32[320,128]{1,0:T(8,128)S(1)} collective-permute-done((f32[320,128]{1,0:T(8,128)S(1)}, f32[320,128]{1,0:T(8,128)S(1)}, u32[]{:S(2)}, u32[]{:S(2)}) %collective-permute-start.13) | collective-permute-done | bytes 163872 | tf_op jit(solution)/shard_map/ppermute | solution.py:33
  66.3 1.8 %collective-permute-done.15.packed = f32[1280,128]{1,0:T(8,128)S(1)} collective-permute-done((f32[1280,128]{1,0:T(8,128)S(1)}, f32[1280,128]{1,0:T(8,128)S(1)}, u32[]{:S(2)}, u32[]{:S(2)}) %collective-permute-start.15) | collective-permute-done | bytes 655392 | tf_op jit(solution)/shard_map/ppermute | solution.py:33
  68.1 5.2 %first.1 = (f32[2,400,400]{2,1,0:T(8,128)S(1)}, f32[2,400,400]{2,1,0:T(8,128)S(1)}, f32[408,512]{1,0:T(8,128)S(1)}, bf16[512,768]{1,0:T(8,128)(2,1)S(1)}, bf16[512,768]{1,0:T(8,128)(2,1)S(1)}) custom-call(s32[4]{0:T(128)S(1)} %bitcast.13, s32[1]{0:T(128)} %bitcast.1.me, ...), custom_call_target="tpu_custom_call", output_to_operand_aliasing={{0}: (5, {}), {1}: (6, {})} | custom-call | flops 2211840000 | tf_op jit(solution)/shard_map/first/pallas_call | solution.py:399
  73.5 5.4 %second.3 = (f32[400,768]{1,0:T(8,128)S(1)}, f32[1,1,768]{2,1,0:T(1,128)S(1)}, f32[400,512]{1,0:T(8,128)S(1)}, bf16[512,768]{1,0:T(8,128)(2,1)S(1)}, bf16[512,76...) custom-call(s32[4]{0:T(128)S(1)} %bitcast.14, ...), custom_call_target="tpu_custom_call" | custom-call | flops 2949120000 | tf_op jit(solution)/shard_map/second/pallas_call | solution.py:399
  78.9 7.3 %collective-permute-done.16.target = f32[408,512]{1,0:T(8,128)S(1)} collective-permute-done((f32[408,512]{1,0:T(8,128)S(1)}, f32[408,512]{1,0:T(8,128)S(1)}, u32[]{:S(2)}, u32[]{:S(2)}) %collective-permute-start.16) | collective-permute-done | bytes 835616 | tf_op jit(solution)/shard_map/ppermute | solution.py:27
  86.2 4.7 %third.3 = (f32[2560,128]{1,0:T(8,128)S(1)}, bf16[512,768]{1,0:T(8,128)(2,1)S(1)}, bf16[512,768]{1,0:T(8,128)(2,1)S(1)}, bf16[512,768]{1,0:T(8,128)(2,1)S(1)}, bf16[512,768]{1,0:T(8,128)(2,1)S(1)}) custom-call(s32[4]{0:T(128)S(1)} %bitcast.15, s32[1]{0:T(128)} %bitcast.1.me, s32[4,1,1,768]{3,2,1,0:T(1,128)S(1)} %copy-done.1, ...), custom_call_target="tpu_custom_call" | custom-call | flops 2211840000 | tf_op jit(solution)/shard_map/third/pallas_call | solution.py:399
  91.0 2.1 %collective-permute-done.17 = f32[1280,128]{1,0:T(8,128)S(1)} collective-permute-done((f32[1280,128]{1,0:T(8,128)S(1)}, f32[1280,128]{1,0:T(8,128)S(1)}, u32[]{:S(2)}, u32[]{:S(2)}) %collective-permute-start.17) | collective-permute-done | bytes 655392 | tf_op jit(solution)/shard_map/ppermute | solution.py:33
  96.8 4.1 %fourth.3 = (f32[408,512]{1,0:T(8,128)S(1)}, f32[400,768]{1,0:T(8,128)}, f32[1,1,768]{2,1,0:T(1,128)}) custom-call(s32[4]{0:T(128)S(1)} %bitcast.16, f32[2,400,400]{2,1,0:T(8,128)S(1)} %get-tuple-element.161.relations, f32[400,768]{1,0:T(8,128)S(1)} %get-tuple-element.162.source, f32[1,1,768]{2,1,0:T(1,128)S(1)} %get-tuple-element.163.source_state, ...), custom_call_target="tpu_custom_call" | custom-call | flops 1474560000 | tf_op jit(solution)/shard_map/fourth/pallas_call | solution.py:399
  101.3 2.6 %collective-permute-done.20 = f32[320,128]{1,0:T(8,128)S(1)} collective-permute-done((f32[320,128]{1,0:T(8,128)S(1)}, f32[320,128]{1,0:T(8,128)S(1)}, u32[]{:S(2)}, u32[]{:S(2)}) %collective-permute-start.20) | collective-permute-done | bytes 163872 | tf_op jit(solution)/shard_map/ppermute | solution.py:33
  104.0 3.1 %collective-permute-start.21 = (f32[80,128]{1,0:T(8,128)S(1)}, f32[80,128]{1,0:T(8,128)S(1)}, u32[]{:S(2)}, u32[]{:S(2)}) collective-permute-start(f32[80,128]{1,0:T(8,128)S(1)} %get-tuple-element.194), channel_id=1, source_target_pairs={{0,3},{1,2},{2,1},{3,0},{4,7},{5,6},{6,5},{7,4},{8,11},{9,10},{10,... | collective-permute-start | bytes 122888 | tf_op jit(solution)/shard_map/ppermute | solution.py:33
  108.5 1.8 %collective-permute-done.21 = f32[80,128]{1,0:T(8,128)S(1)} collective-permute-done((f32[80,128]{1,0:T(8,128)S(1)}, f32[80,128]{1,0:T(8,128)S(1)}, u32[]{:S(2)}, u32[]{:S(2)}) %collective-permute-start.21) | collective-permute-done | bytes 40992 | tf_op jit(solution)/shard_map/ppermute | solution.py:33
  110.3 1.7 %collective-permute-done.23 = f32[80,128]{1,0:T(8,128)S(1)} collective-permute-done((f32[80,128]{1,0:T(8,128)S(1)}, f32[80,128]{1,0:T(8,128)S(1)}, u32[]{:S(2)}, u32[]{:S(2)}) %collective-permute-start.23) | collective-permute-done | bytes 40992 | tf_op jit(solution)/shard_map/ppermute | solution.py:33
  112.0 2.5 %collective-permute-start.26 = (f32[80,128]{1,0:T(8,128)S(1)}, f32[80,128]{1,0:T(8,128)S(1)}, u32[]{:S(2)}, u32[]{:S(2)}) collective-permute-start(f32[80,128]{1,0:T(8,128)S(1)} %add_add_fusion.2), channel_id=1, source_target_pairs={{0,3},{1,2},{2,1},{3,0},{4,7},{5,6},{6,5},{7,4},{8,11},{9,10},{10,... | collective-permute-start | bytes 122888 | tf_op jit(solution)/shard_map/ppermute | solution.py:33
  114.5 1.9 %collective-permute-start.24 = (f32[80,128]{1,0:T(8,128)S(1)}, f32[80,128]{1,0:T(8,128)S(1)}, u32[]{:S(2)}, u32[]{:S(2)}) collective-permute-start(f32[80,128]{1,0:T(8,128)S(1)} %add_add_fusion.2), channel_id=1, source_target_pairs={{0,1},{1,0},{2,3},{3,2},{4,5},{5,4},{6,7},{7,6},{8,9},{9,8},{10,11... | collective-permute-start | bytes 122888 | tf_op jit(solution)/shard_map/ppermute | solution.py:33
  117.9 1.7 %collective-permute-done.25 = f32[80,128]{1,0:T(8,128)S(1)} collective-permute-done((f32[80,128]{1,0:T(8,128)S(1)}, f32[80,128]{1,0:T(8,128)S(1)}, u32[]{:S(2)}, u32[]{:S(2)}) %collective-permute-start.25) | collective-permute-done | bytes 40992 | tf_op jit(solution)/shard_map/ppermute | solution.py:33
  124.7 2.7 %collective-permute-done.30 = f32[320,128]{1,0:T(8,128)S(1)} collective-permute-done((f32[320,128]{1,0:T(8,128)S(1)}, f32[320,128]{1,0:T(8,128)S(1)}, u32[]{:S(2)}, u32[]{:S(2)}) %collective-permute-start.30) | collective-permute-done | bytes 163872 | tf_op jit(solution)/shard_map/ppermute | solution.py:33
  128.9 1.5 %closing.2 = (f32[2,2,400,400]{3,2,1,0:T(8,128)}, f32[2,400,400]{2,1,0:T(8,128)}) custom-call(s32[1]{0:T(128)} %bitcast.1.me, f32[1280,128]{1,0:T(8,128)S(1)} %pad_maximum_fusion.1.packed, f32[2,400,400]{2,1,0:T(8,128)S(1)} %get-tuple-element.161.relations, f32[2,2,400,400]{3,2,1,0:T(8,128)} %get-tuple-element.183.refs_0_), custom_call_target="tpu_custom_call", output_to_operand_aliasing={{0}: (3, {})} | custom-call | flops 184320000 | tf_op jit(solution)/shard_map/closing/pallas_call | solution.py:399
  (74 shorter events, 27.0 us)
Async XLA Ops:
  7.7 13.8 %collective-permute-start = (f32[408,512]{1,0:T(8,128)S(1)}, f32[408,512]{1,0:T(8,128)S(1)}, u32[]{:S(2)}, u32[]{:S(2)}) collective-permute-start(f32[408,512]{1,0:T(8,128)S(1)} %get-tuple-element.101), channel_id=1, source_target_pairs={{0,4},{4,8},{8,12},{12,16},{16,20},{20,24},{24,28},{28,0},{1,5},{5... | collective-permute-start | bytes 2506760 | tf_op jit(solution)/shard_map/ppermute | solution.py:27
  26.3 2.2 %collective-permute-start.1 = (f32[1280,128]{1,0:T(8,128)S(1)}, f32[1280,128]{1,0:T(8,128)S(1)}, u32[]{:S(2)}, u32[]{:S(2)}) collective-permute-start(f32[1280,128]{1,0:T(8,128)S(1)} %slice.87), channel_id=1, source_target_pairs={{0,4},{1,5},{2,6},{3,7},{4,0},{5,1},{6,2},{7,3},{8,12},{9,13},{10,... | collective-permute-start | bytes 1966088 | tf_op jit(solution)/shard_map/ppermute | solution.py:33
  28.6 8.0 %collective-permute-start.2 = (f32[320,128]{1,0:T(8,128)S(1)}, f32[320,128]{1,0:T(8,128)S(1)}, u32[]{:S(2)}, u32[]{:S(2)}) collective-permute-start(f32[320,128]{1,0:T(8,128)S(1)} %get-tuple-element.191), channel_id=1, source_target_pairs={{0,24},{1,25},{2,26},{3,27},{4,28},{5,29},{6,30},{7,31},{8,16},{9,... | collective-permute-start | bytes 491528 | tf_op jit(solution)/shard_map/ppermute | solution.py:33
  30.9 8.4 %collective-permute-start.4 = (f32[320,128]{1,0:T(8,128)S(1)}, f32[320,128]{1,0:T(8,128)S(1)}, u32[]{:S(2)}, u32[]{:S(2)}) collective-permute-start(f32[320,128]{1,0:T(8,128)S(1)} %get-tuple-element.192), channel_id=1, source_target_pairs={{0,16},{1,17},{2,18},{3,19},{4,20},{5,21},{6,22},{7,23},{8,24},{9,... | collective-permute-start | bytes 491528 | tf_op jit(solution)/shard_map/ppermute | solution.py:33
  31.4 8.7 %collective-permute-start.3 = (f32[320,128]{1,0:T(8,128)S(1)}, f32[320,128]{1,0:T(8,128)S(1)}, u32[]{:S(2)}, u32[]{:S(2)}) collective-permute-start(f32[320,128]{1,0:T(8,128)S(1)} %get-tuple-element.193), channel_id=1, source_target_pairs={{0,8},{1,9},{2,10},{3,11},{4,12},{5,13},{6,14},{7,15},{8,0},{9,1},... | collective-permute-start | bytes 491528 | tf_op jit(solution)/shard_map/ppermute | solution.py:33
  40.2 16.2 %collective-permute-start.11 = (f32[408,512]{1,0:T(8,128)S(1)}, f32[408,512]{1,0:T(8,128)S(1)}, u32[]{:S(2)}, u32[]{:S(2)}) collective-permute-start(f32[408,512]{1,0:T(8,128)S(1)} %get-tuple-element.125), channel_id=1, source_target_pairs={{0,4},{4,8},{8,12},{12,16},{16,20},{20,24},{24,28},{28,0},{1,5},{5... | collective-permute-start | bytes 2506760 | tf_op jit(solution)/shard_map/ppermute | solution.py:27
  40.5 6.1 %collective-permute-start.5 = (f32[80,128]{1,0:T(8,128)S(1)}, f32[80,128]{1,0:T(8,128)S(1)}, u32[]{:S(2)}, u32[]{:S(2)}) collective-permute-start(f32[80,128]{1,0:T(8,128)S(1)} %get-tuple-element.197), channel_id=1, source_target_pairs={{0,3},{1,2},{2,1},{3,0},{4,7},{5,6},{6,5},{7,4},{8,11},{9,10},{10,... | collective-permute-start | bytes 122888 | tf_op jit(solution)/shard_map/ppermute | solution.py:33
  44.2 4.9 %collective-permute-start.7 = (f32[80,128]{1,0:T(8,128)S(1)}, f32[80,128]{1,0:T(8,128)S(1)}, u32[]{:S(2)}, u32[]{:S(2)}) collective-permute-start(f32[80,128]{1,0:T(8,128)S(1)} %get-tuple-element.198), channel_id=1, source_target_pairs={{0,2},{1,3},{2,0},{3,1},{4,6},{5,7},{6,4},{7,5},{8,10},{9,11},{10,... | collective-permute-start | bytes 122888 | tf_op jit(solution)/shard_map/ppermute | solution.py:33
  44.2 4.9 %collective-permute-start.6 = (f32[80,128]{1,0:T(8,128)S(1)}, f32[80,128]{1,0:T(8,128)S(1)}, u32[]{:S(2)}, u32[]{:S(2)}) collective-permute-start(f32[80,128]{1,0:T(8,128)S(1)} %get-tuple-element.199), channel_id=1, source_target_pairs={{0,1},{1,0},{2,3},{3,2},{4,5},{5,4},{6,7},{7,6},{8,9},{9,8},{10,11... | collective-permute-start | bytes 122888 | tf_op jit(solution)/shard_map/ppermute | solution.py:33
  49.1 5.9 %collective-permute-start.10 = (f32[80,128]{1,0:T(8,128)S(1)}, f32[80,128]{1,0:T(8,128)S(1)}, u32[]{:S(2)}, u32[]{:S(2)}) collective-permute-start(f32[80,128]{1,0:T(8,128)S(1)} %add_add_fusion.3), channel_id=1, source_target_pairs={{0,3},{1,2},{2,1},{3,0},{4,7},{5,6},{6,5},{7,4},{8,11},{9,10},{10,... | collective-permute-start | bytes 122888 | tf_op jit(solution)/shard_map/ppermute | solution.py:33
  51.1 5.3 %collective-permute-start.9 = (f32[80,128]{1,0:T(8,128)S(1)}, f32[80,128]{1,0:T(8,128)S(1)}, u32[]{:S(2)}, u32[]{:S(2)}) collective-permute-start(f32[80,128]{1,0:T(8,128)S(1)} %add_add_fusion.3), channel_id=1, source_target_pairs={{0,2},{1,3},{2,0},{3,1},{4,6},{5,7},{6,4},{7,5},{8,10},{9,11},{10,... | collective-permute-start | bytes 122888 | tf_op jit(solution)/shard_map/ppermute | solution.py:33
  51.6 4.8 %collective-permute-start.8 = (f32[80,128]{1,0:T(8,128)S(1)}, f32[80,128]{1,0:T(8,128)S(1)}, u32[]{:S(2)}, u32[]{:S(2)}) collective-permute-start(f32[80,128]{1,0:T(8,128)S(1)} %add_add_fusion.3), channel_id=1, source_target_pairs={{0,1},{1,0},{2,3},{3,2},{4,5},{5,4},{6,7},{7,6},{8,9},{9,8},{10,11... | collective-permute-start | bytes 122888 | tf_op jit(solution)/shard_map/ppermute | solution.py:33
  56.4 7.8 %collective-permute-start.14 = (f32[320,128]{1,0:T(8,128)S(1)}, f32[320,128]{1,0:T(8,128)S(1)}, u32[]{:S(2)}, u32[]{:S(2)}) collective-permute-start(f32[320,128]{1,0:T(8,128)S(1)} %pad_maximum_fusion.2), channel_id=1, source_target_pairs={{0,24},{1,25},{2,26},{3,27},{4,28},{5,29},{6,30},{7,31},{8,16},{9,... | collective-permute-start | bytes 491528 | tf_op jit(solution)/shard_map/ppermute | solution.py:33
  58.4 7.4 %collective-permute-start.13 = (f32[320,128]{1,0:T(8,128)S(1)}, f32[320,128]{1,0:T(8,128)S(1)}, u32[]{:S(2)}, u32[]{:S(2)}) collective-permute-start(f32[320,128]{1,0:T(8,128)S(1)} %pad_maximum_fusion.2), channel_id=1, source_target_pairs={{0,16},{1,17},{2,18},{3,19},{4,20},{5,21},{6,22},{7,23},{8,24},{9,... | collective-permute-start | bytes 491528 | tf_op jit(solution)/shard_map/ppermute | solution.py:33
  58.9 7.0 %collective-permute-start.12 = (f32[320,128]{1,0:T(8,128)S(1)}, f32[320,128]{1,0:T(8,128)S(1)}, u32[]{:S(2)}, u32[]{:S(2)}) collective-permute-start(f32[320,128]{1,0:T(8,128)S(1)} %pad_maximum_fusion.2), channel_id=1, source_target_pairs={{0,8},{1,9},{2,10},{3,11},{4,12},{5,13},{6,14},{7,15},{8,0},{9,1},... | collective-permute-start | bytes 491528 | tf_op jit(solution)/shard_map/ppermute | solution.py:33
  65.9 2.2 %collective-permute-start.15 = (f32[1280,128]{1,0:T(8,128)S(1)}, f32[1280,128]{1,0:T(8,128)S(1)}, u32[]{:S(2)}, u32[]{:S(2)}) collective-permute-start(f32[1280,128]{1,0:T(8,128)S(1)} %pad_maximum_fusion.packed), channel_id=1, source_target_pairs={{0,4},{1,5},{2,6},{3,7},{4,0},{5,1},{6,2},{7,3},{8,12},{9,13},{10,... | collective-permute-start | bytes 1966088 | tf_op jit(solution)/shard_map/ppermute | solution.py:33
  73.3 12.9 %collective-permute-start.16 = (f32[408,512]{1,0:T(8,128)S(1)}, f32[408,512]{1,0:T(8,128)S(1)}, u32[]{:S(2)}, u32[]{:S(2)}) collective-permute-start(f32[408,512]{1,0:T(8,128)S(1)} %get-tuple-element.149), channel_id=1, source_target_pairs={{0,4},{4,8},{8,12},{12,16},{16,20},{20,24},{24,28},{28,0},{1,5},{5... | collective-permute-start | bytes 2506760 | tf_op jit(solution)/shard_map/ppermute | solution.py:27
  90.9 2.2 %collective-permute-start.17 = (f32[1280,128]{1,0:T(8,128)S(1)}, f32[1280,128]{1,0:T(8,128)S(1)}, u32[]{:S(2)}, u32[]{:S(2)}) collective-permute-start(f32[1280,128]{1,0:T(8,128)S(1)} %slice.97), channel_id=1, source_target_pairs={{0,4},{1,5},{2,6},{3,7},{4,0},{5,1},{6,2},{7,3},{8,12},{9,13},{10,... | collective-permute-start | bytes 1966088 | tf_op jit(solution)/shard_map/ppermute | solution.py:33
  93.2 8.1 %collective-permute-start.18 = (f32[320,128]{1,0:T(8,128)S(1)}, f32[320,128]{1,0:T(8,128)S(1)}, u32[]{:S(2)}, u32[]{:S(2)}) collective-permute-start(f32[320,128]{1,0:T(8,128)S(1)} %get-tuple-element.188), channel_id=1, source_target_pairs={{0,24},{1,25},{2,26},{3,27},{4,28},{5,29},{6,30},{7,31},{8,16},{9,... | collective-permute-start | bytes 491528 | tf_op jit(solution)/shard_map/ppermute | solution.py:33
  94.6 9.3 %collective-permute-start.20 = (f32[320,128]{1,0:T(8,128)S(1)}, f32[320,128]{1,0:T(8,128)S(1)}, u32[]{:S(2)}, u32[]{:S(2)}) collective-permute-start(f32[320,128]{1,0:T(8,128)S(1)} %get-tuple-element.189), channel_id=1, source_target_pairs={{0,16},{1,17},{2,18},{3,19},{4,20},{5,21},{6,22},{7,23},{8,24},{9,... | collective-permute-start | bytes 491528 | tf_op jit(solution)/shard_map/ppermute | solution.py:33
  95.3 8.6 %collective-permute-start.19 = (f32[320,128]{1,0:T(8,128)S(1)}, f32[320,128]{1,0:T(8,128)S(1)}, u32[]{:S(2)}, u32[]{:S(2)}) collective-permute-start(f32[320,128]{1,0:T(8,128)S(1)} %get-tuple-element.190), channel_id=1, source_target_pairs={{0,8},{1,9},{2,10},{3,11},{4,12},{5,13},{6,14},{7,15},{8,0},{9,1},... | collective-permute-start | bytes 491528 | tf_op jit(solution)/shard_map/ppermute | solution.py:33
  104.0 15.7 %collective-permute-start.27 = (f32[408,512]{1,0:T(8,128)S(1)}, f32[408,512]{1,0:T(8,128)S(1)}, u32[]{:S(2)}, u32[]{:S(2)}) collective-permute-start(f32[408,512]{1,0:T(8,128)S(1)} %get-tuple-element.173), channel_id=1, source_target_pairs={{0,4},{4,8},{8,12},{12,16},{16,20},{20,24},{24,28},{28,0},{1,5},{5... | collective-permute-start | bytes 2506760 | tf_op jit(solution)/shard_map/ppermute | solution.py:27
  104.0 6.3 %collective-permute-start.21 = (f32[80,128]{1,0:T(8,128)S(1)}, f32[80,128]{1,0:T(8,128)S(1)}, u32[]{:S(2)}, u32[]{:S(2)}) collective-permute-start(f32[80,128]{1,0:T(8,128)S(1)} %get-tuple-element.194), channel_id=1, source_target_pairs={{0,3},{1,2},{2,1},{3,0},{4,7},{5,6},{6,5},{7,4},{8,11},{9,10},{10,... | collective-permute-start | bytes 122888 | tf_op jit(solution)/shard_map/ppermute | solution.py:33
  107.1 4.9 %collective-permute-start.23 = (f32[80,128]{1,0:T(8,128)S(1)}, f32[80,128]{1,0:T(8,128)S(1)}, u32[]{:S(2)}, u32[]{:S(2)}) collective-permute-start(f32[80,128]{1,0:T(8,128)S(1)} %get-tuple-element.195), channel_id=1, source_target_pairs={{0,2},{1,3},{2,0},{3,1},{4,6},{5,7},{6,4},{7,5},{8,10},{9,11},{10,... | collective-permute-start | bytes 122888 | tf_op jit(solution)/shard_map/ppermute | solution.py:33
  107.1 4.9 %collective-permute-start.22 = (f32[80,128]{1,0:T(8,128)S(1)}, f32[80,128]{1,0:T(8,128)S(1)}, u32[]{:S(2)}, u32[]{:S(2)}) collective-permute-start(f32[80,128]{1,0:T(8,128)S(1)} %get-tuple-element.196), channel_id=1, source_target_pairs={{0,1},{1,0},{2,3},{3,2},{4,5},{5,4},{6,7},{7,6},{8,9},{9,8},{10,11... | collective-permute-start | bytes 122888 | tf_op jit(solution)/shard_map/ppermute | solution.py:33
  112.0 5.9 %collective-permute-start.26 = (f32[80,128]{1,0:T(8,128)S(1)}, f32[80,128]{1,0:T(8,128)S(1)}, u32[]{:S(2)}, u32[]{:S(2)}) collective-permute-start(f32[80,128]{1,0:T(8,128)S(1)} %add_add_fusion.2), channel_id=1, source_target_pairs={{0,3},{1,2},{2,1},{3,0},{4,7},{5,6},{6,5},{7,4},{8,11},{9,10},{10,... | collective-permute-start | bytes 122888 | tf_op jit(solution)/shard_map/ppermute | solution.py:33
  114.5 5.0 %collective-permute-start.25 = (f32[80,128]{1,0:T(8,128)S(1)}, f32[80,128]{1,0:T(8,128)S(1)}, u32[]{:S(2)}, u32[]{:S(2)}) collective-permute-start(f32[80,128]{1,0:T(8,128)S(1)} %add_add_fusion.2), channel_id=1, source_target_pairs={{0,2},{1,3},{2,0},{3,1},{4,6},{5,7},{6,4},{7,5},{8,10},{9,11},{10,... | collective-permute-start | bytes 122888 | tf_op jit(solution)/shard_map/ppermute | solution.py:33
  114.5 5.0 %collective-permute-start.24 = (f32[80,128]{1,0:T(8,128)S(1)}, f32[80,128]{1,0:T(8,128)S(1)}, u32[]{:S(2)}, u32[]{:S(2)}) collective-permute-start(f32[80,128]{1,0:T(8,128)S(1)} %add_add_fusion.2), channel_id=1, source_target_pairs={{0,1},{1,0},{2,3},{3,2},{4,5},{5,4},{6,7},{7,6},{8,9},{9,8},{10,11... | collective-permute-start | bytes 122888 | tf_op jit(solution)/shard_map/ppermute | solution.py:33
  119.6 7.8 %collective-permute-start.30 = (f32[320,128]{1,0:T(8,128)S(1)}, f32[320,128]{1,0:T(8,128)S(1)}, u32[]{:S(2)}, u32[]{:S(2)}) collective-permute-start(f32[320,128]{1,0:T(8,128)S(1)} %pad_maximum_fusion.3), channel_id=1, source_target_pairs={{0,24},{1,25},{2,26},{3,27},{4,28},{5,29},{6,30},{7,31},{8,16},{9,... | collective-permute-start | bytes 491528 | tf_op jit(solution)/shard_map/ppermute | solution.py:33
  120.8 8.0 %collective-permute-start.29 = (f32[320,128]{1,0:T(8,128)S(1)}, f32[320,128]{1,0:T(8,128)S(1)}, u32[]{:S(2)}, u32[]{:S(2)}) collective-permute-start(f32[320,128]{1,0:T(8,128)S(1)} %pad_maximum_fusion.3), channel_id=1, source_target_pairs={{0,16},{1,17},{2,18},{3,19},{4,20},{5,21},{6,22},{7,23},{8,24},{9,... | collective-permute-start | bytes 491528 | tf_op jit(solution)/shard_map/ppermute | solution.py:33
  122.0 6.8 %collective-permute-start.28 = (f32[320,128]{1,0:T(8,128)S(1)}, f32[320,128]{1,0:T(8,128)S(1)}, u32[]{:S(2)}, u32[]{:S(2)}) collective-permute-start(f32[320,128]{1,0:T(8,128)S(1)} %pad_maximum_fusion.3), channel_id=1, source_target_pairs={{0,8},{1,9},{2,10},{3,11},{4,12},{5,13},{6,14},{7,15},{8,0},{9,1},... | collective-permute-start | bytes 491528 | tf_op jit(solution)/shard_map/ppermute | solution.py:33
  128.8 2.2 %collective-permute-start.31 = (f32[1280,128]{1,0:T(8,128)S(1)}, f32[1280,128]{1,0:T(8,128)S(1)}, u32[]{:S(2)}, u32[]{:S(2)}) collective-permute-start(f32[1280,128]{1,0:T(8,128)S(1)} %pad_maximum_fusion.1.packed), channel_id=1, source_target_pairs={{0,4},{1,5},{2,6},{3,7},{4,0},{5,1},{6,2},{7,3},{8,12},{9,13},{10,... | collective-permute-start | bytes 1966088 | tf_op jit(solution)/shard_map/ppermute | solution.py:33
  (6 other events, 51.7 us)

commit v4 on v3

--- a/solution.py
+++ b/solution.py
@@ -297,11 +297,12 @@
     square_of(square, matrix[ids_in[0]])
     loads[2].wait()
     put_split((xh, xl), source_in[...])
-    queries_into((qh, ql), square, (xh, xl), width)
     for load in loads[3:]:
         load.wait()
     body = target_in[...]
-    score_grad_into((sgh, sgl), scores, (qh, ql), split(pad_rows(body, qh.shape[0]).T), partners_in[0])
+    turned = split(pad_rows(body, qh.shape[0]).T)
+    queries_into((qh, ql), square, (xh, xl), width)
+    score_grad_into((sgh, sgl), scores, (qh, ql), turned, partners_in[0])
     target_into(target_out, (qh, ql), (sgh, sgl), body, state_in[0])
 
 

time: 133 us -> 132 us (level)
  no operation moved by 1% of the time
where the time goes in v4:
time: 132 us
  waiting for transfers between devices  52.2 us (40%)
  Pallas kernels  42.8 us (32%)
  starting transfers between devices  33.8 us (26%)
  local copies, waits for them, and re-layouts  1.73 us (1%)
    pallas_call x12, Pallas kernels, call(): pl.pallas_call(kernel, in_specs=args_in, out_specs=outs_in or [VMEM] * le...  42.8 us
    ppermute x28, waiting for transfers between devices, exchange(): return lax.ppermute(value, AXES, pairs)  37.1 us
    ppermute x28, starting transfers between devices, exchange(): return lax.ppermute(value, AXES, pairs)  32.6 us
    ppermute x4, waiting for transfers between devices, from_behind(): return lax.ppermute(value, axis, pairs)  15.1 us
  transfers between devices with their start and end apart: 32, of which 24 were waited for; matrix products, arithmetic and copies ran while one was open for 1% of the time, Pallas kernels for 15%

profile of v4, /device:TPU:0, one launch (start us, length us, event | category | flops | bytes accessed | tf_op | source)
XLA Modules:
  0.0 132.2 jit_solution(1509784140399784990)
XLA Ops:
  0.8 6.5 %opening.1 = (f32[408,512]{1,0:T(8,128)S(1)}, bf16[512,768]{1,0:T(8,128)(2,1)S(1)}, bf16[512,768]{1,0:T(8,128)(2,1)S(1)}) custom-call(s32[1]{0:T(128)} %bitcast.1.me, s32[4]{0:T(128)} %bitcast.9, s32[4,1,1,768]{3,2,1,0:T(1,128)} %partners.7, f32[2,400,400]{2,1,0:T(8,128)} %relations.8, f32[400,768]{1,0:T(8,128)} %bitcast.17, f32[400,512]{1,0:T(8,128)} %bitcast.19, ...), custom_call_target="tpu_custom_call" | custom-call | flops 2211840000 | tf_op jit(solution)/shard_map/opening/pallas_call | solution.py:400
  8.0 5.2 %second.2 = (f32[400,768]{1,0:T(8,128)S(1)}, f32[1,1,768]{2,1,0:T(1,128)S(1)}, f32[400,512]{1,0:T(8,128)S(1)}, bf16[512,768]{1,0:T(8,128)(2,1)S(1)}, bf16[512,76...) custom-call(s32[4]{0:T(128)S(1)} %bitcast.10, f32[2,400,400]{2,1,0:T(8,128)S(1)} %copy-done, ...), custom_call_target="tpu_custom_call" | custom-call | flops 2949120000 | tf_op jit(solution)/shard_map/second/pallas_call | solution.py:400
  13.2 7.8 %collective-permute-done.target = f32[408,512]{1,0:T(8,128)S(1)} collective-permute-done((f32[408,512]{1,0:T(8,128)S(1)}, f32[408,512]{1,0:T(8,128)S(1)}, u32[]{:S(2)}, u32[]{:S(2)}) %collective-permute-start) | collective-permute-done | bytes 835616 | tf_op jit(solution)/shard_map/ppermute | solution.py:27
  21.0 4.7 %third.2 = (f32[2560,128]{1,0:T(8,128)S(1)}, bf16[512,768]{1,0:T(8,128)(2,1)S(1)}, bf16[512,768]{1,0:T(8,128)(2,1)S(1)}, bf16[512,768]{1,0:T(8,128)(2,1)S(1)}, bf16[512,768]{1,0:T(8,128)(2,1)S(1)}) custom-call(s32[4]{0:T(128)S(1)} %bitcast.11, s32[1]{0:T(128)} %bitcast.1.me, s32[4,1,1,768]{3,2,1,0:T(1,128)S(1)} %copy-done.1, ...), custom_call_target="tpu_custom_call" | custom-call | flops 2211840000 | tf_op jit(solution)/shard_map/third/pallas_call | solution.py:400
  25.9 2.1 %collective-permute-done.1 = f32[1280,128]{1,0:T(8,128)S(1)} collective-permute-done((f32[1280,128]{1,0:T(8,128)S(1)}, f32[1280,128]{1,0:T(8,128)S(1)}, u32[]{:S(2)}, u32[]{:S(2)}) %collective-permute-start.1) | collective-permute-done | bytes 655392 | tf_op jit(solution)/shard_map/ppermute | solution.py:33
  28.1 2.4 %collective-permute-start.2 = (f32[320,128]{1,0:T(8,128)S(1)}, f32[320,128]{1,0:T(8,128)S(1)}, u32[]{:S(2)}, u32[]{:S(2)}) collective-permute-start(f32[320,128]{1,0:T(8,128)S(1)} %get-tuple-element.191), channel_id=1, source_target_pairs={{0,24},{1,25},{2,26},{3,27},{4,28},{5,29},{6,30},{7,31},{8,16},{9,... | collective-permute-start | bytes 491528 | tf_op jit(solution)/shard_map/ppermute | solution.py:33
  31.9 3.4 %fourth.2 = (f32[408,512]{1,0:T(8,128)S(1)}, f32[400,768]{1,0:T(8,128)S(1)}, f32[1,1,768]{2,1,0:T(1,128)S(1)}, bf16[512,768]{1,0:T(8,128)(2,1)S(1)}, bf16[512,768]{1,0:T(8,128)(2,1)S(1)}) custom-call(s32[4]{0:T(128)S(1)} %bitcast.12, f32[2,400,400]{2,1,0:T(8,128)S(1)} %copy-done, f32[400,768]{1,0:T(8,128)S(1)} %get-tuple-element.114.source, ...), custom_call_target="tpu_custom_call" | custom-call | flops 1474560000 | tf_op jit(solution)/shard_map/fourth/pallas_call | solution.py:400
  36.1 2.7 %collective-permute-done.4 = f32[320,128]{1,0:T(8,128)S(1)} collective-permute-done((f32[320,128]{1,0:T(8,128)S(1)}, f32[320,128]{1,0:T(8,128)S(1)}, u32[]{:S(2)}, u32[]{:S(2)}) %collective-permute-start.4) | collective-permute-done | bytes 163872 | tf_op jit(solution)/shard_map/ppermute | solution.py:33
  40.0 3.7 %collective-permute-start.5 = (f32[80,128]{1,0:T(8,128)S(1)}, f32[80,128]{1,0:T(8,128)S(1)}, u32[]{:S(2)}, u32[]{:S(2)}) collective-permute-start(f32[80,128]{1,0:T(8,128)S(1)} %get-tuple-element.197), channel_id=1, source_target_pairs={{0,3},{1,2},{2,1},{3,0},{4,7},{5,6},{6,5},{7,4},{8,11},{9,10},{10,... | collective-permute-start | bytes 122888 | tf_op jit(solution)/shard_map/ppermute | solution.py:33
  44.4 1.7 %collective-permute-done.5 = f32[80,128]{1,0:T(8,128)S(1)} collective-permute-done((f32[80,128]{1,0:T(8,128)S(1)}, f32[80,128]{1,0:T(8,128)S(1)}, u32[]{:S(2)}, u32[]{:S(2)}) %collective-permute-start.5) | collective-permute-done | bytes 40992 | tf_op jit(solution)/shard_map/ppermute | solution.py:33
  46.1 2.5 %collective-permute-done.7 = f32[80,128]{1,0:T(8,128)S(1)} collective-permute-done((f32[80,128]{1,0:T(8,128)S(1)}, f32[80,128]{1,0:T(8,128)S(1)}, u32[]{:S(2)}, u32[]{:S(2)}) %collective-permute-start.7) | collective-permute-done | bytes 40992 | tf_op jit(solution)/shard_map/ppermute | solution.py:33
  48.6 2.0 %collective-permute-start.10 = (f32[80,128]{1,0:T(8,128)S(1)}, f32[80,128]{1,0:T(8,128)S(1)}, u32[]{:S(2)}, u32[]{:S(2)}) collective-permute-start(f32[80,128]{1,0:T(8,128)S(1)} %add_add_fusion.3), channel_id=1, source_target_pairs={{0,3},{1,2},{2,1},{3,0},{4,7},{5,6},{6,5},{7,4},{8,11},{9,10},{10,... | collective-permute-start | bytes 122888 | tf_op jit(solution)/shard_map/ppermute | solution.py:33
  51.1 1.9 %collective-permute-start.8 = (f32[80,128]{1,0:T(8,128)S(1)}, f32[80,128]{1,0:T(8,128)S(1)}, u32[]{:S(2)}, u32[]{:S(2)}) collective-permute-start(f32[80,128]{1,0:T(8,128)S(1)} %add_add_fusion.3), channel_id=1, source_target_pairs={{0,1},{1,0},{2,3},{3,2},{4,5},{5,4},{6,7},{7,6},{8,9},{9,8},{10,11... | collective-permute-start | bytes 122888 | tf_op jit(solution)/shard_map/ppermute | solution.py:33
  55.9 2.0 %collective-permute-start.14 = (f32[320,128]{1,0:T(8,128)S(1)}, f32[320,128]{1,0:T(8,128)S(1)}, u32[]{:S(2)}, u32[]{:S(2)}) collective-permute-start(f32[320,128]{1,0:T(8,128)S(1)} %pad_maximum_fusion.2), channel_id=1, source_target_pairs={{0,24},{1,25},{2,26},{3,27},{4,28},{5,29},{6,30},{7,31},{8,16},{9,... | collective-permute-start | bytes 491528 | tf_op jit(solution)/shard_map/ppermute | solution.py:33
  59.8 3.9 %collective-permute-done.14 = f32[320,128]{1,0:T(8,128)S(1)} collective-permute-done((f32[320,128]{1,0:T(8,128)S(1)}, f32[320,128]{1,0:T(8,128)S(1)}, u32[]{:S(2)}, u32[]{:S(2)}) %collective-permute-start.14) | collective-permute-done | bytes 163872 | tf_op jit(solution)/shard_map/ppermute | solution.py:33
  63.7 1.5 %collective-permute-done.13 = f32[320,128]{1,0:T(8,128)S(1)} collective-permute-done((f32[320,128]{1,0:T(8,128)S(1)}, f32[320,128]{1,0:T(8,128)S(1)}, u32[]{:S(2)}, u32[]{:S(2)}) %collective-permute-start.13) | collective-permute-done | bytes 163872 | tf_op jit(solution)/shard_map/ppermute | solution.py:33
  65.8 1.8 %collective-permute-done.15.packed = f32[1280,128]{1,0:T(8,128)S(1)} collective-permute-done((f32[1280,128]{1,0:T(8,128)S(1)}, f32[1280,128]{1,0:T(8,128)S(1)}, u32[]{:S(2)}, u32[]{:S(2)}) %collective-permute-start.15) | collective-permute-done | bytes 655392 | tf_op jit(solution)/shard_map/ppermute | solution.py:33
  67.6 5.2 %first.1 = (f32[2,400,400]{2,1,0:T(8,128)S(1)}, f32[2,400,400]{2,1,0:T(8,128)S(1)}, f32[408,512]{1,0:T(8,128)S(1)}, bf16[512,768]{1,0:T(8,128)(2,1)S(1)}, bf16[512,768]{1,0:T(8,128)(2,1)S(1)}) custom-call(s32[4]{0:T(128)S(1)} %bitcast.13, s32[1]{0:T(128)} %bitcast.1.me, ...), custom_call_target="tpu_custom_call", output_to_operand_aliasing={{0}: (5, {}), {1}: (6, {})} | custom-call | flops 2211840000 | tf_op jit(solution)/shard_map/first/pallas_call | solution.py:400
  73.0 5.4 %second.3 = (f32[400,768]{1,0:T(8,128)S(1)}, f32[1,1,768]{2,1,0:T(1,128)S(1)}, f32[400,512]{1,0:T(8,128)S(1)}, bf16[512,768]{1,0:T(8,128)(2,1)S(1)}, bf16[512,76...) custom-call(s32[4]{0:T(128)S(1)} %bitcast.14, ...), custom_call_target="tpu_custom_call" | custom-call | flops 2949120000 | tf_op jit(solution)/shard_map/second/pallas_call | solution.py:400
  78.4 7.3 %collective-permute-done.16.target = f32[408,512]{1,0:T(8,128)S(1)} collective-permute-done((f32[408,512]{1,0:T(8,128)S(1)}, f32[408,512]{1,0:T(8,128)S(1)}, u32[]{:S(2)}, u32[]{:S(2)}) %collective-permute-start.16) | collective-permute-done | bytes 835616 | tf_op jit(solution)/shard_map/ppermute | solution.py:27
  85.7 4.7 %third.3 = (f32[2560,128]{1,0:T(8,128)S(1)}, bf16[512,768]{1,0:T(8,128)(2,1)S(1)}, bf16[512,768]{1,0:T(8,128)(2,1)S(1)}, bf16[512,768]{1,0:T(8,128)(2,1)S(1)}, bf16[512,768]{1,0:T(8,128)(2,1)S(1)}) custom-call(s32[4]{0:T(128)S(1)} %bitcast.15, s32[1]{0:T(128)} %bitcast.1.me, s32[4,1,1,768]{3,2,1,0:T(1,128)S(1)} %copy-done.1, ...), custom_call_target="tpu_custom_call" | custom-call | flops 2211840000 | tf_op jit(solution)/shard_map/third/pallas_call | solution.py:400
  90.5 2.1 %collective-permute-done.17 = f32[1280,128]{1,0:T(8,128)S(1)} collective-permute-done((f32[1280,128]{1,0:T(8,128)S(1)}, f32[1280,128]{1,0:T(8,128)S(1)}, u32[]{:S(2)}, u32[]{:S(2)}) %collective-permute-start.17) | collective-permute-done | bytes 655392 | tf_op jit(solution)/shard_map/ppermute | solution.py:33
  96.3 4.1 %fourth.3 = (f32[408,512]{1,0:T(8,128)S(1)}, f32[400,768]{1,0:T(8,128)}, f32[1,1,768]{2,1,0:T(1,128)}) custom-call(s32[4]{0:T(128)S(1)} %bitcast.16, f32[2,400,400]{2,1,0:T(8,128)S(1)} %get-tuple-element.161.relations, f32[400,768]{1,0:T(8,128)S(1)} %get-tuple-element.162.source, f32[1,1,768]{2,1,0:T(1,128)S(1)} %get-tuple-element.163.source_state, ...), custom_call_target="tpu_custom_call" | custom-call | flops 1474560000 | tf_op jit(solution)/shard_map/fourth/pallas_call | solution.py:400
  100.8 2.6 %collective-permute-done.20 = f32[320,128]{1,0:T(8,128)S(1)} collective-permute-done((f32[320,128]{1,0:T(8,128)S(1)}, f32[320,128]{1,0:T(8,128)S(1)}, u32[]{:S(2)}, u32[]{:S(2)}) %collective-permute-start.20) | collective-permute-done | bytes 163872 | tf_op jit(solution)/shard_map/ppermute | solution.py:33
  103.5 3.1 %collective-permute-start.21 = (f32[80,128]{1,0:T(8,128)S(1)}, f32[80,128]{1,0:T(8,128)S(1)}, u32[]{:S(2)}, u32[]{:S(2)}) collective-permute-start(f32[80,128]{1,0:T(8,128)S(1)} %get-tuple-element.194), channel_id=1, source_target_pairs={{0,3},{1,2},{2,1},{3,0},{4,7},{5,6},{6,5},{7,4},{8,11},{9,10},{10,... | collective-permute-start | bytes 122888 | tf_op jit(solution)/shard_map/ppermute | solution.py:33
  108.0 1.9 %collective-permute-done.21 = f32[80,128]{1,0:T(8,128)S(1)} collective-permute-done((f32[80,128]{1,0:T(8,128)S(1)}, f32[80,128]{1,0:T(8,128)S(1)}, u32[]{:S(2)}, u32[]{:S(2)}) %collective-permute-start.21) | collective-permute-done | bytes 40992 | tf_op jit(solution)/shard_map/ppermute | solution.py:33
  109.9 1.7 %collective-permute-done.23 = f32[80,128]{1,0:T(8,128)S(1)} collective-permute-done((f32[80,128]{1,0:T(8,128)S(1)}, f32[80,128]{1,0:T(8,128)S(1)}, u32[]{:S(2)}, u32[]{:S(2)}) %collective-permute-start.23) | collective-permute-done | bytes 40992 | tf_op jit(solution)/shard_map/ppermute | solution.py:33
  111.5 2.5 %collective-permute-start.26 = (f32[80,128]{1,0:T(8,128)S(1)}, f32[80,128]{1,0:T(8,128)S(1)}, u32[]{:S(2)}, u32[]{:S(2)}) collective-permute-start(f32[80,128]{1,0:T(8,128)S(1)} %add_add_fusion.2), channel_id=1, source_target_pairs={{0,3},{1,2},{2,1},{3,0},{4,7},{5,6},{6,5},{7,4},{8,11},{9,10},{10,... | collective-permute-start | bytes 122888 | tf_op jit(solution)/shard_map/ppermute | solution.py:33
  114.0 1.9 %collective-permute-start.24 = (f32[80,128]{1,0:T(8,128)S(1)}, f32[80,128]{1,0:T(8,128)S(1)}, u32[]{:S(2)}, u32[]{:S(2)}) collective-permute-start(f32[80,128]{1,0:T(8,128)S(1)} %add_add_fusion.2), channel_id=1, source_target_pairs={{0,1},{1,0},{2,3},{3,2},{4,5},{5,4},{6,7},{7,6},{8,9},{9,8},{10,11... | collective-permute-start | bytes 122888 | tf_op jit(solution)/shard_map/ppermute | solution.py:33
  117.4 1.7 %collective-permute-done.25 = f32[80,128]{1,0:T(8,128)S(1)} collective-permute-done((f32[80,128]{1,0:T(8,128)S(1)}, f32[80,128]{1,0:T(8,128)S(1)}, u32[]{:S(2)}, u32[]{:S(2)}) %collective-permute-start.25) | collective-permute-done | bytes 40992 | tf_op jit(solution)/shard_map/ppermute | solution.py:33
  124.2 2.8 %collective-permute-done.30 = f32[320,128]{1,0:T(8,128)S(1)} collective-permute-done((f32[320,128]{1,0:T(8,128)S(1)}, f32[320,128]{1,0:T(8,128)S(1)}, u32[]{:S(2)}, u32[]{:S(2)}) %collective-permute-start.30) | collective-permute-done | bytes 163872 | tf_op jit(solution)/shard_map/ppermute | solution.py:33
  128.4 1.5 %closing.2 = (f32[2,2,400,400]{3,2,1,0:T(8,128)}, f32[2,400,400]{2,1,0:T(8,128)}) custom-call(s32[1]{0:T(128)} %bitcast.1.me, f32[1280,128]{1,0:T(8,128)S(1)} %pad_maximum_fusion.1.packed, f32[2,400,400]{2,1,0:T(8,128)S(1)} %get-tuple-element.161.relations, f32[2,2,400,400]{3,2,1,0:T(8,128)} %get-tuple-element.183.refs_0_), custom_call_target="tpu_custom_call", output_to_operand_aliasing={{0}: (3, {})} | custom-call | flops 184320000 | tf_op jit(solution)/shard_map/closing/pallas_call | solution.py:400
  (74 shorter events, 27.0 us)
Async XLA Ops:
  7.3 13.8 %collective-permute-start = (f32[408,512]{1,0:T(8,128)S(1)}, f32[408,512]{1,0:T(8,128)S(1)}, u32[]{:S(2)}, u32[]{:S(2)}) collective-permute-start(f32[408,512]{1,0:T(8,128)S(1)} %get-tuple-element.101), channel_id=1, source_target_pairs={{0,4},{4,8},{8,12},{12,16},{16,20},{20,24},{24,28},{28,0},{1,5},{5... | collective-permute-start | bytes 2506760 | tf_op jit(solution)/shard_map/ppermute | solution.py:27
  25.8 2.2 %collective-permute-start.1 = (f32[1280,128]{1,0:T(8,128)S(1)}, f32[1280,128]{1,0:T(8,128)S(1)}, u32[]{:S(2)}, u32[]{:S(2)}) collective-permute-start(f32[1280,128]{1,0:T(8,128)S(1)} %slice.87), channel_id=1, source_target_pairs={{0,4},{1,5},{2,6},{3,7},{4,0},{5,1},{6,2},{7,3},{8,12},{9,13},{10,... | collective-permute-start | bytes 1966088 | tf_op jit(solution)/shard_map/ppermute | solution.py:33
  28.1 8.0 %collective-permute-start.2 = (f32[320,128]{1,0:T(8,128)S(1)}, f32[320,128]{1,0:T(8,128)S(1)}, u32[]{:S(2)}, u32[]{:S(2)}) collective-permute-start(f32[320,128]{1,0:T(8,128)S(1)} %get-tuple-element.191), channel_id=1, source_target_pairs={{0,24},{1,25},{2,26},{3,27},{4,28},{5,29},{6,30},{7,31},{8,16},{9,... | collective-permute-start | bytes 491528 | tf_op jit(solution)/shard_map/ppermute | solution.py:33
  30.4 8.4 %collective-permute-start.4 = (f32[320,128]{1,0:T(8,128)S(1)}, f32[320,128]{1,0:T(8,128)S(1)}, u32[]{:S(2)}, u32[]{:S(2)}) collective-permute-start(f32[320,128]{1,0:T(8,128)S(1)} %get-tuple-element.192), channel_id=1, source_target_pairs={{0,16},{1,17},{2,18},{3,19},{4,20},{5,21},{6,22},{7,23},{8,24},{9,... | collective-permute-start | bytes 491528 | tf_op jit(solution)/shard_map/ppermute | solution.py:33
  30.9 8.7 %collective-permute-start.3 = (f32[320,128]{1,0:T(8,128)S(1)}, f32[320,128]{1,0:T(8,128)S(1)}, u32[]{:S(2)}, u32[]{:S(2)}) collective-permute-start(f32[320,128]{1,0:T(8,128)S(1)} %get-tuple-element.193), channel_id=1, source_target_pairs={{0,8},{1,9},{2,10},{3,11},{4,12},{5,13},{6,14},{7,15},{8,0},{9,1},... | collective-permute-start | bytes 491528 | tf_op jit(solution)/shard_map/ppermute | solution.py:33
  39.7 16.2 %collective-permute-start.11 = (f32[408,512]{1,0:T(8,128)S(1)}, f32[408,512]{1,0:T(8,128)S(1)}, u32[]{:S(2)}, u32[]{:S(2)}) collective-permute-start(f32[408,512]{1,0:T(8,128)S(1)} %get-tuple-element.125), channel_id=1, source_target_pairs={{0,4},{4,8},{8,12},{12,16},{16,20},{20,24},{24,28},{28,0},{1,5},{5... | collective-permute-start | bytes 2506760 | tf_op jit(solution)/shard_map/ppermute | solution.py:27
  40.0 6.1 %collective-permute-start.5 = (f32[80,128]{1,0:T(8,128)S(1)}, f32[80,128]{1,0:T(8,128)S(1)}, u32[]{:S(2)}, u32[]{:S(2)}) collective-permute-start(f32[80,128]{1,0:T(8,128)S(1)} %get-tuple-element.197), channel_id=1, source_target_pairs={{0,3},{1,2},{2,1},{3,0},{4,7},{5,6},{6,5},{7,4},{8,11},{9,10},{10,... | collective-permute-start | bytes 122888 | tf_op jit(solution)/shard_map/ppermute | solution.py:33
  43.7 4.9 %collective-permute-start.7 = (f32[80,128]{1,0:T(8,128)S(1)}, f32[80,128]{1,0:T(8,128)S(1)}, u32[]{:S(2)}, u32[]{:S(2)}) collective-permute-start(f32[80,128]{1,0:T(8,128)S(1)} %get-tuple-element.198), channel_id=1, source_target_pairs={{0,2},{1,3},{2,0},{3,1},{4,6},{5,7},{6,4},{7,5},{8,10},{9,11},{10,... | collective-permute-start | bytes 122888 | tf_op jit(solution)/shard_map/ppermute | solution.py:33
  43.7 4.9 %collective-permute-start.6 = (f32[80,128]{1,0:T(8,128)S(1)}, f32[80,128]{1,0:T(8,128)S(1)}, u32[]{:S(2)}, u32[]{:S(2)}) collective-permute-start(f32[80,128]{1,0:T(8,128)S(1)} %get-tuple-element.199), channel_id=1, source_target_pairs={{0,1},{1,0},{2,3},{3,2},{4,5},{5,4},{6,7},{7,6},{8,9},{9,8},{10,11... | collective-permute-start | bytes 122888 | tf_op jit(solution)/shard_map/ppermute | solution.py:33
  48.6 5.9 %collective-permute-start.10 = (f32[80,128]{1,0:T(8,128)S(1)}, f32[80,128]{1,0:T(8,128)S(1)}, u32[]{:S(2)}, u32[]{:S(2)}) collective-permute-start(f32[80,128]{1,0:T(8,128)S(1)} %add_add_fusion.3), channel_id=1, source_target_pairs={{0,3},{1,2},{2,1},{3,0},{4,7},{5,6},{6,5},{7,4},{8,11},{9,10},{10,... | collective-permute-start | bytes 122888 | tf_op jit(solution)/shard_map/ppermute | solution.py:33
  50.6 5.2 %collective-permute-start.9 = (f32[80,128]{1,0:T(8,128)S(1)}, f32[80,128]{1,0:T(8,128)S(1)}, u32[]{:S(2)}, u32[]{:S(2)}) collective-permute-start(f32[80,128]{1,0:T(8,128)S(1)} %add_add_fusion.3), channel_id=1, source_target_pairs={{0,2},{1,3},{2,0},{3,1},{4,6},{5,7},{6,4},{7,5},{8,10},{9,11},{10,... | collective-permute-start | bytes 122888 | tf_op jit(solution)/shard_map/ppermute | solution.py:33
  51.1 4.8 %collective-permute-start.8 = (f32[80,128]{1,0:T(8,128)S(1)}, f32[80,128]{1,0:T(8,128)S(1)}, u32[]{:S(2)}, u32[]{:S(2)}) collective-permute-start(f32[80,128]{1,0:T(8,128)S(1)} %add_add_fusion.3), channel_id=1, source_target_pairs={{0,1},{1,0},{2,3},{3,2},{4,5},{5,4},{6,7},{7,6},{8,9},{9,8},{10,11... | collective-permute-start | bytes 122888 | tf_op jit(solution)/shard_map/ppermute | solution.py:33
  55.9 7.8 %collective-permute-start.14 = (f32[320,128]{1,0:T(8,128)S(1)}, f32[320,128]{1,0:T(8,128)S(1)}, u32[]{:S(2)}, u32[]{:S(2)}) collective-permute-start(f32[320,128]{1,0:T(8,128)S(1)} %pad_maximum_fusion.2), channel_id=1, source_target_pairs={{0,24},{1,25},{2,26},{3,27},{4,28},{5,29},{6,30},{7,31},{8,16},{9,... | collective-permute-start | bytes 491528 | tf_op jit(solution)/shard_map/ppermute | solution.py:33
  57.9 7.4 %collective-permute-start.13 = (f32[320,128]{1,0:T(8,128)S(1)}, f32[320,128]{1,0:T(8,128)S(1)}, u32[]{:S(2)}, u32[]{:S(2)}) collective-permute-start(f32[320,128]{1,0:T(8,128)S(1)} %pad_maximum_fusion.2), channel_id=1, source_target_pairs={{0,16},{1,17},{2,18},{3,19},{4,20},{5,21},{6,22},{7,23},{8,24},{9,... | collective-permute-start | bytes 491528 | tf_op jit(solution)/shard_map/ppermute | solution.py:33
  58.4 7.0 %collective-permute-start.12 = (f32[320,128]{1,0:T(8,128)S(1)}, f32[320,128]{1,0:T(8,128)S(1)}, u32[]{:S(2)}, u32[]{:S(2)}) collective-permute-start(f32[320,128]{1,0:T(8,128)S(1)} %pad_maximum_fusion.2), channel_id=1, source_target_pairs={{0,8},{1,9},{2,10},{3,11},{4,12},{5,13},{6,14},{7,15},{8,0},{9,1},... | collective-permute-start | bytes 491528 | tf_op jit(solution)/shard_map/ppermute | solution.py:33
  65.4 2.2 %collective-permute-start.15 = (f32[1280,128]{1,0:T(8,128)S(1)}, f32[1280,128]{1,0:T(8,128)S(1)}, u32[]{:S(2)}, u32[]{:S(2)}) collective-permute-start(f32[1280,128]{1,0:T(8,128)S(1)} %pad_maximum_fusion.packed), channel_id=1, source_target_pairs={{0,4},{1,5},{2,6},{3,7},{4,0},{5,1},{6,2},{7,3},{8,12},{9,13},{10,... | collective-permute-start | bytes 1966088 | tf_op jit(solution)/shard_map/ppermute | solution.py:33
  72.8 12.9 %collective-permute-start.16 = (f32[408,512]{1,0:T(8,128)S(1)}, f32[408,512]{1,0:T(8,128)S(1)}, u32[]{:S(2)}, u32[]{:S(2)}) collective-permute-start(f32[408,512]{1,0:T(8,128)S(1)} %get-tuple-element.149), channel_id=1, source_target_pairs={{0,4},{4,8},{8,12},{12,16},{16,20},{20,24},{24,28},{28,0},{1,5},{5... | collective-permute-start | bytes 2506760 | tf_op jit(solution)/shard_map/ppermute | solution.py:27
  90.4 2.2 %collective-permute-start.17 = (f32[1280,128]{1,0:T(8,128)S(1)}, f32[1280,128]{1,0:T(8,128)S(1)}, u32[]{:S(2)}, u32[]{:S(2)}) collective-permute-start(f32[1280,128]{1,0:T(8,128)S(1)} %slice.97), channel_id=1, source_target_pairs={{0,4},{1,5},{2,6},{3,7},{4,0},{5,1},{6,2},{7,3},{8,12},{9,13},{10,... | collective-permute-start | bytes 1966088 | tf_op jit(solution)/shard_map/ppermute | solution.py:33
  92.7 8.1 %collective-permute-start.18 = (f32[320,128]{1,0:T(8,128)S(1)}, f32[320,128]{1,0:T(8,128)S(1)}, u32[]{:S(2)}, u32[]{:S(2)}) collective-permute-start(f32[320,128]{1,0:T(8,128)S(1)} %get-tuple-element.188), channel_id=1, source_target_pairs={{0,24},{1,25},{2,26},{3,27},{4,28},{5,29},{6,30},{7,31},{8,16},{9,... | collective-permute-start | bytes 491528 | tf_op jit(solution)/shard_map/ppermute | solution.py:33
  94.1 9.3 %collective-permute-start.20 = (f32[320,128]{1,0:T(8,128)S(1)}, f32[320,128]{1,0:T(8,128)S(1)}, u32[]{:S(2)}, u32[]{:S(2)}) collective-permute-start(f32[320,128]{1,0:T(8,128)S(1)} %get-tuple-element.189), channel_id=1, source_target_pairs={{0,16},{1,17},{2,18},{3,19},{4,20},{5,21},{6,22},{7,23},{8,24},{9,... | collective-permute-start | bytes 491528 | tf_op jit(solution)/shard_map/ppermute | solution.py:33
  94.8 8.6 %collective-permute-start.19 = (f32[320,128]{1,0:T(8,128)S(1)}, f32[320,128]{1,0:T(8,128)S(1)}, u32[]{:S(2)}, u32[]{:S(2)}) collective-permute-start(f32[320,128]{1,0:T(8,128)S(1)} %get-tuple-element.190), channel_id=1, source_target_pairs={{0,8},{1,9},{2,10},{3,11},{4,12},{5,13},{6,14},{7,15},{8,0},{9,1},... | collective-permute-start | bytes 491528 | tf_op jit(solution)/shard_map/ppermute | solution.py:33
  103.5 15.7 %collective-permute-start.27 = (f32[408,512]{1,0:T(8,128)S(1)}, f32[408,512]{1,0:T(8,128)S(1)}, u32[]{:S(2)}, u32[]{:S(2)}) collective-permute-start(f32[408,512]{1,0:T(8,128)S(1)} %get-tuple-element.173), channel_id=1, source_target_pairs={{0,4},{4,8},{8,12},{12,16},{16,20},{20,24},{24,28},{28,0},{1,5},{5... | collective-permute-start | bytes 2506760 | tf_op jit(solution)/shard_map/ppermute | solution.py:27
  103.5 6.3 %collective-permute-start.21 = (f32[80,128]{1,0:T(8,128)S(1)}, f32[80,128]{1,0:T(8,128)S(1)}, u32[]{:S(2)}, u32[]{:S(2)}) collective-permute-start(f32[80,128]{1,0:T(8,128)S(1)} %get-tuple-element.194), channel_id=1, source_target_pairs={{0,3},{1,2},{2,1},{3,0},{4,7},{5,6},{6,5},{7,4},{8,11},{9,10},{10,... | collective-permute-start | bytes 122888 | tf_op jit(solution)/shard_map/ppermute | solution.py:33
  106.6 4.9 %collective-permute-start.23 = (f32[80,128]{1,0:T(8,128)S(1)}, f32[80,128]{1,0:T(8,128)S(1)}, u32[]{:S(2)}, u32[]{:S(2)}) collective-permute-start(f32[80,128]{1,0:T(8,128)S(1)} %get-tuple-element.195), channel_id=1, source_target_pairs={{0,2},{1,3},{2,0},{3,1},{4,6},{5,7},{6,4},{7,5},{8,10},{9,11},{10,... | collective-permute-start | bytes 122888 | tf_op jit(solution)/shard_map/ppermute | solution.py:33
  106.6 4.9 %collective-permute-start.22 = (f32[80,128]{1,0:T(8,128)S(1)}, f32[80,128]{1,0:T(8,128)S(1)}, u32[]{:S(2)}, u32[]{:S(2)}) collective-permute-start(f32[80,128]{1,0:T(8,128)S(1)} %get-tuple-element.196), channel_id=1, source_target_pairs={{0,1},{1,0},{2,3},{3,2},{4,5},{5,4},{6,7},{7,6},{8,9},{9,8},{10,11... | collective-permute-start | bytes 122888 | tf_op jit(solution)/shard_map/ppermute | solution.py:33
  111.5 5.9 %collective-permute-start.26 = (f32[80,128]{1,0:T(8,128)S(1)}, f32[80,128]{1,0:T(8,128)S(1)}, u32[]{:S(2)}, u32[]{:S(2)}) collective-permute-start(f32[80,128]{1,0:T(8,128)S(1)} %add_add_fusion.2), channel_id=1, source_target_pairs={{0,3},{1,2},{2,1},{3,0},{4,7},{5,6},{6,5},{7,4},{8,11},{9,10},{10,... | collective-permute-start | bytes 122888 | tf_op jit(solution)/shard_map/ppermute | solution.py:33
  114.0 5.1 %collective-permute-start.25 = (f32[80,128]{1,0:T(8,128)S(1)}, f32[80,128]{1,0:T(8,128)S(1)}, u32[]{:S(2)}, u32[]{:S(2)}) collective-permute-start(f32[80,128]{1,0:T(8,128)S(1)} %add_add_fusion.2), channel_id=1, source_target_pairs={{0,2},{1,3},{2,0},{3,1},{4,6},{5,7},{6,4},{7,5},{8,10},{9,11},{10,... | collective-permute-start | bytes 122888 | tf_op jit(solution)/shard_map/ppermute | solution.py:33
  114.0 5.1 %collective-permute-start.24 = (f32[80,128]{1,0:T(8,128)S(1)}, f32[80,128]{1,0:T(8,128)S(1)}, u32[]{:S(2)}, u32[]{:S(2)}) collective-permute-start(f32[80,128]{1,0:T(8,128)S(1)} %add_add_fusion.2), channel_id=1, source_target_pairs={{0,1},{1,0},{2,3},{3,2},{4,5},{5,4},{6,7},{7,6},{8,9},{9,8},{10,11... | collective-permute-start | bytes 122888 | tf_op jit(solution)/shard_map/ppermute | solution.py:33
  119.1 7.8 %collective-permute-start.30 = (f32[320,128]{1,0:T(8,128)S(1)}, f32[320,128]{1,0:T(8,128)S(1)}, u32[]{:S(2)}, u32[]{:S(2)}) collective-permute-start(f32[320,128]{1,0:T(8,128)S(1)} %pad_maximum_fusion.3), channel_id=1, source_target_pairs={{0,24},{1,25},{2,26},{3,27},{4,28},{5,29},{6,30},{7,31},{8,16},{9,... | collective-permute-start | bytes 491528 | tf_op jit(solution)/shard_map/ppermute | solution.py:33
  120.3 8.0 %collective-permute-start.29 = (f32[320,128]{1,0:T(8,128)S(1)}, f32[320,128]{1,0:T(8,128)S(1)}, u32[]{:S(2)}, u32[]{:S(2)}) collective-permute-start(f32[320,128]{1,0:T(8,128)S(1)} %pad_maximum_fusion.3), channel_id=1, source_target_pairs={{0,16},{1,17},{2,18},{3,19},{4,20},{5,21},{6,22},{7,23},{8,24},{9,... | collective-permute-start | bytes 491528 | tf_op jit(solution)/shard_map/ppermute | solution.py:33
  121.5 6.8 %collective-permute-start.28 = (f32[320,128]{1,0:T(8,128)S(1)}, f32[320,128]{1,0:T(8,128)S(1)}, u32[]{:S(2)}, u32[]{:S(2)}) collective-permute-start(f32[320,128]{1,0:T(8,128)S(1)} %pad_maximum_fusion.3), channel_id=1, source_target_pairs={{0,8},{1,9},{2,10},{3,11},{4,12},{5,13},{6,14},{7,15},{8,0},{9,1},... | collective-permute-start | bytes 491528 | tf_op jit(solution)/shard_map/ppermute | solution.py:33
  128.3 2.2 %collective-permute-start.31 = (f32[1280,128]{1,0:T(8,128)S(1)}, f32[1280,128]{1,0:T(8,128)S(1)}, u32[]{:S(2)}, u32[]{:S(2)}) collective-permute-start(f32[1280,128]{1,0:T(8,128)S(1)} %pad_maximum_fusion.1.packed), channel_id=1, source_target_pairs={{0,4},{1,5},{2,6},{3,7},{4,0},{5,1},{6,2},{7,3},{8,12},{9,13},{10,... | collective-permute-start | bytes 1966088 | tf_op jit(solution)/shard_map/ppermute | solution.py:33
  (6 other events, 49.2 us)

commit v5 on v4

--- a/solution.py
+++ b/solution.py
@@ -168,8 +168,12 @@
             refs[0][rows:, part], refs[1][rows:, part] = blank, blank
 
 
-def queries_into(q_refs, square_ref, x_refs, width):
-    turned = split(square_ref[...].T[:width])
+def turned_halves(square_ref, width):
+    return split(square_ref[...].T[:width])
+
+
+def queries_into(q_refs, square_ref, x_refs, width, turned=None):
+    turned = turned_halves(square_ref, width) if turned is None else turned
     split_columns(q_refs, lambda part: dot3(*turned, *columns_of(x_refs, part), NN))
 
 
@@ -295,13 +299,14 @@
     loads[0].wait()
     loads[1].wait()
     square_of(square, matrix[ids_in[0]])
+    halves = turned_halves(square, width)
     loads[2].wait()
     put_split((xh, xl), source_in[...])
     for load in loads[3:]:
         load.wait()
     body = target_in[...]
     turned = split(pad_rows(body, qh.shape[0]).T)
-    queries_into((qh, ql), square, (xh, xl), width)
+    queries_into((qh, ql), square, (xh, xl), width, halves)
     score_grad_into((sgh, sgl), scores, (qh, ql), turned, partners_in[0])
     target_into(target_out, (qh, ql), (sgh, sgl), body, state_in[0])
 

time: 132 us -> 132 us (level)
  no operation moved by 1% of the time
where the time goes in v5:
time: 132 us
  waiting for transfers between devices  52.2 us (40%)
  Pallas kernels  42.7 us (32%)
  starting transfers between devices  33.8 us (26%)
  local copies, waits for them, and re-layouts  1.73 us (1%)
    pallas_call x12, Pallas kernels, call(): pl.pallas_call(kernel, in_specs=args_in, out_specs=outs_in or [VMEM] * le...  42.7 us
    ppermute x28, waiting for transfers between devices, exchange(): return lax.ppermute(value, AXES, pairs)  37.1 us
    ppermute x28, starting transfers between devices, exchange(): return lax.ppermute(value, AXES, pairs)  32.6 us
    ppermute x4, waiting for transfers between devices, from_behind(): return lax.ppermute(value, axis, pairs)  15.1 us
  transfers between devices with their start and end apart: 32, of which 24 were waited for; matrix products, arithmetic and copies ran while one was open for 1% of the time, Pallas kernels for 15%

profile of v5, /device:TPU:0, one launch (start us, length us, event | category | flops | bytes accessed | tf_op | source)
XLA Modules:
  0.0 132.1 jit_solution(4447998655764488332)
XLA Ops:
  0.8 6.4 %opening.1 = (f32[408,512]{1,0:T(8,128)S(1)}, bf16[512,768]{1,0:T(8,128)(2,1)S(1)}, bf16[512,768]{1,0:T(8,128)(2,1)S(1)}) custom-call(s32[1]{0:T(128)} %bitcast.1.me, s32[4]{0:T(128)} %bitcast.9, s32[4,1,1,768]{3,2,1,0:T(1,128)} %partners.7, f32[2,400,400]{2,1,0:T(8,128)} %relations.8, f32[400,768]{1,0:T(8,128)} %bitcast.17, f32[400,512]{1,0:T(8,128)} %bitcast.19, ...), custom_call_target="tpu_custom_call" | custom-call | flops 2211840000 | tf_op jit(solution)/shard_map/opening/pallas_call | solution.py:405
  7.9 5.2 %second.2 = (f32[400,768]{1,0:T(8,128)S(1)}, f32[1,1,768]{2,1,0:T(1,128)S(1)}, f32[400,512]{1,0:T(8,128)S(1)}, bf16[512,768]{1,0:T(8,128)(2,1)S(1)}, bf16[512,76...) custom-call(s32[4]{0:T(128)S(1)} %bitcast.10, f32[2,400,400]{2,1,0:T(8,128)S(1)} %copy-done, ...), custom_call_target="tpu_custom_call" | custom-call | flops 2949120000 | tf_op jit(solution)/shard_map/second/pallas_call | solution.py:405
  13.1 7.8 %collective-permute-done.target = f32[408,512]{1,0:T(8,128)S(1)} collective-permute-done((f32[408,512]{1,0:T(8,128)S(1)}, f32[408,512]{1,0:T(8,128)S(1)}, u32[]{:S(2)}, u32[]{:S(2)}) %collective-permute-start) | collective-permute-done | bytes 835616 | tf_op jit(solution)/shard_map/ppermute | solution.py:27
  20.9 4.7 %third.2 = (f32[2560,128]{1,0:T(8,128)S(1)}, bf16[512,768]{1,0:T(8,128)(2,1)S(1)}, bf16[512,768]{1,0:T(8,128)(2,1)S(1)}, bf16[512,768]{1,0:T(8,128)(2,1)S(1)}, bf16[512,768]{1,0:T(8,128)(2,1)S(1)}) custom-call(s32[4]{0:T(128)S(1)} %bitcast.11, s32[1]{0:T(128)} %bitcast.1.me, s32[4,1,1,768]{3,2,1,0:T(1,128)S(1)} %copy-done.1, ...), custom_call_target="tpu_custom_call" | custom-call | flops 2211840000 | tf_op jit(solution)/shard_map/third/pallas_call | solution.py:405
  25.7 2.1 %collective-permute-done.1 = f32[1280,128]{1,0:T(8,128)S(1)} collective-permute-done((f32[1280,128]{1,0:T(8,128)S(1)}, f32[1280,128]{1,0:T(8,128)S(1)}, u32[]{:S(2)}, u32[]{:S(2)}) %collective-permute-start.1) | collective-permute-done | bytes 655392 | tf_op jit(solution)/shard_map/ppermute | solution.py:33
  27.9 2.4 %collective-permute-start.2 = (f32[320,128]{1,0:T(8,128)S(1)}, f32[320,128]{1,0:T(8,128)S(1)}, u32[]{:S(2)}, u32[]{:S(2)}) collective-permute-start(f32[320,128]{1,0:T(8,128)S(1)} %get-tuple-element.191), channel_id=1, source_target_pairs={{0,24},{1,25},{2,26},{3,27},{4,28},{5,29},{6,30},{7,31},{8,16},{9,... | collective-permute-start | bytes 491528 | tf_op jit(solution)/shard_map/ppermute | solution.py:33
  31.7 3.4 %fourth.2 = (f32[408,512]{1,0:T(8,128)S(1)}, f32[400,768]{1,0:T(8,128)S(1)}, f32[1,1,768]{2,1,0:T(1,128)S(1)}, bf16[512,768]{1,0:T(8,128)(2,1)S(1)}, bf16[512,768]{1,0:T(8,128)(2,1)S(1)}) custom-call(s32[4]{0:T(128)S(1)} %bitcast.12, f32[2,400,400]{2,1,0:T(8,128)S(1)} %copy-done, f32[400,768]{1,0:T(8,128)S(1)} %get-tuple-element.114.source, ...), custom_call_target="tpu_custom_call" | custom-call | flops 1474560000 | tf_op jit(solution)/shard_map/fourth/pallas_call | solution.py:405
  36.0 2.7 %collective-permute-done.4 = f32[320,128]{1,0:T(8,128)S(1)} collective-permute-done((f32[320,128]{1,0:T(8,128)S(1)}, f32[320,128]{1,0:T(8,128)S(1)}, u32[]{:S(2)}, u32[]{:S(2)}) %collective-permute-start.4) | collective-permute-done | bytes 163872 | tf_op jit(solution)/shard_map/ppermute | solution.py:33
  39.9 3.7 %collective-permute-start.5 = (f32[80,128]{1,0:T(8,128)S(1)}, f32[80,128]{1,0:T(8,128)S(1)}, u32[]{:S(2)}, u32[]{:S(2)}) collective-permute-start(f32[80,128]{1,0:T(8,128)S(1)} %get-tuple-element.197), channel_id=1, source_target_pairs={{0,3},{1,2},{2,1},{3,0},{4,7},{5,6},{6,5},{7,4},{8,11},{9,10},{10,... | collective-permute-start | bytes 122888 | tf_op jit(solution)/shard_map/ppermute | solution.py:33
  44.3 1.7 %collective-permute-done.5 = f32[80,128]{1,0:T(8,128)S(1)} collective-permute-done((f32[80,128]{1,0:T(8,128)S(1)}, f32[80,128]{1,0:T(8,128)S(1)}, u32[]{:S(2)}, u32[]{:S(2)}) %collective-permute-start.5) | collective-permute-done | bytes 40992 | tf_op jit(solution)/shard_map/ppermute | solution.py:33
  46.0 2.4 %collective-permute-done.7 = f32[80,128]{1,0:T(8,128)S(1)} collective-permute-done((f32[80,128]{1,0:T(8,128)S(1)}, f32[80,128]{1,0:T(8,128)S(1)}, u32[]{:S(2)}, u32[]{:S(2)}) %collective-permute-start.7) | collective-permute-done | bytes 40992 | tf_op jit(solution)/shard_map/ppermute | solution.py:33
  48.5 2.1 %collective-permute-start.10 = (f32[80,128]{1,0:T(8,128)S(1)}, f32[80,128]{1,0:T(8,128)S(1)}, u32[]{:S(2)}, u32[]{:S(2)}) collective-permute-start(f32[80,128]{1,0:T(8,128)S(1)} %add_add_fusion.3), channel_id=1, source_target_pairs={{0,3},{1,2},{2,1},{3,0},{4,7},{5,6},{6,5},{7,4},{8,11},{9,10},{10,... | collective-permute-start | bytes 122888 | tf_op jit(solution)/shard_map/ppermute | solution.py:33
  51.0 1.9 %collective-permute-start.8 = (f32[80,128]{1,0:T(8,128)S(1)}, f32[80,128]{1,0:T(8,128)S(1)}, u32[]{:S(2)}, u32[]{:S(2)}) collective-permute-start(f32[80,128]{1,0:T(8,128)S(1)} %add_add_fusion.3), channel_id=1, source_target_pairs={{0,1},{1,0},{2,3},{3,2},{4,5},{5,4},{6,7},{7,6},{8,9},{9,8},{10,11... | collective-permute-start | bytes 122888 | tf_op jit(solution)/shard_map/ppermute | solution.py:33
  55.8 1.9 %collective-permute-start.14 = (f32[320,128]{1,0:T(8,128)S(1)}, f32[320,128]{1,0:T(8,128)S(1)}, u32[]{:S(2)}, u32[]{:S(2)}) collective-permute-start(f32[320,128]{1,0:T(8,128)S(1)} %pad_maximum_fusion.2), channel_id=1, source_target_pairs={{0,24},{1,25},{2,26},{3,27},{4,28},{5,29},{6,30},{7,31},{8,16},{9,... | collective-permute-start | bytes 491528 | tf_op jit(solution)/shard_map/ppermute | solution.py:33
  59.7 3.9 %collective-permute-done.14 = f32[320,128]{1,0:T(8,128)S(1)} collective-permute-done((f32[320,128]{1,0:T(8,128)S(1)}, f32[320,128]{1,0:T(8,128)S(1)}, u32[]{:S(2)}, u32[]{:S(2)}) %collective-permute-start.14) | collective-permute-done | bytes 163872 | tf_op jit(solution)/shard_map/ppermute | solution.py:33
  63.6 1.5 %collective-permute-done.13 = f32[320,128]{1,0:T(8,128)S(1)} collective-permute-done((f32[320,128]{1,0:T(8,128)S(1)}, f32[320,128]{1,0:T(8,128)S(1)}, u32[]{:S(2)}, u32[]{:S(2)}) %collective-permute-start.13) | collective-permute-done | bytes 163872 | tf_op jit(solution)/shard_map/ppermute | solution.py:33
  65.7 1.8 %collective-permute-done.15.packed = f32[1280,128]{1,0:T(8,128)S(1)} collective-permute-done((f32[1280,128]{1,0:T(8,128)S(1)}, f32[1280,128]{1,0:T(8,128)S(1)}, u32[]{:S(2)}, u32[]{:S(2)}) %collective-permute-start.15) | collective-permute-done | bytes 655392 | tf_op jit(solution)/shard_map/ppermute | solution.py:33
  67.5 5.2 %first.1 = (f32[2,400,400]{2,1,0:T(8,128)S(1)}, f32[2,400,400]{2,1,0:T(8,128)S(1)}, f32[408,512]{1,0:T(8,128)S(1)}, bf16[512,768]{1,0:T(8,128)(2,1)S(1)}, bf16[512,768]{1,0:T(8,128)(2,1)S(1)}) custom-call(s32[4]{0:T(128)S(1)} %bitcast.13, s32[1]{0:T(128)} %bitcast.1.me, ...), custom_call_target="tpu_custom_call", output_to_operand_aliasing={{0}: (5, {}), {1}: (6, {})} | custom-call | flops 2211840000 | tf_op jit(solution)/shard_map/first/pallas_call | solution.py:405
  72.9 5.4 %second.3 = (f32[400,768]{1,0:T(8,128)S(1)}, f32[1,1,768]{2,1,0:T(1,128)S(1)}, f32[400,512]{1,0:T(8,128)S(1)}, bf16[512,768]{1,0:T(8,128)(2,1)S(1)}, bf16[512,76...) custom-call(s32[4]{0:T(128)S(1)} %bitcast.14, ...), custom_call_target="tpu_custom_call" | custom-call | flops 2949120000 | tf_op jit(solution)/shard_map/second/pallas_call | solution.py:405
  78.3 7.3 %collective-permute-done.16.target = f32[408,512]{1,0:T(8,128)S(1)} collective-permute-done((f32[408,512]{1,0:T(8,128)S(1)}, f32[408,512]{1,0:T(8,128)S(1)}, u32[]{:S(2)}, u32[]{:S(2)}) %collective-permute-start.16) | collective-permute-done | bytes 835616 | tf_op jit(solution)/shard_map/ppermute | solution.py:27
  85.6 4.7 %third.3 = (f32[2560,128]{1,0:T(8,128)S(1)}, bf16[512,768]{1,0:T(8,128)(2,1)S(1)}, bf16[512,768]{1,0:T(8,128)(2,1)S(1)}, bf16[512,768]{1,0:T(8,128)(2,1)S(1)}, bf16[512,768]{1,0:T(8,128)(2,1)S(1)}) custom-call(s32[4]{0:T(128)S(1)} %bitcast.15, s32[1]{0:T(128)} %bitcast.1.me, s32[4,1,1,768]{3,2,1,0:T(1,128)S(1)} %copy-done.1, ...), custom_call_target="tpu_custom_call" | custom-call | flops 2211840000 | tf_op jit(solution)/shard_map/third/pallas_call | solution.py:405
  90.4 2.1 %collective-permute-done.17 = f32[1280,128]{1,0:T(8,128)S(1)} collective-permute-done((f32[1280,128]{1,0:T(8,128)S(1)}, f32[1280,128]{1,0:T(8,128)S(1)}, u32[]{:S(2)}, u32[]{:S(2)}) %collective-permute-start.17) | collective-permute-done | bytes 655392 | tf_op jit(solution)/shard_map/ppermute | solution.py:33
  96.1 4.1 %fourth.3 = (f32[408,512]{1,0:T(8,128)S(1)}, f32[400,768]{1,0:T(8,128)}, f32[1,1,768]{2,1,0:T(1,128)}) custom-call(s32[4]{0:T(128)S(1)} %bitcast.16, f32[2,400,400]{2,1,0:T(8,128)S(1)} %get-tuple-element.161.relations, f32[400,768]{1,0:T(8,128)S(1)} %get-tuple-element.162.source, f32[1,1,768]{2,1,0:T(1,128)S(1)} %get-tuple-element.163.source_state, ...), custom_call_target="tpu_custom_call" | custom-call | flops 1474560000 | tf_op jit(solution)/shard_map/fourth/pallas_call | solution.py:405
  100.7 2.6 %collective-permute-done.20 = f32[320,128]{1,0:T(8,128)S(1)} collective-permute-done((f32[320,128]{1,0:T(8,128)S(1)}, f32[320,128]{1,0:T(8,128)S(1)}, u32[]{:S(2)}, u32[]{:S(2)}) %collective-permute-start.20) | collective-permute-done | bytes 163872 | tf_op jit(solution)/shard_map/ppermute | solution.py:33
  103.4 3.1 %collective-permute-start.21 = (f32[80,128]{1,0:T(8,128)S(1)}, f32[80,128]{1,0:T(8,128)S(1)}, u32[]{:S(2)}, u32[]{:S(2)}) collective-permute-start(f32[80,128]{1,0:T(8,128)S(1)} %get-tuple-element.194), channel_id=1, source_target_pairs={{0,3},{1,2},{2,1},{3,0},{4,7},{5,6},{6,5},{7,4},{8,11},{9,10},{10,... | collective-permute-start | bytes 122888 | tf_op jit(solution)/shard_map/ppermute | solution.py:33
  107.9 1.8 %collective-permute-done.21 = f32[80,128]{1,0:T(8,128)S(1)} collective-permute-done((f32[80,128]{1,0:T(8,128)S(1)}, f32[80,128]{1,0:T(8,128)S(1)}, u32[]{:S(2)}, u32[]{:S(2)}) %collective-permute-start.21) | collective-permute-done | bytes 40992 | tf_op jit(solution)/shard_map/ppermute | solution.py:33
  109.7 1.7 %collective-permute-done.23 = f32[80,128]{1,0:T(8,128)S(1)} collective-permute-done((f32[80,128]{1,0:T(8,128)S(1)}, f32[80,128]{1,0:T(8,128)S(1)}, u32[]{:S(2)}, u32[]{:S(2)}) %collective-permute-start.23) | collective-permute-done | bytes 40992 | tf_op jit(solution)/shard_map/ppermute | solution.py:33
  111.4 2.5 %collective-permute-start.26 = (f32[80,128]{1,0:T(8,128)S(1)}, f32[80,128]{1,0:T(8,128)S(1)}, u32[]{:S(2)}, u32[]{:S(2)}) collective-permute-start(f32[80,128]{1,0:T(8,128)S(1)} %add_add_fusion.2), channel_id=1, source_target_pairs={{0,3},{1,2},{2,1},{3,0},{4,7},{5,6},{6,5},{7,4},{8,11},{9,10},{10,... | collective-permute-start | bytes 122888 | tf_op jit(solution)/shard_map/ppermute | solution.py:33
  113.9 1.9 %collective-permute-start.24 = (f32[80,128]{1,0:T(8,128)S(1)}, f32[80,128]{1,0:T(8,128)S(1)}, u32[]{:S(2)}, u32[]{:S(2)}) collective-permute-start(f32[80,128]{1,0:T(8,128)S(1)} %add_add_fusion.2), channel_id=1, source_target_pairs={{0,1},{1,0},{2,3},{3,2},{4,5},{5,4},{6,7},{7,6},{8,9},{9,8},{10,11... | collective-permute-start | bytes 122888 | tf_op jit(solution)/shard_map/ppermute | solution.py:33
  117.3 1.7 %collective-permute-done.25 = f32[80,128]{1,0:T(8,128)S(1)} collective-permute-done((f32[80,128]{1,0:T(8,128)S(1)}, f32[80,128]{1,0:T(8,128)S(1)}, u32[]{:S(2)}, u32[]{:S(2)}) %collective-permute-start.25) | collective-permute-done | bytes 40992 | tf_op jit(solution)/shard_map/ppermute | solution.py:33
  124.1 2.7 %collective-permute-done.30 = f32[320,128]{1,0:T(8,128)S(1)} collective-permute-done((f32[320,128]{1,0:T(8,128)S(1)}, f32[320,128]{1,0:T(8,128)S(1)}, u32[]{:S(2)}, u32[]{:S(2)}) %collective-permute-start.30) | collective-permute-done | bytes 163872 | tf_op jit(solution)/shard_map/ppermute | solution.py:33
  128.3 1.5 %closing.2 = (f32[2,2,400,400]{3,2,1,0:T(8,128)}, f32[2,400,400]{2,1,0:T(8,128)}) custom-call(s32[1]{0:T(128)} %bitcast.1.me, f32[1280,128]{1,0:T(8,128)S(1)} %pad_maximum_fusion.1.packed, f32[2,400,400]{2,1,0:T(8,128)S(1)} %get-tuple-element.161.relations, f32[2,2,400,400]{3,2,1,0:T(8,128)} %get-tuple-element.183.refs_0_), custom_call_target="tpu_custom_call", output_to_operand_aliasing={{0}: (3, {})} | custom-call | flops 184320000 | tf_op jit(solution)/shard_map/closing/pallas_call | solution.py:405
  (74 shorter events, 27.1 us)
Async XLA Ops:
  7.1 13.8 %collective-permute-start = (f32[408,512]{1,0:T(8,128)S(1)}, f32[408,512]{1,0:T(8,128)S(1)}, u32[]{:S(2)}, u32[]{:S(2)}) collective-permute-start(f32[408,512]{1,0:T(8,128)S(1)} %get-tuple-element.101), channel_id=1, source_target_pairs={{0,4},{4,8},{8,12},{12,16},{16,20},{20,24},{24,28},{28,0},{1,5},{5... | collective-permute-start | bytes 2506760 | tf_op jit(solution)/shard_map/ppermute | solution.py:27
  25.7 2.2 %collective-permute-start.1 = (f32[1280,128]{1,0:T(8,128)S(1)}, f32[1280,128]{1,0:T(8,128)S(1)}, u32[]{:S(2)}, u32[]{:S(2)}) collective-permute-start(f32[1280,128]{1,0:T(8,128)S(1)} %slice.87), channel_id=1, source_target_pairs={{0,4},{1,5},{2,6},{3,7},{4,0},{5,1},{6,2},{7,3},{8,12},{9,13},{10,... | collective-permute-start | bytes 1966088 | tf_op jit(solution)/shard_map/ppermute | solution.py:33
  27.9 8.0 %collective-permute-start.2 = (f32[320,128]{1,0:T(8,128)S(1)}, f32[320,128]{1,0:T(8,128)S(1)}, u32[]{:S(2)}, u32[]{:S(2)}) collective-permute-start(f32[320,128]{1,0:T(8,128)S(1)} %get-tuple-element.191), channel_id=1, source_target_pairs={{0,24},{1,25},{2,26},{3,27},{4,28},{5,29},{6,30},{7,31},{8,16},{9,... | collective-permute-start | bytes 491528 | tf_op jit(solution)/shard_map/ppermute | solution.py:33
  30.3 8.4 %collective-permute-start.4 = (f32[320,128]{1,0:T(8,128)S(1)}, f32[320,128]{1,0:T(8,128)S(1)}, u32[]{:S(2)}, u32[]{:S(2)}) collective-permute-start(f32[320,128]{1,0:T(8,128)S(1)} %get-tuple-element.192), channel_id=1, source_target_pairs={{0,16},{1,17},{2,18},{3,19},{4,20},{5,21},{6,22},{7,23},{8,24},{9,... | collective-permute-start | bytes 491528 | tf_op jit(solution)/shard_map/ppermute | solution.py:33
  30.8 8.7 %collective-permute-start.3 = (f32[320,128]{1,0:T(8,128)S(1)}, f32[320,128]{1,0:T(8,128)S(1)}, u32[]{:S(2)}, u32[]{:S(2)}) collective-permute-start(f32[320,128]{1,0:T(8,128)S(1)} %get-tuple-element.193), channel_id=1, source_target_pairs={{0,8},{1,9},{2,10},{3,11},{4,12},{5,13},{6,14},{7,15},{8,0},{9,1},... | collective-permute-start | bytes 491528 | tf_op jit(solution)/shard_map/ppermute | solution.py:33
  39.6 16.2 %collective-permute-start.11 = (f32[408,512]{1,0:T(8,128)S(1)}, f32[408,512]{1,0:T(8,128)S(1)}, u32[]{:S(2)}, u32[]{:S(2)}) collective-permute-start(f32[408,512]{1,0:T(8,128)S(1)} %get-tuple-element.125), channel_id=1, source_target_pairs={{0,4},{4,8},{8,12},{12,16},{16,20},{20,24},{24,28},{28,0},{1,5},{5... | collective-permute-start | bytes 2506760 | tf_op jit(solution)/shard_map/ppermute | solution.py:27
  39.9 6.1 %collective-permute-start.5 = (f32[80,128]{1,0:T(8,128)S(1)}, f32[80,128]{1,0:T(8,128)S(1)}, u32[]{:S(2)}, u32[]{:S(2)}) collective-permute-start(f32[80,128]{1,0:T(8,128)S(1)} %get-tuple-element.197), channel_id=1, source_target_pairs={{0,3},{1,2},{2,1},{3,0},{4,7},{5,6},{6,5},{7,4},{8,11},{9,10},{10,... | collective-permute-start | bytes 122888 | tf_op jit(solution)/shard_map/ppermute | solution.py:33
  43.5 4.9 %collective-permute-start.7 = (f32[80,128]{1,0:T(8,128)S(1)}, f32[80,128]{1,0:T(8,128)S(1)}, u32[]{:S(2)}, u32[]{:S(2)}) collective-permute-start(f32[80,128]{1,0:T(8,128)S(1)} %get-tuple-element.198), channel_id=1, source_target_pairs={{0,2},{1,3},{2,0},{3,1},{4,6},{5,7},{6,4},{7,5},{8,10},{9,11},{10,... | collective-permute-start | bytes 122888 | tf_op jit(solution)/shard_map/ppermute | solution.py:33
  43.5 4.9 %collective-permute-start.6 = (f32[80,128]{1,0:T(8,128)S(1)}, f32[80,128]{1,0:T(8,128)S(1)}, u32[]{:S(2)}, u32[]{:S(2)}) collective-permute-start(f32[80,128]{1,0:T(8,128)S(1)} %get-tuple-element.199), channel_id=1, source_target_pairs={{0,1},{1,0},{2,3},{3,2},{4,5},{5,4},{6,7},{7,6},{8,9},{9,8},{10,11... | collective-permute-start | bytes 122888 | tf_op jit(solution)/shard_map/ppermute | solution.py:33
  48.5 5.9 %collective-permute-start.10 = (f32[80,128]{1,0:T(8,128)S(1)}, f32[80,128]{1,0:T(8,128)S(1)}, u32[]{:S(2)}, u32[]{:S(2)}) collective-permute-start(f32[80,128]{1,0:T(8,128)S(1)} %add_add_fusion.3), channel_id=1, source_target_pairs={{0,3},{1,2},{2,1},{3,0},{4,7},{5,6},{6,5},{7,4},{8,11},{9,10},{10,... | collective-permute-start | bytes 122888 | tf_op jit(solution)/shard_map/ppermute | solution.py:33
  50.5 5.3 %collective-permute-start.9 = (f32[80,128]{1,0:T(8,128)S(1)}, f32[80,128]{1,0:T(8,128)S(1)}, u32[]{:S(2)}, u32[]{:S(2)}) collective-permute-start(f32[80,128]{1,0:T(8,128)S(1)} %add_add_fusion.3), channel_id=1, source_target_pairs={{0,2},{1,3},{2,0},{3,1},{4,6},{5,7},{6,4},{7,5},{8,10},{9,11},{10,... | collective-permute-start | bytes 122888 | tf_op jit(solution)/shard_map/ppermute | solution.py:33
  51.0 4.8 %collective-permute-start.8 = (f32[80,128]{1,0:T(8,128)S(1)}, f32[80,128]{1,0:T(8,128)S(1)}, u32[]{:S(2)}, u32[]{:S(2)}) collective-permute-start(f32[80,128]{1,0:T(8,128)S(1)} %add_add_fusion.3), channel_id=1, source_target_pairs={{0,1},{1,0},{2,3},{3,2},{4,5},{5,4},{6,7},{7,6},{8,9},{9,8},{10,11... | collective-permute-start | bytes 122888 | tf_op jit(solution)/shard_map/ppermute | solution.py:33
  55.8 7.8 %collective-permute-start.14 = (f32[320,128]{1,0:T(8,128)S(1)}, f32[320,128]{1,0:T(8,128)S(1)}, u32[]{:S(2)}, u32[]{:S(2)}) collective-permute-start(f32[320,128]{1,0:T(8,128)S(1)} %pad_maximum_fusion.2), channel_id=1, source_target_pairs={{0,24},{1,25},{2,26},{3,27},{4,28},{5,29},{6,30},{7,31},{8,16},{9,... | collective-permute-start | bytes 491528 | tf_op jit(solution)/shard_map/ppermute | solution.py:33
  57.7 7.4 %collective-permute-start.13 = (f32[320,128]{1,0:T(8,128)S(1)}, f32[320,128]{1,0:T(8,128)S(1)}, u32[]{:S(2)}, u32[]{:S(2)}) collective-permute-start(f32[320,128]{1,0:T(8,128)S(1)} %pad_maximum_fusion.2), channel_id=1, source_target_pairs={{0,16},{1,17},{2,18},{3,19},{4,20},{5,21},{6,22},{7,23},{8,24},{9,... | collective-permute-start | bytes 491528 | tf_op jit(solution)/shard_map/ppermute | solution.py:33
  58.3 7.0 %collective-permute-start.12 = (f32[320,128]{1,0:T(8,128)S(1)}, f32[320,128]{1,0:T(8,128)S(1)}, u32[]{:S(2)}, u32[]{:S(2)}) collective-permute-start(f32[320,128]{1,0:T(8,128)S(1)} %pad_maximum_fusion.2), channel_id=1, source_target_pairs={{0,8},{1,9},{2,10},{3,11},{4,12},{5,13},{6,14},{7,15},{8,0},{9,1},... | collective-permute-start | bytes 491528 | tf_op jit(solution)/shard_map/ppermute | solution.py:33
  65.3 2.2 %collective-permute-start.15 = (f32[1280,128]{1,0:T(8,128)S(1)}, f32[1280,128]{1,0:T(8,128)S(1)}, u32[]{:S(2)}, u32[]{:S(2)}) collective-permute-start(f32[1280,128]{1,0:T(8,128)S(1)} %pad_maximum_fusion.packed), channel_id=1, source_target_pairs={{0,4},{1,5},{2,6},{3,7},{4,0},{5,1},{6,2},{7,3},{8,12},{9,13},{10,... | collective-permute-start | bytes 1966088 | tf_op jit(solution)/shard_map/ppermute | solution.py:33
  72.7 12.9 %collective-permute-start.16 = (f32[408,512]{1,0:T(8,128)S(1)}, f32[408,512]{1,0:T(8,128)S(1)}, u32[]{:S(2)}, u32[]{:S(2)}) collective-permute-start(f32[408,512]{1,0:T(8,128)S(1)} %get-tuple-element.149), channel_id=1, source_target_pairs={{0,4},{4,8},{8,12},{12,16},{16,20},{20,24},{24,28},{28,0},{1,5},{5... | collective-permute-start | bytes 2506760 | tf_op jit(solution)/shard_map/ppermute | solution.py:27
  90.3 2.2 %collective-permute-start.17 = (f32[1280,128]{1,0:T(8,128)S(1)}, f32[1280,128]{1,0:T(8,128)S(1)}, u32[]{:S(2)}, u32[]{:S(2)}) collective-permute-start(f32[1280,128]{1,0:T(8,128)S(1)} %slice.97), channel_id=1, source_target_pairs={{0,4},{1,5},{2,6},{3,7},{4,0},{5,1},{6,2},{7,3},{8,12},{9,13},{10,... | collective-permute-start | bytes 1966088 | tf_op jit(solution)/shard_map/ppermute | solution.py:33
  92.6 8.1 %collective-permute-start.18 = (f32[320,128]{1,0:T(8,128)S(1)}, f32[320,128]{1,0:T(8,128)S(1)}, u32[]{:S(2)}, u32[]{:S(2)}) collective-permute-start(f32[320,128]{1,0:T(8,128)S(1)} %get-tuple-element.188), channel_id=1, source_target_pairs={{0,24},{1,25},{2,26},{3,27},{4,28},{5,29},{6,30},{7,31},{8,16},{9,... | collective-permute-start | bytes 491528 | tf_op jit(solution)/shard_map/ppermute | solution.py:33
  94.0 9.4 %collective-permute-start.20 = (f32[320,128]{1,0:T(8,128)S(1)}, f32[320,128]{1,0:T(8,128)S(1)}, u32[]{:S(2)}, u32[]{:S(2)}) collective-permute-start(f32[320,128]{1,0:T(8,128)S(1)} %get-tuple-element.189), channel_id=1, source_target_pairs={{0,16},{1,17},{2,18},{3,19},{4,20},{5,21},{6,22},{7,23},{8,24},{9,... | collective-permute-start | bytes 491528 | tf_op jit(solution)/shard_map/ppermute | solution.py:33
  94.7 8.6 %collective-permute-start.19 = (f32[320,128]{1,0:T(8,128)S(1)}, f32[320,128]{1,0:T(8,128)S(1)}, u32[]{:S(2)}, u32[]{:S(2)}) collective-permute-start(f32[320,128]{1,0:T(8,128)S(1)} %get-tuple-element.190), channel_id=1, source_target_pairs={{0,8},{1,9},{2,10},{3,11},{4,12},{5,13},{6,14},{7,15},{8,0},{9,1},... | collective-permute-start | bytes 491528 | tf_op jit(solution)/shard_map/ppermute | solution.py:33
  103.4 15.6 %collective-permute-start.27 = (f32[408,512]{1,0:T(8,128)S(1)}, f32[408,512]{1,0:T(8,128)S(1)}, u32[]{:S(2)}, u32[]{:S(2)}) collective-permute-start(f32[408,512]{1,0:T(8,128)S(1)} %get-tuple-element.173), channel_id=1, source_target_pairs={{0,4},{4,8},{8,12},{12,16},{16,20},{20,24},{24,28},{28,0},{1,5},{5... | collective-permute-start | bytes 2506760 | tf_op jit(solution)/shard_map/ppermute | solution.py:27
  103.4 6.3 %collective-permute-start.21 = (f32[80,128]{1,0:T(8,128)S(1)}, f32[80,128]{1,0:T(8,128)S(1)}, u32[]{:S(2)}, u32[]{:S(2)}) collective-permute-start(f32[80,128]{1,0:T(8,128)S(1)} %get-tuple-element.194), channel_id=1, source_target_pairs={{0,3},{1,2},{2,1},{3,0},{4,7},{5,6},{6,5},{7,4},{8,11},{9,10},{10,... | collective-permute-start | bytes 122888 | tf_op jit(solution)/shard_map/ppermute | solution.py:33
  106.5 4.9 %collective-permute-start.23 = (f32[80,128]{1,0:T(8,128)S(1)}, f32[80,128]{1,0:T(8,128)S(1)}, u32[]{:S(2)}, u32[]{:S(2)}) collective-permute-start(f32[80,128]{1,0:T(8,128)S(1)} %get-tuple-element.195), channel_id=1, source_target_pairs={{0,2},{1,3},{2,0},{3,1},{4,6},{5,7},{6,4},{7,5},{8,10},{9,11},{10,... | collective-permute-start | bytes 122888 | tf_op jit(solution)/shard_map/ppermute | solution.py:33
  106.5 4.9 %collective-permute-start.22 = (f32[80,128]{1,0:T(8,128)S(1)}, f32[80,128]{1,0:T(8,128)S(1)}, u32[]{:S(2)}, u32[]{:S(2)}) collective-permute-start(f32[80,128]{1,0:T(8,128)S(1)} %get-tuple-element.196), channel_id=1, source_target_pairs={{0,1},{1,0},{2,3},{3,2},{4,5},{5,4},{6,7},{7,6},{8,9},{9,8},{10,11... | collective-permute-start | bytes 122888 | tf_op jit(solution)/shard_map/ppermute | solution.py:33
  111.4 5.9 %collective-permute-start.26 = (f32[80,128]{1,0:T(8,128)S(1)}, f32[80,128]{1,0:T(8,128)S(1)}, u32[]{:S(2)}, u32[]{:S(2)}) collective-permute-start(f32[80,128]{1,0:T(8,128)S(1)} %add_add_fusion.2), channel_id=1, source_target_pairs={{0,3},{1,2},{2,1},{3,0},{4,7},{5,6},{6,5},{7,4},{8,11},{9,10},{10,... | collective-permute-start | bytes 122888 | tf_op jit(solution)/shard_map/ppermute | solution.py:33
  113.9 5.0 %collective-permute-start.25 = (f32[80,128]{1,0:T(8,128)S(1)}, f32[80,128]{1,0:T(8,128)S(1)}, u32[]{:S(2)}, u32[]{:S(2)}) collective-permute-start(f32[80,128]{1,0:T(8,128)S(1)} %add_add_fusion.2), channel_id=1, source_target_pairs={{0,2},{1,3},{2,0},{3,1},{4,6},{5,7},{6,4},{7,5},{8,10},{9,11},{10,... | collective-permute-start | bytes 122888 | tf_op jit(solution)/shard_map/ppermute | solution.py:33
  113.9 5.0 %collective-permute-start.24 = (f32[80,128]{1,0:T(8,128)S(1)}, f32[80,128]{1,0:T(8,128)S(1)}, u32[]{:S(2)}, u32[]{:S(2)}) collective-permute-start(f32[80,128]{1,0:T(8,128)S(1)} %add_add_fusion.2), channel_id=1, source_target_pairs={{0,1},{1,0},{2,3},{3,2},{4,5},{5,4},{6,7},{7,6},{8,9},{9,8},{10,11... | collective-permute-start | bytes 122888 | tf_op jit(solution)/shard_map/ppermute | solution.py:33
  119.0 7.8 %collective-permute-start.30 = (f32[320,128]{1,0:T(8,128)S(1)}, f32[320,128]{1,0:T(8,128)S(1)}, u32[]{:S(2)}, u32[]{:S(2)}) collective-permute-start(f32[320,128]{1,0:T(8,128)S(1)} %pad_maximum_fusion.3), channel_id=1, source_target_pairs={{0,24},{1,25},{2,26},{3,27},{4,28},{5,29},{6,30},{7,31},{8,16},{9,... | collective-permute-start | bytes 491528 | tf_op jit(solution)/shard_map/ppermute | solution.py:33
  120.2 8.0 %collective-permute-start.29 = (f32[320,128]{1,0:T(8,128)S(1)}, f32[320,128]{1,0:T(8,128)S(1)}, u32[]{:S(2)}, u32[]{:S(2)}) collective-permute-start(f32[320,128]{1,0:T(8,128)S(1)} %pad_maximum_fusion.3), channel_id=1, source_target_pairs={{0,16},{1,17},{2,18},{3,19},{4,20},{5,21},{6,22},{7,23},{8,24},{9,... | collective-permute-start | bytes 491528 | tf_op jit(solution)/shard_map/ppermute | solution.py:33
  121.4 6.8 %collective-permute-start.28 = (f32[320,128]{1,0:T(8,128)S(1)}, f32[320,128]{1,0:T(8,128)S(1)}, u32[]{:S(2)}, u32[]{:S(2)}) collective-permute-start(f32[320,128]{1,0:T(8,128)S(1)} %pad_maximum_fusion.3), channel_id=1, source_target_pairs={{0,8},{1,9},{2,10},{3,11},{4,12},{5,13},{6,14},{7,15},{8,0},{9,1},... | collective-permute-start | bytes 491528 | tf_op jit(solution)/shard_map/ppermute | solution.py:33
  128.2 2.2 %collective-permute-start.31 = (f32[1280,128]{1,0:T(8,128)S(1)}, f32[1280,128]{1,0:T(8,128)S(1)}, u32[]{:S(2)}, u32[]{:S(2)}) collective-permute-start(f32[1280,128]{1,0:T(8,128)S(1)} %pad_maximum_fusion.1.packed), channel_id=1, source_target_pairs={{0,4},{1,5},{2,6},{3,7},{4,0},{5,1},{6,2},{7,3},{8,12},{9,13},{10,... | collective-permute-start | bytes 1966088 | tf_op jit(solution)/shard_map/ppermute | solution.py:33
  (6 other events, 48.7 us)

commit v6 on v5

--- a/solution.py
+++ b/solution.py
@@ -292,7 +292,7 @@
 
 def opening_kernel(me, ids, partners, relations, source, target, target_state, target_out, sgh, sgl, square, xh, xl, qh, ql, scores, matrix, source_in, target_in, state_in, partners_in, ids_in, sems):
     width = source.shape[0]
-    pairs = ((ids, ids_in), (relations, matrix), (source, source_in), (target, target_in), (target_state, state_in), (partners.at[0], partners_in))
+    pairs = ((ids, ids_in), (relations, matrix), (target, target_in), (source, source_in), (target_state, state_in), (partners.at[0], partners_in))
     loads = [pltpu.make_async_copy(here, there, sems.at[place]) for place, (here, there) in enumerate(pairs)]
     for load in loads:
         load.start()
@@ -301,11 +301,11 @@
     square_of(square, matrix[ids_in[0]])
     halves = turned_halves(square, width)
     loads[2].wait()
-    put_split((xh, xl), source_in[...])
+    body = target_in[...]
+    turned = split(pad_rows(body, qh.shape[0]).T)
     for load in loads[3:]:
         load.wait()
-    body = target_in[...]
-    turned = split(pad_rows(body, qh.shape[0]).T)
+    put_split((xh, xl), source_in[...])
     queries_into((qh, ql), square, (xh, xl), width, halves)
     score_grad_into((sgh, sgl), scores, (qh, ql), turned, partners_in[0])
     target_into(target_out, (qh, ql), (sgh, sgl), body, state_in[0])

time: 132 us -> 132 us (level)
  no operation moved by 1% of the time
where the time goes in v6:
time: 132 us
  waiting for transfers between devices  52.2 us (40%)
  Pallas kernels  42.9 us (32%)
  starting transfers between devices  33.8 us (26%)
  local copies, waits for them, and re-layouts  1.73 us (1%)
    pallas_call x12, Pallas kernels, call(): pl.pallas_call(kernel, in_specs=args_in, out_specs=outs_in or [VMEM] * le...  42.9 us
    ppermute x28, waiting for transfers between devices, exchange(): return lax.ppermute(value, AXES, pairs)  37.1 us
    ppermute x28, starting transfers between devices, exchange(): return lax.ppermute(value, AXES, pairs)  32.6 us
    ppermute x4, waiting for transfers between devices, from_behind(): return lax.ppermute(value, axis, pairs)  15.1 us
  transfers between devices with their start and end apart: 32, of which 24 were waited for; matrix products, arithmetic and copies ran while one was open for 1% of the time, Pallas kernels for 15%

profile of v6, /device:TPU:0, one launch (start us, length us, event | category | flops | bytes accessed | tf_op | source)
XLA Modules:
  0.0 132.2 jit_solution(18156117898213355423)
XLA Ops:
  0.8 6.5 %opening.1 = (f32[408,512]{1,0:T(8,128)S(1)}, bf16[512,768]{1,0:T(8,128)(2,1)S(1)}, bf16[512,768]{1,0:T(8,128)(2,1)S(1)}) custom-call(s32[1]{0:T(128)} %bitcast.1.me, s32[4]{0:T(128)} %bitcast.9, s32[4,1,1,768]{3,2,1,0:T(1,128)} %partners.7, f32[2,400,400]{2,1,0:T(8,128)} %relations.8, f32[400,768]{1,0:T(8,128)} %bitcast.17, f32[400,512]{1,0:T(8,128)} %bitcast.19, ...), custom_call_target="tpu_custom_call" | custom-call | flops 2211840000 | tf_op jit(solution)/shard_map/opening/pallas_call | solution.py:405
  8.1 5.2 %second.2 = (f32[400,768]{1,0:T(8,128)S(1)}, f32[1,1,768]{2,1,0:T(1,128)S(1)}, f32[400,512]{1,0:T(8,128)S(1)}, bf16[512,768]{1,0:T(8,128)(2,1)S(1)}, bf16[512,76...) custom-call(s32[4]{0:T(128)S(1)} %bitcast.10, f32[2,400,400]{2,1,0:T(8,128)S(1)} %copy-done, ...), custom_call_target="tpu_custom_call" | custom-call | flops 2949120000 | tf_op jit(solution)/shard_map/second/pallas_call | solution.py:405
  13.3 7.8 %collective-permute-done.target = f32[408,512]{1,0:T(8,128)S(1)} collective-permute-done((f32[408,512]{1,0:T(8,128)S(1)}, f32[408,512]{1,0:T(8,128)S(1)}, u32[]{:S(2)}, u32[]{:S(2)}) %collective-permute-start) | collective-permute-done | bytes 835616 | tf_op jit(solution)/shard_map/ppermute | solution.py:27
  21.1 4.7 %third.2 = (f32[2560,128]{1,0:T(8,128)S(1)}, bf16[512,768]{1,0:T(8,128)(2,1)S(1)}, bf16[512,768]{1,0:T(8,128)(2,1)S(1)}, bf16[512,768]{1,0:T(8,128)(2,1)S(1)}, bf16[512,768]{1,0:T(8,128)(2,1)S(1)}) custom-call(s32[4]{0:T(128)S(1)} %bitcast.11, s32[1]{0:T(128)} %bitcast.1.me, s32[4,1,1,768]{3,2,1,0:T(1,128)S(1)} %copy-done.1, ...), custom_call_target="tpu_custom_call" | custom-call | flops 2211840000 | tf_op jit(solution)/shard_map/third/pallas_call | solution.py:405
  25.9 2.1 %collective-permute-done.1 = f32[1280,128]{1,0:T(8,128)S(1)} collective-permute-done((f32[1280,128]{1,0:T(8,128)S(1)}, f32[1280,128]{1,0:T(8,128)S(1)}, u32[]{:S(2)}, u32[]{:S(2)}) %collective-permute-start.1) | collective-permute-done | bytes 655392 | tf_op jit(solution)/shard_map/ppermute | solution.py:33
  28.1 2.4 %collective-permute-start.2 = (f32[320,128]{1,0:T(8,128)S(1)}, f32[320,128]{1,0:T(8,128)S(1)}, u32[]{:S(2)}, u32[]{:S(2)}) collective-permute-start(f32[320,128]{1,0:T(8,128)S(1)} %get-tuple-element.191), channel_id=1, source_target_pairs={{0,24},{1,25},{2,26},{3,27},{4,28},{5,29},{6,30},{7,31},{8,16},{9,... | collective-permute-start | bytes 491528 | tf_op jit(solution)/shard_map/ppermute | solution.py:33
  31.9 3.4 %fourth.2 = (f32[408,512]{1,0:T(8,128)S(1)}, f32[400,768]{1,0:T(8,128)S(1)}, f32[1,1,768]{2,1,0:T(1,128)S(1)}, bf16[512,768]{1,0:T(8,128)(2,1)S(1)}, bf16[512,768]{1,0:T(8,128)(2,1)S(1)}) custom-call(s32[4]{0:T(128)S(1)} %bitcast.12, f32[2,400,400]{2,1,0:T(8,128)S(1)} %copy-done, f32[400,768]{1,0:T(8,128)S(1)} %get-tuple-element.114.source, ...), custom_call_target="tpu_custom_call" | custom-call | flops 1474560000 | tf_op jit(solution)/shard_map/fourth/pallas_call | solution.py:405
  36.2 2.7 %collective-permute-done.4 = f32[320,128]{1,0:T(8,128)S(1)} collective-permute-done((f32[320,128]{1,0:T(8,128)S(1)}, f32[320,128]{1,0:T(8,128)S(1)}, u32[]{:S(2)}, u32[]{:S(2)}) %collective-permute-start.4) | collective-permute-done | bytes 163872 | tf_op jit(solution)/shard_map/ppermute | solution.py:33
  40.0 3.7 %collective-permute-start.5 = (f32[80,128]{1,0:T(8,128)S(1)}, f32[80,128]{1,0:T(8,128)S(1)}, u32[]{:S(2)}, u32[]{:S(2)}) collective-permute-start(f32[80,128]{1,0:T(8,128)S(1)} %get-tuple-element.197), channel_id=1, source_target_pairs={{0,3},{1,2},{2,1},{3,0},{4,7},{5,6},{6,5},{7,4},{8,11},{9,10},{10,... | collective-permute-start | bytes 122888 | tf_op jit(solution)/shard_map/ppermute | solution.py:33
  44.5 1.7 %collective-permute-done.5 = f32[80,128]{1,0:T(8,128)S(1)} collective-permute-done((f32[80,128]{1,0:T(8,128)S(1)}, f32[80,128]{1,0:T(8,128)S(1)}, u32[]{:S(2)}, u32[]{:S(2)}) %collective-permute-start.5) | collective-permute-done | bytes 40992 | tf_op jit(solution)/shard_map/ppermute | solution.py:33
  46.2 2.5 %collective-permute-done.7 = f32[80,128]{1,0:T(8,128)S(1)} collective-permute-done((f32[80,128]{1,0:T(8,128)S(1)}, f32[80,128]{1,0:T(8,128)S(1)}, u32[]{:S(2)}, u32[]{:S(2)}) %collective-permute-start.7) | collective-permute-done | bytes 40992 | tf_op jit(solution)/shard_map/ppermute | solution.py:33
  48.6 2.1 %collective-permute-start.10 = (f32[80,128]{1,0:T(8,128)S(1)}, f32[80,128]{1,0:T(8,128)S(1)}, u32[]{:S(2)}, u32[]{:S(2)}) collective-permute-start(f32[80,128]{1,0:T(8,128)S(1)} %add_add_fusion.3), channel_id=1, source_target_pairs={{0,3},{1,2},{2,1},{3,0},{4,7},{5,6},{6,5},{7,4},{8,11},{9,10},{10,... | collective-permute-start | bytes 122888 | tf_op jit(solution)/shard_map/ppermute | solution.py:33
  51.2 1.9 %collective-permute-start.8 = (f32[80,128]{1,0:T(8,128)S(1)}, f32[80,128]{1,0:T(8,128)S(1)}, u32[]{:S(2)}, u32[]{:S(2)}) collective-permute-start(f32[80,128]{1,0:T(8,128)S(1)} %add_add_fusion.3), channel_id=1, source_target_pairs={{0,1},{1,0},{2,3},{3,2},{4,5},{5,4},{6,7},{7,6},{8,9},{9,8},{10,11... | collective-permute-start | bytes 122888 | tf_op jit(solution)/shard_map/ppermute | solution.py:33
  56.0 1.9 %collective-permute-start.14 = (f32[320,128]{1,0:T(8,128)S(1)}, f32[320,128]{1,0:T(8,128)S(1)}, u32[]{:S(2)}, u32[]{:S(2)}) collective-permute-start(f32[320,128]{1,0:T(8,128)S(1)} %pad_maximum_fusion.2), channel_id=1, source_target_pairs={{0,24},{1,25},{2,26},{3,27},{4,28},{5,29},{6,30},{7,31},{8,16},{9,... | collective-permute-start | bytes 491528 | tf_op jit(solution)/shard_map/ppermute | solution.py:33
  59.9 3.9 %collective-permute-done.14 = f32[320,128]{1,0:T(8,128)S(1)} collective-permute-done((f32[320,128]{1,0:T(8,128)S(1)}, f32[320,128]{1,0:T(8,128)S(1)}, u32[]{:S(2)}, u32[]{:S(2)}) %collective-permute-start.14) | collective-permute-done | bytes 163872 | tf_op jit(solution)/shard_map/ppermute | solution.py:33
  63.8 1.5 %collective-permute-done.13 = f32[320,128]{1,0:T(8,128)S(1)} collective-permute-done((f32[320,128]{1,0:T(8,128)S(1)}, f32[320,128]{1,0:T(8,128)S(1)}, u32[]{:S(2)}, u32[]{:S(2)}) %collective-permute-start.13) | collective-permute-done | bytes 163872 | tf_op jit(solution)/shard_map/ppermute | solution.py:33
  65.9 1.8 %collective-permute-done.15.packed = f32[1280,128]{1,0:T(8,128)S(1)} collective-permute-done((f32[1280,128]{1,0:T(8,128)S(1)}, f32[1280,128]{1,0:T(8,128)S(1)}, u32[]{:S(2)}, u32[]{:S(2)}) %collective-permute-start.15) | collective-permute-done | bytes 655392 | tf_op jit(solution)/shard_map/ppermute | solution.py:33
  67.7 5.2 %first.1 = (f32[2,400,400]{2,1,0:T(8,128)S(1)}, f32[2,400,400]{2,1,0:T(8,128)S(1)}, f32[408,512]{1,0:T(8,128)S(1)}, bf16[512,768]{1,0:T(8,128)(2,1)S(1)}, bf16[512,768]{1,0:T(8,128)(2,1)S(1)}) custom-call(s32[4]{0:T(128)S(1)} %bitcast.13, s32[1]{0:T(128)} %bitcast.1.me, ...), custom_call_target="tpu_custom_call", output_to_operand_aliasing={{0}: (5, {}), {1}: (6, {})} | custom-call | flops 2211840000 | tf_op jit(solution)/shard_map/first/pallas_call | solution.py:405
  73.0 5.4 %second.3 = (f32[400,768]{1,0:T(8,128)S(1)}, f32[1,1,768]{2,1,0:T(1,128)S(1)}, f32[400,512]{1,0:T(8,128)S(1)}, bf16[512,768]{1,0:T(8,128)(2,1)S(1)}, bf16[512,76...) custom-call(s32[4]{0:T(128)S(1)} %bitcast.14, ...), custom_call_target="tpu_custom_call" | custom-call | flops 2949120000 | tf_op jit(solution)/shard_map/second/pallas_call | solution.py:405
  78.5 7.3 %collective-permute-done.16.target = f32[408,512]{1,0:T(8,128)S(1)} collective-permute-done((f32[408,512]{1,0:T(8,128)S(1)}, f32[408,512]{1,0:T(8,128)S(1)}, u32[]{:S(2)}, u32[]{:S(2)}) %collective-permute-start.16) | collective-permute-done | bytes 835616 | tf_op jit(solution)/shard_map/ppermute | solution.py:27
  85.7 4.7 %third.3 = (f32[2560,128]{1,0:T(8,128)S(1)}, bf16[512,768]{1,0:T(8,128)(2,1)S(1)}, bf16[512,768]{1,0:T(8,128)(2,1)S(1)}, bf16[512,768]{1,0:T(8,128)(2,1)S(1)}, bf16[512,768]{1,0:T(8,128)(2,1)S(1)}) custom-call(s32[4]{0:T(128)S(1)} %bitcast.15, s32[1]{0:T(128)} %bitcast.1.me, s32[4,1,1,768]{3,2,1,0:T(1,128)S(1)} %copy-done.1, ...), custom_call_target="tpu_custom_call" | custom-call | flops 2211840000 | tf_op jit(solution)/shard_map/third/pallas_call | solution.py:405
  90.6 2.1 %collective-permute-done.17 = f32[1280,128]{1,0:T(8,128)S(1)} collective-permute-done((f32[1280,128]{1,0:T(8,128)S(1)}, f32[1280,128]{1,0:T(8,128)S(1)}, u32[]{:S(2)}, u32[]{:S(2)}) %collective-permute-start.17) | collective-permute-done | bytes 655392 | tf_op jit(solution)/shard_map/ppermute | solution.py:33
  96.3 4.1 %fourth.3 = (f32[408,512]{1,0:T(8,128)S(1)}, f32[400,768]{1,0:T(8,128)}, f32[1,1,768]{2,1,0:T(1,128)}) custom-call(s32[4]{0:T(128)S(1)} %bitcast.16, f32[2,400,400]{2,1,0:T(8,128)S(1)} %get-tuple-element.161.relations, f32[400,768]{1,0:T(8,128)S(1)} %get-tuple-element.162.source, f32[1,1,768]{2,1,0:T(1,128)S(1)} %get-tuple-element.163.source_state, ...), custom_call_target="tpu_custom_call" | custom-call | flops 1474560000 | tf_op jit(solution)/shard_map/fourth/pallas_call | solution.py:405
  100.8 2.6 %collective-permute-done.20 = f32[320,128]{1,0:T(8,128)S(1)} collective-permute-done((f32[320,128]{1,0:T(8,128)S(1)}, f32[320,128]{1,0:T(8,128)S(1)}, u32[]{:S(2)}, u32[]{:S(2)}) %collective-permute-start.20) | collective-permute-done | bytes 163872 | tf_op jit(solution)/shard_map/ppermute | solution.py:33
  103.6 3.1 %collective-permute-start.21 = (f32[80,128]{1,0:T(8,128)S(1)}, f32[80,128]{1,0:T(8,128)S(1)}, u32[]{:S(2)}, u32[]{:S(2)}) collective-permute-start(f32[80,128]{1,0:T(8,128)S(1)} %get-tuple-element.194), channel_id=1, source_target_pairs={{0,3},{1,2},{2,1},{3,0},{4,7},{5,6},{6,5},{7,4},{8,11},{9,10},{10,... | collective-permute-start | bytes 122888 | tf_op jit(solution)/shard_map/ppermute | solution.py:33
  108.1 1.9 %collective-permute-done.21 = f32[80,128]{1,0:T(8,128)S(1)} collective-permute-done((f32[80,128]{1,0:T(8,128)S(1)}, f32[80,128]{1,0:T(8,128)S(1)}, u32[]{:S(2)}, u32[]{:S(2)}) %collective-permute-start.21) | collective-permute-done | bytes 40992 | tf_op jit(solution)/shard_map/ppermute | solution.py:33
  109.9 1.6 %collective-permute-done.23 = f32[80,128]{1,0:T(8,128)S(1)} collective-permute-done((f32[80,128]{1,0:T(8,128)S(1)}, f32[80,128]{1,0:T(8,128)S(1)}, u32[]{:S(2)}, u32[]{:S(2)}) %collective-permute-start.23) | collective-permute-done | bytes 40992 | tf_op jit(solution)/shard_map/ppermute | solution.py:33
  111.6 2.5 %collective-permute-start.26 = (f32[80,128]{1,0:T(8,128)S(1)}, f32[80,128]{1,0:T(8,128)S(1)}, u32[]{:S(2)}, u32[]{:S(2)}) collective-permute-start(f32[80,128]{1,0:T(8,128)S(1)} %add_add_fusion.2), channel_id=1, source_target_pairs={{0,3},{1,2},{2,1},{3,0},{4,7},{5,6},{6,5},{7,4},{8,11},{9,10},{10,... | collective-permute-start | bytes 122888 | tf_op jit(solution)/shard_map/ppermute | solution.py:33
  114.1 1.9 %collective-permute-start.24 = (f32[80,128]{1,0:T(8,128)S(1)}, f32[80,128]{1,0:T(8,128)S(1)}, u32[]{:S(2)}, u32[]{:S(2)}) collective-permute-start(f32[80,128]{1,0:T(8,128)S(1)} %add_add_fusion.2), channel_id=1, source_target_pairs={{0,1},{1,0},{2,3},{3,2},{4,5},{5,4},{6,7},{7,6},{8,9},{9,8},{10,11... | collective-permute-start | bytes 122888 | tf_op jit(solution)/shard_map/ppermute | solution.py:33
  117.5 1.6 %collective-permute-done.25 = f32[80,128]{1,0:T(8,128)S(1)} collective-permute-done((f32[80,128]{1,0:T(8,128)S(1)}, f32[80,128]{1,0:T(8,128)S(1)}, u32[]{:S(2)}, u32[]{:S(2)}) %collective-permute-start.25) | collective-permute-done | bytes 40992 | tf_op jit(solution)/shard_map/ppermute | solution.py:33
  124.2 2.7 %collective-permute-done.30 = f32[320,128]{1,0:T(8,128)S(1)} collective-permute-done((f32[320,128]{1,0:T(8,128)S(1)}, f32[320,128]{1,0:T(8,128)S(1)}, u32[]{:S(2)}, u32[]{:S(2)}) %collective-permute-start.30) | collective-permute-done | bytes 163872 | tf_op jit(solution)/shard_map/ppermute | solution.py:33
  128.5 1.5 %closing.2 = (f32[2,2,400,400]{3,2,1,0:T(8,128)}, f32[2,400,400]{2,1,0:T(8,128)}) custom-call(s32[1]{0:T(128)} %bitcast.1.me, f32[1280,128]{1,0:T(8,128)S(1)} %pad_maximum_fusion.1.packed, f32[2,400,400]{2,1,0:T(8,128)S(1)} %get-tuple-element.161.relations, f32[2,2,400,400]{3,2,1,0:T(8,128)} %get-tuple-element.183.refs_0_), custom_call_target="tpu_custom_call", output_to_operand_aliasing={{0}: (3, {})} | custom-call | flops 184320000 | tf_op jit(solution)/shard_map/closing/pallas_call | solution.py:405
  (74 shorter events, 27.2 us)
Async XLA Ops:
  7.3 13.8 %collective-permute-start = (f32[408,512]{1,0:T(8,128)S(1)}, f32[408,512]{1,0:T(8,128)S(1)}, u32[]{:S(2)}, u32[]{:S(2)}) collective-permute-start(f32[408,512]{1,0:T(8,128)S(1)} %get-tuple-element.101), channel_id=1, source_target_pairs={{0,4},{4,8},{8,12},{12,16},{16,20},{20,24},{24,28},{28,0},{1,5},{5... | collective-permute-start | bytes 2506760 | tf_op jit(solution)/shard_map/ppermute | solution.py:27
  25.8 2.2 %collective-permute-start.1 = (f32[1280,128]{1,0:T(8,128)S(1)}, f32[1280,128]{1,0:T(8,128)S(1)}, u32[]{:S(2)}, u32[]{:S(2)}) collective-permute-start(f32[1280,128]{1,0:T(8,128)S(1)} %slice.87), channel_id=1, source_target_pairs={{0,4},{1,5},{2,6},{3,7},{4,0},{5,1},{6,2},{7,3},{8,12},{9,13},{10,... | collective-permute-start | bytes 1966088 | tf_op jit(solution)/shard_map/ppermute | solution.py:33
  28.1 8.0 %collective-permute-start.2 = (f32[320,128]{1,0:T(8,128)S(1)}, f32[320,128]{1,0:T(8,128)S(1)}, u32[]{:S(2)}, u32[]{:S(2)}) collective-permute-start(f32[320,128]{1,0:T(8,128)S(1)} %get-tuple-element.191), channel_id=1, source_target_pairs={{0,24},{1,25},{2,26},{3,27},{4,28},{5,29},{6,30},{7,31},{8,16},{9,... | collective-permute-start | bytes 491528 | tf_op jit(solution)/shard_map/ppermute | solution.py:33
  30.5 8.4 %collective-permute-start.4 = (f32[320,128]{1,0:T(8,128)S(1)}, f32[320,128]{1,0:T(8,128)S(1)}, u32[]{:S(2)}, u32[]{:S(2)}) collective-permute-start(f32[320,128]{1,0:T(8,128)S(1)} %get-tuple-element.192), channel_id=1, source_target_pairs={{0,16},{1,17},{2,18},{3,19},{4,20},{5,21},{6,22},{7,23},{8,24},{9,... | collective-permute-start | bytes 491528 | tf_op jit(solution)/shard_map/ppermute | solution.py:33
  31.0 8.7 %collective-permute-start.3 = (f32[320,128]{1,0:T(8,128)S(1)}, f32[320,128]{1,0:T(8,128)S(1)}, u32[]{:S(2)}, u32[]{:S(2)}) collective-permute-start(f32[320,128]{1,0:T(8,128)S(1)} %get-tuple-element.193), channel_id=1, source_target_pairs={{0,8},{1,9},{2,10},{3,11},{4,12},{5,13},{6,14},{7,15},{8,0},{9,1},... | collective-permute-start | bytes 491528 | tf_op jit(solution)/shard_map/ppermute | solution.py:33
  39.7 16.2 %collective-permute-start.11 = (f32[408,512]{1,0:T(8,128)S(1)}, f32[408,512]{1,0:T(8,128)S(1)}, u32[]{:S(2)}, u32[]{:S(2)}) collective-permute-start(f32[408,512]{1,0:T(8,128)S(1)} %get-tuple-element.125), channel_id=1, source_target_pairs={{0,4},{4,8},{8,12},{12,16},{16,20},{20,24},{24,28},{28,0},{1,5},{5... | collective-permute-start | bytes 2506760 | tf_op jit(solution)/shard_map/ppermute | solution.py:27
  40.0 6.1 %collective-permute-start.5 = (f32[80,128]{1,0:T(8,128)S(1)}, f32[80,128]{1,0:T(8,128)S(1)}, u32[]{:S(2)}, u32[]{:S(2)}) collective-permute-start(f32[80,128]{1,0:T(8,128)S(1)} %get-tuple-element.197), channel_id=1, source_target_pairs={{0,3},{1,2},{2,1},{3,0},{4,7},{5,6},{6,5},{7,4},{8,11},{9,10},{10,... | collective-permute-start | bytes 122888 | tf_op jit(solution)/shard_map/ppermute | solution.py:33
  43.7 4.9 %collective-permute-start.7 = (f32[80,128]{1,0:T(8,128)S(1)}, f32[80,128]{1,0:T(8,128)S(1)}, u32[]{:S(2)}, u32[]{:S(2)}) collective-permute-start(f32[80,128]{1,0:T(8,128)S(1)} %get-tuple-element.198), channel_id=1, source_target_pairs={{0,2},{1,3},{2,0},{3,1},{4,6},{5,7},{6,4},{7,5},{8,10},{9,11},{10,... | collective-permute-start | bytes 122888 | tf_op jit(solution)/shard_map/ppermute | solution.py:33
  43.7 4.9 %collective-permute-start.6 = (f32[80,128]{1,0:T(8,128)S(1)}, f32[80,128]{1,0:T(8,128)S(1)}, u32[]{:S(2)}, u32[]{:S(2)}) collective-permute-start(f32[80,128]{1,0:T(8,128)S(1)} %get-tuple-element.199), channel_id=1, source_target_pairs={{0,1},{1,0},{2,3},{3,2},{4,5},{5,4},{6,7},{7,6},{8,9},{9,8},{10,11... | collective-permute-start | bytes 122888 | tf_op jit(solution)/shard_map/ppermute | solution.py:33
  48.6 5.9 %collective-permute-start.10 = (f32[80,128]{1,0:T(8,128)S(1)}, f32[80,128]{1,0:T(8,128)S(1)}, u32[]{:S(2)}, u32[]{:S(2)}) collective-permute-start(f32[80,128]{1,0:T(8,128)S(1)} %add_add_fusion.3), channel_id=1, source_target_pairs={{0,3},{1,2},{2,1},{3,0},{4,7},{5,6},{6,5},{7,4},{8,11},{9,10},{10,... | collective-permute-start | bytes 122888 | tf_op jit(solution)/shard_map/ppermute | solution.py:33
  50.7 5.3 %collective-permute-start.9 = (f32[80,128]{1,0:T(8,128)S(1)}, f32[80,128]{1,0:T(8,128)S(1)}, u32[]{:S(2)}, u32[]{:S(2)}) collective-permute-start(f32[80,128]{1,0:T(8,128)S(1)} %add_add_fusion.3), channel_id=1, source_target_pairs={{0,2},{1,3},{2,0},{3,1},{4,6},{5,7},{6,4},{7,5},{8,10},{9,11},{10,... | collective-permute-start | bytes 122888 | tf_op jit(solution)/shard_map/ppermute | solution.py:33
  51.2 4.8 %collective-permute-start.8 = (f32[80,128]{1,0:T(8,128)S(1)}, f32[80,128]{1,0:T(8,128)S(1)}, u32[]{:S(2)}, u32[]{:S(2)}) collective-permute-start(f32[80,128]{1,0:T(8,128)S(1)} %add_add_fusion.3), channel_id=1, source_target_pairs={{0,1},{1,0},{2,3},{3,2},{4,5},{5,4},{6,7},{7,6},{8,9},{9,8},{10,11... | collective-permute-start | bytes 122888 | tf_op jit(solution)/shard_map/ppermute | solution.py:33
  56.0 7.8 %collective-permute-start.14 = (f32[320,128]{1,0:T(8,128)S(1)}, f32[320,128]{1,0:T(8,128)S(1)}, u32[]{:S(2)}, u32[]{:S(2)}) collective-permute-start(f32[320,128]{1,0:T(8,128)S(1)} %pad_maximum_fusion.2), channel_id=1, source_target_pairs={{0,24},{1,25},{2,26},{3,27},{4,28},{5,29},{6,30},{7,31},{8,16},{9,... | collective-permute-start | bytes 491528 | tf_op jit(solution)/shard_map/ppermute | solution.py:33
  57.9 7.4 %collective-permute-start.13 = (f32[320,128]{1,0:T(8,128)S(1)}, f32[320,128]{1,0:T(8,128)S(1)}, u32[]{:S(2)}, u32[]{:S(2)}) collective-permute-start(f32[320,128]{1,0:T(8,128)S(1)} %pad_maximum_fusion.2), channel_id=1, source_target_pairs={{0,16},{1,17},{2,18},{3,19},{4,20},{5,21},{6,22},{7,23},{8,24},{9,... | collective-permute-start | bytes 491528 | tf_op jit(solution)/shard_map/ppermute | solution.py:33
  58.4 7.0 %collective-permute-start.12 = (f32[320,128]{1,0:T(8,128)S(1)}, f32[320,128]{1,0:T(8,128)S(1)}, u32[]{:S(2)}, u32[]{:S(2)}) collective-permute-start(f32[320,128]{1,0:T(8,128)S(1)} %pad_maximum_fusion.2), channel_id=1, source_target_pairs={{0,8},{1,9},{2,10},{3,11},{4,12},{5,13},{6,14},{7,15},{8,0},{9,1},... | collective-permute-start | bytes 491528 | tf_op jit(solution)/shard_map/ppermute | solution.py:33
  65.5 2.2 %collective-permute-start.15 = (f32[1280,128]{1,0:T(8,128)S(1)}, f32[1280,128]{1,0:T(8,128)S(1)}, u32[]{:S(2)}, u32[]{:S(2)}) collective-permute-start(f32[1280,128]{1,0:T(8,128)S(1)} %pad_maximum_fusion.packed), channel_id=1, source_target_pairs={{0,4},{1,5},{2,6},{3,7},{4,0},{5,1},{6,2},{7,3},{8,12},{9,13},{10,... | collective-permute-start | bytes 1966088 | tf_op jit(solution)/shard_map/ppermute | solution.py:33
  72.8 12.9 %collective-permute-start.16 = (f32[408,512]{1,0:T(8,128)S(1)}, f32[408,512]{1,0:T(8,128)S(1)}, u32[]{:S(2)}, u32[]{:S(2)}) collective-permute-start(f32[408,512]{1,0:T(8,128)S(1)} %get-tuple-element.149), channel_id=1, source_target_pairs={{0,4},{4,8},{8,12},{12,16},{16,20},{20,24},{24,28},{28,0},{1,5},{5... | collective-permute-start | bytes 2506760 | tf_op jit(solution)/shard_map/ppermute | solution.py:27
  90.5 2.2 %collective-permute-start.17 = (f32[1280,128]{1,0:T(8,128)S(1)}, f32[1280,128]{1,0:T(8,128)S(1)}, u32[]{:S(2)}, u32[]{:S(2)}) collective-permute-start(f32[1280,128]{1,0:T(8,128)S(1)} %slice.97), channel_id=1, source_target_pairs={{0,4},{1,5},{2,6},{3,7},{4,0},{5,1},{6,2},{7,3},{8,12},{9,13},{10,... | collective-permute-start | bytes 1966088 | tf_op jit(solution)/shard_map/ppermute | solution.py:33
  92.8 8.1 %collective-permute-start.18 = (f32[320,128]{1,0:T(8,128)S(1)}, f32[320,128]{1,0:T(8,128)S(1)}, u32[]{:S(2)}, u32[]{:S(2)}) collective-permute-start(f32[320,128]{1,0:T(8,128)S(1)} %get-tuple-element.188), channel_id=1, source_target_pairs={{0,24},{1,25},{2,26},{3,27},{4,28},{5,29},{6,30},{7,31},{8,16},{9,... | collective-permute-start | bytes 491528 | tf_op jit(solution)/shard_map/ppermute | solution.py:33
  94.1 9.3 %collective-permute-start.20 = (f32[320,128]{1,0:T(8,128)S(1)}, f32[320,128]{1,0:T(8,128)S(1)}, u32[]{:S(2)}, u32[]{:S(2)}) collective-permute-start(f32[320,128]{1,0:T(8,128)S(1)} %get-tuple-element.189), channel_id=1, source_target_pairs={{0,16},{1,17},{2,18},{3,19},{4,20},{5,21},{6,22},{7,23},{8,24},{9,... | collective-permute-start | bytes 491528 | tf_op jit(solution)/shard_map/ppermute | solution.py:33
  94.9 8.6 %collective-permute-start.19 = (f32[320,128]{1,0:T(8,128)S(1)}, f32[320,128]{1,0:T(8,128)S(1)}, u32[]{:S(2)}, u32[]{:S(2)}) collective-permute-start(f32[320,128]{1,0:T(8,128)S(1)} %get-tuple-element.190), channel_id=1, source_target_pairs={{0,8},{1,9},{2,10},{3,11},{4,12},{5,13},{6,14},{7,15},{8,0},{9,1},... | collective-permute-start | bytes 491528 | tf_op jit(solution)/shard_map/ppermute | solution.py:33
  103.5 15.6 %collective-permute-start.27 = (f32[408,512]{1,0:T(8,128)S(1)}, f32[408,512]{1,0:T(8,128)S(1)}, u32[]{:S(2)}, u32[]{:S(2)}) collective-permute-start(f32[408,512]{1,0:T(8,128)S(1)} %get-tuple-element.173), channel_id=1, source_target_pairs={{0,4},{4,8},{8,12},{12,16},{16,20},{20,24},{24,28},{28,0},{1,5},{5... | collective-permute-start | bytes 2506760 | tf_op jit(solution)/shard_map/ppermute | solution.py:27
  103.6 6.3 %collective-permute-start.21 = (f32[80,128]{1,0:T(8,128)S(1)}, f32[80,128]{1,0:T(8,128)S(1)}, u32[]{:S(2)}, u32[]{:S(2)}) collective-permute-start(f32[80,128]{1,0:T(8,128)S(1)} %get-tuple-element.194), channel_id=1, source_target_pairs={{0,3},{1,2},{2,1},{3,0},{4,7},{5,6},{6,5},{7,4},{8,11},{9,10},{10,... | collective-permute-start | bytes 122888 | tf_op jit(solution)/shard_map/ppermute | solution.py:33
  106.7 4.9 %collective-permute-start.23 = (f32[80,128]{1,0:T(8,128)S(1)}, f32[80,128]{1,0:T(8,128)S(1)}, u32[]{:S(2)}, u32[]{:S(2)}) collective-permute-start(f32[80,128]{1,0:T(8,128)S(1)} %get-tuple-element.195), channel_id=1, source_target_pairs={{0,2},{1,3},{2,0},{3,1},{4,6},{5,7},{6,4},{7,5},{8,10},{9,11},{10,... | collective-permute-start | bytes 122888 | tf_op jit(solution)/shard_map/ppermute | solution.py:33
  106.7 4.9 %collective-permute-start.22 = (f32[80,128]{1,0:T(8,128)S(1)}, f32[80,128]{1,0:T(8,128)S(1)}, u32[]{:S(2)}, u32[]{:S(2)}) collective-permute-start(f32[80,128]{1,0:T(8,128)S(1)} %get-tuple-element.196), channel_id=1, source_target_pairs={{0,1},{1,0},{2,3},{3,2},{4,5},{5,4},{6,7},{7,6},{8,9},{9,8},{10,11... | collective-permute-start | bytes 122888 | tf_op jit(solution)/shard_map/ppermute | solution.py:33
  111.6 5.9 %collective-permute-start.26 = (f32[80,128]{1,0:T(8,128)S(1)}, f32[80,128]{1,0:T(8,128)S(1)}, u32[]{:S(2)}, u32[]{:S(2)}) collective-permute-start(f32[80,128]{1,0:T(8,128)S(1)} %add_add_fusion.2), channel_id=1, source_target_pairs={{0,3},{1,2},{2,1},{3,0},{4,7},{5,6},{6,5},{7,4},{8,11},{9,10},{10,... | collective-permute-start | bytes 122888 | tf_op jit(solution)/shard_map/ppermute | solution.py:33
  114.1 5.0 %collective-permute-start.25 = (f32[80,128]{1,0:T(8,128)S(1)}, f32[80,128]{1,0:T(8,128)S(1)}, u32[]{:S(2)}, u32[]{:S(2)}) collective-permute-start(f32[80,128]{1,0:T(8,128)S(1)} %add_add_fusion.2), channel_id=1, source_target_pairs={{0,2},{1,3},{2,0},{3,1},{4,6},{5,7},{6,4},{7,5},{8,10},{9,11},{10,... | collective-permute-start | bytes 122888 | tf_op jit(solution)/shard_map/ppermute | solution.py:33
  114.1 5.0 %collective-permute-start.24 = (f32[80,128]{1,0:T(8,128)S(1)}, f32[80,128]{1,0:T(8,128)S(1)}, u32[]{:S(2)}, u32[]{:S(2)}) collective-permute-start(f32[80,128]{1,0:T(8,128)S(1)} %add_add_fusion.2), channel_id=1, source_target_pairs={{0,1},{1,0},{2,3},{3,2},{4,5},{5,4},{6,7},{7,6},{8,9},{9,8},{10,11... | collective-permute-start | bytes 122888 | tf_op jit(solution)/shard_map/ppermute | solution.py:33
  119.1 7.8 %collective-permute-start.30 = (f32[320,128]{1,0:T(8,128)S(1)}, f32[320,128]{1,0:T(8,128)S(1)}, u32[]{:S(2)}, u32[]{:S(2)}) collective-permute-start(f32[320,128]{1,0:T(8,128)S(1)} %pad_maximum_fusion.3), channel_id=1, source_target_pairs={{0,24},{1,25},{2,26},{3,27},{4,28},{5,29},{6,30},{7,31},{8,16},{9,... | collective-permute-start | bytes 491528 | tf_op jit(solution)/shard_map/ppermute | solution.py:33
  120.4 8.0 %collective-permute-start.29 = (f32[320,128]{1,0:T(8,128)S(1)}, f32[320,128]{1,0:T(8,128)S(1)}, u32[]{:S(2)}, u32[]{:S(2)}) collective-permute-start(f32[320,128]{1,0:T(8,128)S(1)} %pad_maximum_fusion.3), channel_id=1, source_target_pairs={{0,16},{1,17},{2,18},{3,19},{4,20},{5,21},{6,22},{7,23},{8,24},{9,... | collective-permute-start | bytes 491528 | tf_op jit(solution)/shard_map/ppermute | solution.py:33
  121.5 6.8 %collective-permute-start.28 = (f32[320,128]{1,0:T(8,128)S(1)}, f32[320,128]{1,0:T(8,128)S(1)}, u32[]{:S(2)}, u32[]{:S(2)}) collective-permute-start(f32[320,128]{1,0:T(8,128)S(1)} %pad_maximum_fusion.3), channel_id=1, source_target_pairs={{0,8},{1,9},{2,10},{3,11},{4,12},{5,13},{6,14},{7,15},{8,0},{9,1},... | collective-permute-start | bytes 491528 | tf_op jit(solution)/shard_map/ppermute | solution.py:33
  128.4 2.2 %collective-permute-start.31 = (f32[1280,128]{1,0:T(8,128)S(1)}, f32[1280,128]{1,0:T(8,128)S(1)}, u32[]{:S(2)}, u32[]{:S(2)}) collective-permute-start(f32[1280,128]{1,0:T(8,128)S(1)} %pad_maximum_fusion.1.packed), channel_id=1, source_target_pairs={{0,4},{1,5},{2,6},{3,7},{4,0},{5,1},{6,2},{7,3},{8,12},{9,13},{10,... | collective-permute-start | bytes 1966088 | tf_op jit(solution)/shard_map/ppermute | solution.py:33
  (6 other events, 49.5 us)
